TPU v7x, 32 devices: a whole 2x2x4 slice. The times are simulated.
32 devices in a mesh: space: 8 (over y, x, core), mem: 4 (over z).
Axes of the slice: x: 2, y: 2, z: 4, core: 2. Of those that a mesh axis runs over, the one named last changes fastest.
Arguments:
- increment: float32 [16, 65536], P(None, 'space'), may hold values from -6 to 6
- anomalies: bfloat16 [32, 16, 65536], P('mem', None, 'space'), may hold values from -6 to 6
- interp_index: int32 [3, 65536], P(None, 'space'), may hold values from 0 to 2302, as said below
- interp_weight: float32 [3, 65536], P(None, 'space'), may hold values from 0.2 to 1
- neighbour_blocks: int32 [9, 128], P(None, 'space'), may hold values from 0 to 31, as said below
- tiles: bfloat16 [128, 9, 128, 128], P('space'), may hold values from -0.1875 to 0.1875
Outputs:
- covariance_image: float32 [16, 65536], P(None, ('space', 'mem'))
Inputs may be any that keep to these rules, and one draw needn't show every extreme that they name: `interp_index`: column j of a patch, at position i = j % 8192, names points from c - 128 to c + 127, where c = 128 + i * 2048 // 8192. `neighbour_blocks`: row 0 names the block itself (8 plus its place in the patch); the others lie within 8 blocks of it.
All inputs are finite; a program needn't handle non-finite values.
Results may differ from a plain program's by a relative error of at most 0.015.
Values may be sent and summed in bfloat16 or wider, within the bound.
No kernel may reach another device: no remote copies, remote signals or barrier semaphores. Data moves between devices by JAX's collectives and lax.ppermute only.
A program may use at most 64 MiB of HBM per device.

v0:
```python
import jax
import jax.numpy as jnp
from jax import lax
from jax.sharding import PartitionSpec as P

BLOCK = 128
HI = 128
INTP = 3
SUB_DEV = 2048
HB = 8
HS = 1024


def with_halo(block, sides, width):
    for axis, dim in sides:
        count = lax.axis_size(axis)
        forward = [(i, i + 1) for i in range(count - 1)]
        backward = [(target, source) for source, target in forward]
        low = lax.ppermute(
            lax.slice_in_dim(block, block.shape[dim] - width, None, axis=dim), axis, forward
        )
        high = lax.ppermute(lax.slice_in_dim(block, 0, width, axis=dim), axis, backward)
        block = jnp.concatenate([low, block, high], axis=dim)
    return block


def interp_table(interp_index, interp_weight, piece):
    columns = interp_index.shape[1]
    col_blocks = columns // (4 * piece)
    index_blocks = interp_index.reshape(INTP, col_blocks, 4 * piece)
    weight_blocks = interp_weight.reshape(INTP, col_blocks, 4 * piece)
    base = (jnp.arange(col_blocks, dtype=jnp.int32) * piece)[:, None]
    slots = jnp.arange(3 * piece, dtype=jnp.int32)
    table = jnp.zeros((col_blocks, 3 * piece, 4 * piece), jnp.float32)
    for which in range(INTP):
        local = index_blocks[which] - base
        table = table + jnp.where(
            local[:, None, :] == slots[None, :, None], weight_blocks[which][:, None, :], 0.0
        )
    return table


def shards(increment, anomalies, interp_index, interp_weight, neighbour_blocks, tiles):
    mem_dev, n_fields, columns = anomalies.shape
    row_count = mem_dev * n_fields
    piece = HI
    col_blocks = columns // (4 * piece)
    table = interp_table(interp_index, interp_weight, piece)
    weighted = (anomalies.astype(jnp.float32) * increment[None]).reshape(
        row_count, col_blocks, 4 * piece
    )
    window = jnp.einsum("rcj,cpj->rcp", weighted, table, precision=lax.Precision.HIGHEST)
    window = window.reshape(row_count, col_blocks, 3, piece)
    spread = jnp.pad(window[:, :, 0], ((0, 0), (0, 2), (0, 0)))
    spread = spread + jnp.pad(window[:, :, 1], ((0, 0), (1, 1), (0, 0)))
    spread = spread + jnp.pad(window[:, :, 2], ((0, 0), (2, 0), (0, 0)))
    spread = spread.reshape(row_count, SUB_DEV + 2 * HI)
    reach = HS + HI
    padded = with_halo(spread.astype(jnp.bfloat16), (("space", 1),), reach).astype(spread.dtype)
    left_tail = padded[:, :reach]
    own_part = padded[:, reach : reach + SUB_DEV + 2 * HI]
    right_head = padded[:, reach + SUB_DEV + 2 * HI :]
    full_sum = jnp.zeros((row_count, SUB_DEV + 2 * HS), jnp.float32)
    full_sum = full_sum.at[:, :reach].add(left_tail)
    full_sum = full_sum.at[:, HS - HI : HS + SUB_DEV + HI].add(own_part)
    full_sum = full_sum.at[:, HS + SUB_DEV - HI :].add(right_head)
    device_index = lax.axis_index("space")
    dev_count = lax.axis_size("space")
    position = jnp.arange(SUB_DEV + 2 * HS, dtype=jnp.int32)
    outside = (position < HS) & (device_index == 0) | (position >= HS + SUB_DEV) & (
        device_index == dev_count - 1
    )
    full_sum = jnp.where(outside[None, :], 0.0, full_sum)
    sub_wide = full_sum.astype(jnp.bfloat16)
    ext_blocks = SUB_DEV // BLOCK + 2 * HB
    blocked = sub_wide.reshape(row_count, ext_blocks, BLOCK)
    selector = (
        neighbour_blocks[:, :, None] == jnp.arange(ext_blocks, dtype=jnp.int32)[None, None, :]
    ).astype(jnp.bfloat16)
    picked = jnp.einsum(
        "rek,nbe->rnbk", blocked, selector, preferred_element_type=jnp.float32
    ).astype(jnp.bfloat16)
    smooth = jnp.einsum("rnbk,bnkl->rbl", picked, tiles, preferred_element_type=jnp.float32)
    smooth = smooth.reshape(row_count, SUB_DEV).astype(jnp.bfloat16)
    smooth_wide = with_halo(smooth, (("space", 1),), HI)
    pieces = smooth_wide.astype(jnp.float32).reshape(row_count, col_blocks + 2, piece)
    windows = jnp.concatenate(
        [pieces[:, :col_blocks], pieces[:, 1 : col_blocks + 1], pieces[:, 2:]], axis=2
    )
    returned = jnp.einsum("rcp,cpj->rcj", windows, table, precision=lax.Precision.HIGHEST)
    partial_value = jnp.sum(
        anomalies.astype(jnp.float32) * returned.reshape(mem_dev, n_fields, columns), axis=0
    )
    members = mem_dev * lax.axis_size("mem")
    summed = lax.psum_scatter(
        partial_value.astype(jnp.bfloat16), "mem", scatter_dimension=1, tiled=True
    ).astype(jnp.float32)
    return summed / (members - 1)


def solution(mesh):
    in_specs = (
        P(None, "space"),
        P("mem", None, "space"),
        P(None, "space"),
        P(None, "space"),
        P(None, "space"),
        P("space", None, None, None),
    )
    out_specs = P(None, ("space", "mem"))
    return jax.shard_map(shards, mesh=mesh, in_specs=in_specs, out_specs=out_specs, check_vma=False)
```

profile of v0, /device:TPU:0, one launch (start us, length us, event | category | flops | bytes accessed | tf_op | source)
XLA Modules:
  0.0 153.0 jit_solution(15540545503687765863)
XLA Ops:
  6.5 0.0 reduce-scatter.2.cloned.1.call-start
  6.5 1.3 slice_reduce_fusion.5
  7.9 1.3 slice_reduce_fusion.4
  9.3 2.1 %convert_multiply_fusion.1 = f32[8,16,8192]{2,1,0:T(8,128)S(1)} fusion(bf16[8,16,8192]{2,1,0:T(8,128)(2,1)} %param.13, f32[16,8192]{1,0:T(8,128)} %param.12), kind=kLoop, calls=%fused_computation.22 | loop fusion | flops 2097152 | bytes 6815744 | tf_op jit(solution)/shard_map/mul | solution.py:49
  11.4 3.3 %copy.33 = f32[16,8,16,512]{3,2,1,0:T(8,128)S(1)} copy(f32[16,8,16,512]{3,1,2,0:T(8,128)S(1)} %bitcast.50) | data formatting | bytes 8388608
  14.7 0.1 broadcast_subtract_fusion.2
  14.7 31.4 %fusion.1 = f32[16,384,128]{2,1,0:T(8,128)S(1)} fusion(f32[16,512]{1,0:T(8,128)S(1)} %broadcast_in_dim.59, s32[16,512]{1,0:T(8,128)S(1)} %get-tuple-element.59, f32[16,512]{1,0:T(8,128)S(1)} %broadcast_in_dim.57, s32[16,512]{1,0:T(8,128)S(1)} %get-tuple-element.58, f32[16,512]{1,0:T(8,128)S(1)} %broadcast_in_dim.54, s32[16,512]{1,0:T(8,128)S(1)} %get-tuple-element.57, ...), kind=kOutput, calls=%fused_computation.5 | convolution fusion | flops 4857004032 | bytes 7536640 | tf_op jit(solution)/shard_map/rcj,cpj->rcp/dot_general | solution.py:52
  46.2 0.2 slice_bitcast_fusion.2
  46.4 0.2 add_convert_fusion
  46.6 2.4 %collective-permute-start = (bf16[128,1152]{0,1:T(8,128)(2,1)S(1)}, bf16[128,1152]{0,1:T(8,128)(2,1)S(1)}, u32[]{:S(2)}, u32[]{:S(2)}) collective-permute-start(bf16[128,1152]{0,1:T(8,128)(2,1)S(1)} %get-tuple-element.53), channel_id=1, source_target_pairs={{0,4},{4,8},{8,12},{12,16},{16,20},{20,24},{24,28},{1,5},{5,9},{9,... | collective-permute-start | bytes 884744 | tf_op jit(solution)/shard_map/ppermute | solution.py:19
  49.1 1.5 collective-permute-start.1
  50.6 0.6 compare_reduce_fusion.1
  51.2 0.7 compare_reduce_fusion
  51.9 0.0 collective-permute-done
  51.9 2.7 %collective-permute-done.1 = bf16[128,1152]{0,1:T(8,128)(2,1)S(1)} collective-permute-done((bf16[128,1152]{0,1:T(8,128)(2,1)S(1)}, bf16[128,1152]{0,1:T(8,128)(2,1)S(1)}, u32[]{:S(2)}, u32[]{:S(2)}) %collective-permute-start.1) | collective-permute-done | bytes 294944 | tf_op jit(solution)/shard_map/ppermute | solution.py:22
  54.6 0.7 convert_select_fusion
  55.3 0.1 scatter-add.10
  55.5 0.2 maximum_convert_fusion
  55.6 1.1 fusion.35
  56.7 0.0 copy-start.1
  56.7 0.1 fusion.36
  56.9 2.2 %select_convert_fusion = bf16[128,4096]{0,1:T(8,128)(2,1)S(1)} fusion(f32[128,4096]{0,1:T(8,128)S(1)} %fusion.36, pred[4096]{0:T(1024)(128)(4,1)S(1)} %fusion.42), kind=kLoop, calls=%fused_computation.33 | loop fusion | flops 524288 | bytes 3149824 | tf_op jit(solution)/shard_map/convert_element_type | solution.py:74
  59.0 1.0 copy.24
  60.0 0.0 copy-done.1
  60.0 1.4 fusion.38
  61.4 5.1 %fusion.32 = bf16[16,128,128]{1,2,0:T(8,128)(2,1)S(1)} fusion(bf16[16,9,128,128]{3,2,1,0:T(8,128)(2,1)} %param.17, bf16[9,16,128,128]{3,1,2,0:T(8,128)(2,1)S(1)} %fusion.38), kind=kOutput, calls=%fused_computation.36 | convolution fusion | flops 604241920 | bytes 9961472 | tf_op jit(solution)/shard_map/rnbk,bnkl->rbl/dot_general | solution.py:83
  66.5 7.4 %collective-permute-start.2 = (bf16[128,128]{0,1:T(8,128)(2,1)S(1)}, bf16[128,128]{0,1:T(8,128)(2,1)S(1)}, u32[]{:S(2)}, u32[]{:S(2)}) collective-permute-start(bf16[128,128]{0,1:T(8,128)(2,1)S(1)} %get-tuple-element.55), channel_id=1, source_target_pairs={{0,4},{4,8},{8,12},{12,16},{16,20},{20,24},{24,28},{1,5},{5,9},{9,... | collective-permute-start | bytes 98312 | tf_op jit(solution)/shard_map/ppermute | solution.py:19
  73.9 1.3 collective-permute-start.3
  75.2 0.0 collective-permute-done.2
  75.3 1.8 %collective-permute-done.3 = bf16[128,128]{0,1:T(8,128)(2,1)S(1)} collective-permute-done((bf16[128,128]{0,1:T(8,128)(2,1)S(1)}, bf16[128,128]{0,1:T(8,128)(2,1)S(1)}, u32[]{:S(2)}, u32[]{:S(2)}) %collective-permute-start.3) | collective-permute-done | bytes 32800 | tf_op jit(solution)/shard_map/ppermute | solution.py:22
  77.1 1.4 fusion.47
  78.5 1.6 %copy.30 = f32[128,16,128]{2,0,1:T(8,128)S(1)} copy(f32[128,16,128]{0,2,1:T(8,128)} %get-tuple-element.50) | data formatting | bytes 2097152
  80.0 1.3 copy.31
  81.3 0.3 copy.32
  81.7 1.4 fusion.55
  83.1 23.8 %fusion.26 = f32[128,16,512]{0,2,1:T(8,128)} fusion(f32[16,512]{1,0:T(8,128)S(1)} %broadcast_in_dim.59, s32[16,512]{1,0:T(8,128)S(1)} %get-tuple-element.59, f32[16,512]{1,0:T(8,128)S(1)} %broadcast_in_dim.57, s32[16,512]{1,0:T(8,128)S(1)} %get-tuple-element.58, f32[16,512]{1,0:T(8,128)S(1)} %broadcast_in_dim.54, s32[16,512]{1,0:T(8,128)S(1)} %get-tuple-element.57, ...), kind=kOutput, calls=%fused_computation.32 | convolution fusion | flops 4857004032 | bytes 7536640 | tf_op jit(solution)/shard_map/rcp,cpj->rcj/dot_general | solution.py:90
  106.9 5.5 %copy.21 = f32[128,16,512]{2,1,0:T(8,128)} copy(f32[128,16,512]{0,2,1:T(8,128)} %fusion.26) | data formatting | bytes 8388608 | tf_op jit(solution)/shard_map/rcp,cpj->rcj/transpose | solution.py:90
  112.5 0.0 copy-start
  112.5 5.1 %reshape.175 = f32[8,16,8192]{2,1,0:T(8,128)} reshape(f32[128,16,512]{2,1,0:T(8,128)} %copy.21) | data formatting | bytes 8388608 | tf_op jit(solution)/shard_map/reshape | solution.py:92
  117.6 0.0 copy-done
  117.6 3.4 %fusion.19 = bf16[16,8192]{1,0:T(8,128)(2,1)} fusion(f32[8,16,8192]{2,1,0:T(8,128)} %reshape.175, bf16[8,16,8192]{2,1,0:T(8,128)(2,1)S(1)} %copy-done), kind=kLoop, calls=%fused_computation.25 | loop fusion | flops 3014656 | bytes 6553600 | tf_op jit(solution)/shard_map/reduce_sum | solution.py:91
  121.0 0.0 reduce-scatter.2.cloned.1.call-update
  121.0 23.6 %reduce-scatter.2.cloned.1.call-done = bf16[16,2048]{1,0:T(8,128)(2,1)} async-done(((bf16[16,8192]{1,0:T(8,128)(2,1)}), bf16[16,2048]{1,0:T(8,128)(2,1)}) %reduce-scatter.2.cloned.1.call-update) | async-done | bytes 65552 | tf_op jit(solution)/shard_map/reduce_scatter | solution.py:95
  144.6 1.5 convert_multiply_fusion.2
  (11 shorter events, 0.1 us)
Async XLA Ops:
  6.5 138.1 %reduce-scatter.2.cloned.1.call-start = ((), (), s32[]{:S(2)}) async-start(), calls=%async_computation.1 | async-start | bytes 327680 | tf_op jit(solution)/shard_map/reduce_scatter | solution.py:95
  46.6 5.3 %collective-permute-start = (bf16[128,1152]{0,1:T(8,128)(2,1)S(1)}, bf16[128,1152]{0,1:T(8,128)(2,1)S(1)}, u32[]{:S(2)}, u32[]{:S(2)}) collective-permute-start(bf16[128,1152]{0,1:T(8,128)(2,1)S(1)} %get-tuple-element.53), channel_id=1, source_target_pairs={{0,4},{4,8},{8,12},{12,16},{16,20},{20,24},{24,28},{1,5},{5,9},{9,... | collective-permute-start | bytes 884744 | tf_op jit(solution)/shard_map/ppermute | solution.py:19
  49.1 5.6 %collective-permute-start.1 = (bf16[128,1152]{0,1:T(8,128)(2,1)S(1)}, bf16[128,1152]{0,1:T(8,128)(2,1)S(1)}, u32[]{:S(2)}, u32[]{:S(2)}) collective-permute-start(bf16[128,1152]{0,1:T(8,128)(2,1)S(1)} %get-tuple-element.54), channel_id=1, source_target_pairs={{4,0},{8,4},{12,8},{16,12},{20,16},{24,20},{28,24},{5,1},{9,5},{13... | collective-permute-start | bytes 884744 | tf_op jit(solution)/shard_map/ppermute | solution.py:22
  56.7 3.3 %copy-start.1 = (s32[9,16]{1,0:T(8,128)S(1)}, s32[9,16]{1,0:T(8,128)}, u32[]{:S(2)}) copy-start(s32[9,16]{1,0:T(8,128)} %param.16) | copy-start | bytes 1732
  66.5 8.7 %collective-permute-start.2 = (bf16[128,128]{0,1:T(8,128)(2,1)S(1)}, bf16[128,128]{0,1:T(8,128)(2,1)S(1)}, u32[]{:S(2)}, u32[]{:S(2)}) collective-permute-start(bf16[128,128]{0,1:T(8,128)(2,1)S(1)} %get-tuple-element.55), channel_id=1, source_target_pairs={{0,4},{4,8},{8,12},{12,16},{16,20},{20,24},{24,28},{1,5},{5,9},{9,... | collective-permute-start | bytes 98312 | tf_op jit(solution)/shard_map/ppermute | solution.py:19
  73.9 3.1 %collective-permute-start.3 = (bf16[128,128]{0,1:T(8,128)(2,1)S(1)}, bf16[128,128]{0,1:T(8,128)(2,1)S(1)}, u32[]{:S(2)}, u32[]{:S(2)}) collective-permute-start(bf16[128,128]{0,1:T(8,128)(2,1)S(1)} %get-tuple-element.56), channel_id=1, source_target_pairs={{4,0},{8,4},{12,8},{16,12},{20,16},{24,20},{28,24},{5,1},{9,5},{13... | collective-permute-start | bytes 98312 | tf_op jit(solution)/shard_map/ppermute | solution.py:22
  112.5 5.1 %copy-start = (bf16[8,16,8192]{2,1,0:T(8,128)(2,1)S(1)}, bf16[8,16,8192]{2,1,0:T(8,128)(2,1)}, u32[]{:S(2)}) copy-start(bf16[8,16,8192]{2,1,0:T(8,128)(2,1)} %param.13) | copy-start | bytes 6291460
Sparse Core Ops, SparseCore 0:
  121.1 23.4 reduce-scatter.1
where the time goes:
time: 154 us; the launch traced here: 153 us
  matrix products  61.8 us (40%)
  waiting for transfers between devices  28.1 us (18%)
  local copies, waits for them, and re-layouts  22.5 us (15%)
  other arithmetic  14.4 us (9%)
  between operations  13.7 us (9%)
  starting transfers between devices  12.6 us (8%)
    dot_general x1, matrix products, shards(): jnp.einsum('rcj,cpj->rcp', weighted, table, precision=lax.Precision.HIGHEST)  31.4 us
    dot_general x1, matrix products, shards(): jnp.einsum('rcp,cpj->rcj', windows, table, precision=lax.Precision.HIGHEST)  23.8 us
    reduce_scatter x1, waiting for transfers between devices, shards(): lax.psum_scatter(partial_value.astype(jnp.bfloat16), 'mem', scatter_dimen...  23.6 us
    ppermute x2, starting transfers between devices, with_halo(): lax.ppermute(lax.slice_in_dim(block, block.shape[dim] - width, None, axis...  9.8 us
    unnamed x8, local copies, waits for them, and re-layouts  6.48 us
    transpose x1, local copies, waits for them, and re-layouts, shards(): jnp.einsum('rcp,cpj->rcj', windows, table, precision=lax.Precision.HIGHEST)  5.51 us
    reshape x1, local copies, waits for them, and re-layouts, shards(): returned.reshape(mem_dev, n_fields, columns)  5.12 us
    dot_general x1, matrix products, shards(): jnp.einsum('rnbk,bnkl->rbl', picked, tiles, preferred_element_type=jnp.fl...  5.09 us
  transfers between devices with their start and end apart: 5, of which 3 were waited for; matrix products, arithmetic and copies ran while one was open for 1% of the time, Pallas kernels for 0%

commit v1 on v0

v1 whole, which is shorter than its diff:
```python
import functools

import jax
import jax.numpy as jnp
from jax import lax
from jax.experimental import pallas as pl
from jax.experimental.pallas import tpu as pltpu
from jax.sharding import PartitionSpec as P

BLOCK = 128
HI = 128
INTP = 3
RATIO = 4
CHUNK = RATIO * BLOCK
WIN = 3 * BLOCK
REACH = 2 * HI + 32
F32 = jnp.float32
BF16 = jnp.bfloat16


def params(kib):
    return pltpu.CompilerParams(vmem_limit_bytes=kib * 1024)


def cost(flops, nbytes):
    return pl.CostEstimate(flops=flops, bytes_accessed=nbytes, transcendentals=0)


def build_table(local, weight, table_ref):
    i0, i1, i2 = local[0:1], local[1:2], local[2:3]
    w0, w1, w2 = weight[0:1], weight[1:2], weight[2:3]
    zero = jnp.zeros_like(w0)
    w0 = w0 + jnp.where(i1 == i0, w1, zero) + jnp.where(i2 == i0, w2, zero)
    w1 = w1 + jnp.where(i2 == i1, w2, zero)
    rows = REACH // 16
    iota = lax.broadcasted_iota(jnp.int32, (rows, 16, BLOCK), 0) * 16 + lax.broadcasted_iota(
        jnp.int32, (rows, 16, BLOCK), 1
    )
    iota = iota.astype(jnp.int16)
    for s in range(CHUNK // BLOCK):
        cols = slice(s * BLOCK, (s + 1) * BLOCK)
        base = s * BLOCK // RATIO

        def wide(x, kind):
            return jnp.broadcast_to(x[:, cols], (16, BLOCK)).astype(kind)[None]

        table = jnp.zeros((1, 16, BLOCK), BF16)
        for index, value in ((i2, w2), (i1, w1), (i0, w0)):
            table = jnp.where(wide(index - base, jnp.int16) == iota, wide(value, BF16), table)
        table_ref[base : base + REACH, cols] = table.reshape(REACH, BLOCK)
        if base:
            table_ref[0:base, cols] = jnp.zeros((base, BLOCK), BF16)
        if base + REACH < WIN:
            table_ref[base + REACH : WIN, cols] = jnp.zeros((WIN - base - REACH, BLOCK), BF16)


def spread_kernel(steps, first, last, flip_ref, anom_ref, incr_ref, index_ref, weight_ref, *rest):
    if first:
        table_ref, out_ref, carry_ref, acc_ref = rest
    else:
        carry_ref, _, table_ref, out_ref, acc_ref = rest
    i = pl.program_id(0)
    flip = flip_ref[0]
    chunks = flip_ref[1]
    done = flip_ref[2]
    step = i + done
    c = jnp.where(flip == 1, chunks - 1 - step, step)

    @pl.when(i == 0)
    def _():
        if first:
            acc_ref[0:2] = jnp.zeros((2,) + acc_ref.shape[1:], F32)
        else:
            acc_ref[0:2] = carry_ref[...]

    build_table(index_ref[...] - c * BLOCK, weight_ref[...], table_ref.at[0])
    rows = acc_ref.shape[1]
    weighted = (anom_ref[...].astype(F32) * incr_ref[...][None]).astype(BF16).reshape(rows, CHUNK)
    window = lax.dot_general(
        weighted, table_ref[0], (((1,), (1,)), ((), ())), preferred_element_type=F32
    )
    acc_ref[2] = jnp.zeros(acc_ref.shape[1:], F32)
    for k in range(3):
        slot = jnp.where(flip == 1, 2 - k, k)
        acc_ref[slot] += window[:, k * BLOCK : (k + 1) * BLOCK]
    total = steps if first else steps + 2
    out_ref[jnp.where(flip == 1, total - 1 - i, i)] = acc_ref[0].astype(BF16)
    acc_ref[0] = acc_ref[1]
    acc_ref[1] = acc_ref[2]

    @pl.when(i == steps - 1)
    def _():
        if first:
            carry_ref[...] = acc_ref[0:2]
        else:
            out_ref[jnp.where(flip == 1, 1, steps)] = acc_ref[0].astype(BF16)
            out_ref[jnp.where(flip == 1, 0, steps + 1)] = acc_ref[1].astype(BF16)


def spread_call(steps, first, info, anomalies, increment, index, weight, carry=None):
    members, fields, columns = anomalies.shape
    rows = members * fields
    chunks = columns // CHUNK

    def at(i, info):
        step = i + info[2]
        return jnp.where(info[0] == 1, chunks - 1 - step, step)

    in_specs = [
        pl.BlockSpec((members, fields, CHUNK), lambda i, info: (0, 0, at(i, info))),
        pl.BlockSpec((fields, CHUNK), lambda i, info: (0, at(i, info))),
        pl.BlockSpec((INTP, CHUNK), lambda i, info: (0, at(i, info))),
        pl.BlockSpec((INTP, CHUNK), lambda i, info: (0, at(i, info))),
    ]
    operands = [anomalies, increment, index, weight]
    blocks = steps if first else steps + 2
    out_shape = [
        jax.ShapeDtypeStruct((chunks, WIN, CHUNK), BF16),
        jax.ShapeDtypeStruct((blocks, rows, BLOCK), BF16),
    ]
    out_specs = [
        pl.BlockSpec((1, WIN, CHUNK), lambda i, info: (at(i, info), 0, 0)),
        pl.BlockSpec((blocks, rows, BLOCK), lambda i, info: (0, 0, 0)),
    ]
    aliases = {}
    if first:
        out_shape.append(jax.ShapeDtypeStruct((2, rows, BLOCK), F32))
        out_specs.append(pl.BlockSpec((2, rows, BLOCK), lambda i, info: (0, 0, 0)))
    else:
        in_specs.append(pl.BlockSpec((2, rows, BLOCK), lambda i, info: (0, 0, 0)))
        in_specs.append(pl.BlockSpec(memory_space=pl.ANY))
        operands.extend(carry)
        aliases = {len(operands): 0}
    return pl.pallas_call(
        functools.partial(spread_kernel, steps, first, not first),
        grid_spec=pltpu.PrefetchScalarGridSpec(
            num_scalar_prefetch=1,
            grid=(steps,),
            in_specs=in_specs,
            out_specs=out_specs,
            scratch_shapes=[pltpu.VMEM((3, rows, BLOCK), F32)],
        ),
        out_shape=out_shape,
        input_output_aliases=aliases,
        compiler_params=params(16 * 1024),
        cost_estimate=cost(2 * rows * steps * WIN * CHUNK, steps * WIN * CHUNK * 4),
        name="spread_first" if first else "spread_rest",
    )(info, *operands)


def conv_kernel(blocks, half, info_ref, nbr_ref, own_a, own_b, got_a, got_b, tiles_ref, out_ref, wide_ref):
    b = pl.program_id(0)
    flip = info_ref[0]
    has_left = info_ref[3]
    has_right = info_ref[4]
    reach = half - 1

    @pl.when(b == 0)
    def _():
        def fill(low, high, left, right):
            wide_ref[reach - 1 : reach - 1 + half] = low[...]
            wide_ref[reach - 1 + half : reach - 1 + 2 * half] = high[...]
            zeros = jnp.zeros((half,) + wide_ref.shape[1:], BF16)

            @pl.when(has_left == 1)
            def _():
                wide_ref[0 : reach - 1] = left[0 : reach - 1]
                wide_ref[reach - 1 : reach + 1] = (
                    left[reach - 1 : reach + 1].astype(F32) + low[0:2].astype(F32)
                ).astype(BF16)

            @pl.when(has_left == 0)
            def _():
                wide_ref[0:reach] = zeros[0:reach]

            top = blocks + reach

            @pl.when(has_right == 1)
            def _():
                wide_ref[top - 1 : top + 1] = (
                    right[0:2].astype(F32) + high[half - 2 : half].astype(F32)
                ).astype(BF16)
                wide_ref[top + 1 : top + reach] = right[2:half]

            @pl.when(has_right == 0)
            def _():
                wide_ref[top : top + reach] = zeros[0:reach]

        @pl.when(flip == 0)
        def _():
            fill(own_b, own_a, got_b, got_a)

        @pl.when(flip == 1)
        def _():
            fill(own_a, own_b, got_a, got_b)

    count = tiles_ref.shape[1]
    picked = jnp.concatenate([wide_ref[nbr_ref[n, b]] for n in range(count)], axis=1)
    smooth = jnp.dot(
        picked, tiles_ref[0].reshape(count * BLOCK, BLOCK), preferred_element_type=F32
    )
    out_ref[0] = smooth.astype(BF16)


def conv_call(info, neighbours, own_a, own_b, got_a, got_b, tiles):
    blocks, count = tiles.shape[:2]
    half, rows, _ = own_a.shape
    reach = half - 1
    full = pl.BlockSpec((half, rows, BLOCK), lambda b, info, nbr: (0, 0, 0))
    return pl.pallas_call(
        functools.partial(conv_kernel, blocks, half),
        grid_spec=pltpu.PrefetchScalarGridSpec(
            num_scalar_prefetch=2,
            grid=(blocks,),
            in_specs=[full] * 4
            + [pl.BlockSpec((1, count, BLOCK, BLOCK), lambda b, info, nbr: (b, 0, 0, 0))],
            out_specs=pl.BlockSpec((1, rows, BLOCK), lambda b, info, nbr: (b, 0, 0)),
            scratch_shapes=[pltpu.VMEM((blocks + 2 * reach, rows, BLOCK), BF16)],
        ),
        out_shape=jax.ShapeDtypeStruct((blocks, rows, BLOCK), BF16),
        compiler_params=params(16 * 1024),
        cost_estimate=cost(2 * rows * blocks * count * BLOCK * BLOCK, tiles.size * 2),
        name="convolve",
    )(info, neighbours, own_a, own_b, got_a, got_b, tiles)


def back_kernel(info_ref, smooth_ref, got_a, got_b, table_ref, anom_ref, out_ref, own_ref, wide_ref):
    c = pl.program_id(0)
    blocks = smooth_ref.shape[0]
    flip = info_ref[0]

    @pl.when(c == 0)
    def _():
        wide_ref[1 : blocks + 1] = smooth_ref[...]
        left = jnp.where(flip == 1, got_a[...], got_b[...])
        right = jnp.where(flip == 1, got_b[...], got_a[...])
        wide_ref[0] = jnp.where(info_ref[3] == 1, left, jnp.zeros_like(left))
        wide_ref[blocks + 1] = jnp.where(info_ref[4] == 1, right, jnp.zeros_like(right))

    lhs = jnp.concatenate([wide_ref[c], wide_ref[c + 1], wide_ref[c + 2]], axis=1)
    returned = jnp.dot(lhs, table_ref[0], preferred_element_type=F32)
    anom = anom_ref[...].astype(F32)
    value = jnp.sum(anom * returned.reshape(anom.shape), axis=0)
    out_ref[0] = value.astype(BF16)
    shares = info_ref[5]
    per = blocks // shares

    @pl.when(c // per == info_ref[6])
    def _():
        own_ref[c % per] = value


def back_call(info, shares, smooth, got_a, got_b, table, anomalies):
    members, fields, columns = anomalies.shape
    blocks, rows, _ = smooth.shape
    per = blocks // shares
    edge = pl.BlockSpec((rows, BLOCK), lambda c, info: (0, 0))
    return pl.pallas_call(
        back_kernel,
        grid_spec=pltpu.PrefetchScalarGridSpec(
            num_scalar_prefetch=1,
            grid=(blocks,),
            in_specs=[
                pl.BlockSpec((blocks, rows, BLOCK), lambda c, info: (0, 0, 0)),
                edge,
                edge,
                pl.BlockSpec((1, WIN, CHUNK), lambda c, info: (c, 0, 0)),
                pl.BlockSpec((members, fields, CHUNK), lambda c, info: (0, 0, c)),
            ],
            out_specs=[
                pl.BlockSpec((1, fields, CHUNK), lambda c, info: (c, 0, 0)),
                pl.BlockSpec((per, fields, CHUNK), lambda c, info: (0, 0, 0)),
            ],
            scratch_shapes=[pltpu.VMEM((blocks + 2, rows, BLOCK), BF16)],
        ),
        out_shape=[
            jax.ShapeDtypeStruct((blocks, fields, CHUNK), BF16),
            jax.ShapeDtypeStruct((per, fields, CHUNK), F32),
        ],
        compiler_params=params(16 * 1024),
        cost_estimate=cost(2 * rows * blocks * WIN * CHUNK, table.size * 2),
        name="back",
    )(info, smooth, got_a, got_b, table, anomalies)


def swaps(count):
    inner = [(i, i ^ 1) for i in range(count)]
    outer = [(i, (i + 1) % count if i % 2 else (i - 1) % count) for i in range(count)]
    return inner, outer


def shards(increment, anomalies, interp_index, interp_weight, neighbour_blocks, tiles):
    members, fields, columns = anomalies.shape
    chunks = columns // CHUNK
    space = lax.axis_index("space")
    count = lax.axis_size("space")
    mem = lax.axis_index("mem")
    shares = lax.axis_size("mem")
    flip = space % 2
    inner, outer = swaps(count)
    head = chunks // 2 + 1

    def info_of(done):
        return jnp.stack(
            [
                flip,
                jnp.int32(chunks),
                jnp.int32(done),
                (space > 0).astype(jnp.int32),
                (space < count - 1).astype(jnp.int32),
                jnp.int32(shares),
                mem,
            ]
        ).astype(jnp.int32)

    info = info_of(0)
    table, own_b, carry = spread_call(
        head, True, info, anomalies, increment, interp_index, interp_weight
    )
    got_b = lax.ppermute(own_b, "space", outer)
    table, own_a = spread_call(
        chunks - head,
        False,
        info_of(head),
        anomalies,
        increment,
        interp_index,
        interp_weight,
        (carry, table),
    )
    got_a = lax.ppermute(own_a, "space", inner)
    smooth = conv_call(info, neighbour_blocks, own_a, own_b, got_a, got_b, tiles)
    low, high = smooth[0], smooth[chunks - 1]
    edge_a = lax.ppermute(jnp.where(flip == 1, low, high), "space", inner)
    edge_b = lax.ppermute(jnp.where(flip == 1, high, low), "space", outer)
    pieces, own = back_call(info, shares, smooth, edge_a, edge_b, table, anomalies)
    per = chunks // shares
    pieces = pieces.reshape(shares, per, fields, CHUNK)
    total = own
    for shift in range(1, shares):
        piece = lax.dynamic_index_in_dim(pieces, (mem + shift) % shares, 0, False)
        got = lax.ppermute(piece, "mem", [(i, (i + shift) % shares) for i in range(shares)])
        total = total + got.astype(F32)
    total = total / (members * shares - 1)
    return jnp.swapaxes(total, 0, 1).reshape(fields, per * CHUNK)


def solution(mesh):
    in_specs = (
        P(None, "space"),
        P("mem", None, "space"),
        P(None, "space"),
        P(None, "space"),
        P(None, "space"),
        P("space", None, None, None),
    )
    out_specs = P(None, ("space", "mem"))
    return jax.shard_map(shards, mesh=mesh, in_specs=in_specs, out_specs=out_specs, check_vma=False)
```

time: 154 us -> 60.4 us (0.39)
  matrix products: 61.8 us -> 0 us
  Pallas kernels: 0 us -> 17.3 us
  waiting for transfers between devices: 28.1 us -> 12.5 us
  other arithmetic: 14.4 us -> 0.05 us
  between operations: 13.7 us -> 0.1 us
  local copies, waits for them, and re-layouts: 22.5 us -> 18.3 us
    dot_general x4 -> x0, matrix products: 61.8 us -> none  [the longest x1 31.4 us: shards(): jnp.einsum('rcj,cpj->rcp', weighted, table, precision=lax.Precision.HIGHEST)]
    reduce_scatter x1 -> x0, waiting for transfers between devices: 23.6 us -> none  [shards(): lax.psum_scatter(partial_value.astype(jnp.bfloat16), 'mem', scatter_dimen...]
    pallas_call x0 -> x4, Pallas kernels: none -> 17.3 us  [the longest x2 7.84 us: spread_call(): pl.pallas_call(functools.partial(spread_kernel, steps, first, not first),...]
    unnamed x8 -> x28, local copies, waits for them, and re-layouts: 6.48 us -> 17.4 us
    ppermute x4 -> x7, waiting for transfers between devices: 4.49 us -> 12.5 us  [the longest x1 6.73 us: shards(): got_b = lax.ppermute(own_b, 'space', outer)]
    transpose x1 -> x0, local copies, waits for them, and re-layouts: 5.51 us -> none  [shards(): jnp.einsum('rcp,cpj->rcj', windows, table, precision=lax.Precision.HIGHEST)]
    reshape x2 -> x1, local copies, waits for them, and re-layouts: 6.09 us -> 0.66 us  [shards(): return jnp.swapaxes(total, 0, 1).reshape(fields, per * CHUNK)]
    slice x5 -> x0, local copies, waits for them, and re-layouts: 4.05 us -> none  [the longest x1 1.37 us: shards(): pieces[:, :col_blocks]]
  transfers between devices with their start and end apart: 5 -> 7, of which waited for: 3 -> 5; matrix products, arithmetic and copies ran while one was open for 1% -> 0% of each run, Pallas kernels for 0% -> 0%
where the time goes in v1:
time: 60.4 us; the launch traced here: 60 us
  local copies, waits for them, and re-layouts  18.3 us (30%)
  Pallas kernels  17.3 us (29%)
  waiting for transfers between devices  12.5 us (21%)
  starting transfers between devices  11.8 us (20%)
    unnamed x28, local copies, waits for them, and re-layouts  17.4 us
    pallas_call x2, Pallas kernels, spread_call(): pl.pallas_call(functools.partial(spread_kernel, steps, first, not first),...  7.84 us
    ppermute x1, waiting for transfers between devices, shards(): got_b = lax.ppermute(own_b, 'space', outer)  6.73 us
    ppermute x3, starting transfers between devices, shards(): lax.ppermute(piece, 'mem', [(i, (i + shift) % shares) for i in range(shar...  5.76 us
    pallas_call x1, Pallas kernels, back_call(): pl.pallas_call(back_kernel, grid_spec=pltpu.PrefetchScalarGridSpec(num_sc...  4.86 us
    pallas_call x1, Pallas kernels, conv_call(): pl.pallas_call(functools.partial(conv_kernel, blocks, half), grid_spec=pl...  4.59 us
    ppermute x1, starting transfers between devices, shards(): got_b = lax.ppermute(own_b, 'space', outer)  3.54 us
    ppermute x3, waiting for transfers between devices, shards(): lax.ppermute(piece, 'mem', [(i, (i + shift) % shares) for i in range(shar...  3.36 us
  transfers between devices with their start and end apart: 7, of which 5 were waited for; matrix products, arithmetic and copies ran while one was open for 0% of the time, Pallas kernels for 0%

profile of v1, /device:TPU:0, one launch (start us, length us, event | category | flops | bytes accessed | tf_op | source)
XLA Modules:
  0.0 60.0 jit_solution(3737226096400684359)
XLA Ops:
  0.0 0.0 copy-start.13
  0.0 0.1 stack.34.flip_ref.info_ref
  0.1 0.1 stack.35.flip_ref
  0.2 0.0 copy-start.2
  0.2 1.6 %copy-done.2 = bf16[8,16,8192]{2,1,0:T(8,128)(2,1)S(1)} copy-done((bf16[8,16,8192]{2,1,0:T(8,128)(2,1)S(1)}, bf16[8,16,8192]{2,1,0:T(8,128)(2,1)}, u32[]{:S(2)}) %copy-start.2) | copy-done | bytes 2097176
  1.8 0.0 copy-start.6
  1.8 1.0 %copy-done.6 = f32[16,8192]{1,0:T(8,128)S(1)} copy-done((f32[16,8192]{1,0:T(8,128)S(1)}, f32[16,8192]{1,0:T(8,128)}, u32[]{:S(2)}) %copy-start.6) | copy-done | bytes 524312
  2.8 0.0 copy-start.8
  2.8 0.9 %copy-done.8 = s32[3,8192]{1,0:T(4,128)S(1)} copy-done((s32[3,8192]{1,0:T(4,128)S(1)}, s32[3,8192]{1,0:T(4,128)}, u32[]{:S(2)}) %copy-start.8) | copy-done | bytes 98328
  3.7 0.0 copy-start.10
  3.7 0.9 %copy-done.10 = f32[3,8192]{1,0:T(4,128)S(1)} copy-done((f32[3,8192]{1,0:T(4,128)S(1)}, f32[3,8192]{1,0:T(4,128)}, u32[]{:S(2)}) %copy-start.10) | copy-done | bytes 98328
  4.6 4.3 %spread_first.1 = (bf16[16,384,512]{2,1,0:T(8,128)(2,1)S(1)}, bf16[9,128,128]{2,1,0:T(8,128)(2,1)S(1)}, f32[2,128,128]{2,1,0:T(8,128)S(1)}) custom-call(s32[7]{0:T(128)S(1)} %stack.34.flip_ref.info_ref, bf16[8,16,8192]{2,1,0:T(8,128)(2,1)S(1)} %copy-done.2, f32[16,8192]{1,0:T(8,128)S(1)} %copy-done.6, s32[3,8192]{1,0:T(4,128)S(1)} %copy-done.8, ...), custom_call_target="tpu_custom_call" | custom-call | flops 452984832 | bytes 7077888 | tf_op jit(solution)/shard_map/spread_first/pallas_call | solution.py:134
  9.0 0.0 copy-start.3
  9.0 1.6 %copy-done.3 = bf16[8,16,8192]{2,1,0:T(8,128)(2,1)S(1)} copy-done((bf16[8,16,8192]{2,1,0:T(8,128)(2,1)S(1)}, bf16[8,16,8192]{2,1,0:T(8,128)(2,1)}, u32[]{:S(2)}) %copy-start.3) | copy-done | bytes 2097176
  10.6 0.0 copy-start.7
  10.6 1.0 %copy-done.7 = f32[16,8192]{1,0:T(8,128)S(1)} copy-done((f32[16,8192]{1,0:T(8,128)S(1)}, f32[16,8192]{1,0:T(8,128)}, u32[]{:S(2)}) %copy-start.7) | copy-done | bytes 524312
  11.6 0.0 copy-start.9
  11.6 0.9 %copy-done.9 = s32[3,8192]{1,0:T(4,128)S(1)} copy-done((s32[3,8192]{1,0:T(4,128)S(1)}, s32[3,8192]{1,0:T(4,128)}, u32[]{:S(2)}) %copy-start.9) | copy-done | bytes 98328
  12.5 0.0 copy-start.4
  12.5 3.5 %spread_rest.1 = (bf16[16,384,512]{2,1,0:T(8,128)(2,1)S(1)}, bf16[9,128,128]{2,1,0:T(8,128)(2,1)S(1)}) custom-call(s32[7]{0:T(128)S(1)} %stack.35.flip_ref, bf16[8,16,8192]{2,1,0:T(8,128)(2,1)S(1)} %copy-done.3, f32[16,8192]{1,0:T(8,128)S(1)} %copy-done.7, s32[3,8192]{1,0:T(4,128)S(1)} %copy-done.9, ...), custom_call_target="tpu_custom_call", output_to_operand_aliasing={{0}: (6, {})} | custom-call | flops 352321536 | bytes 5505024 | tf_op jit(solution)/shard_map/spread_rest/pallas_call | solution.py:134
  16.0 0.0 copy-start
  16.0 2.6 %copy-done = bf16[16,384,512]{2,1,0:T(8,128)(2,1)} copy-done((bf16[16,384,512]{2,1,0:T(8,128)(2,1)}, bf16[16,384,512]{2,1,0:T(8,128)(2,1)S(1)}, u32[]{:S(2)}) %copy-start) | copy-done | bytes 6291480
  18.7 0.5 collective-permute-start
  19.2 3.5 %collective-permute-start.1 = (bf16[9,128,128]{2,1,0:T(8,128)(2,1)S(1)}, bf16[9,128,128]{2,1,0:T(8,128)(2,1)S(1)}, u32[]{:S(2)}, u32[]{:S(2)}) collective-permute-start(bf16[9,128,128]{2,1,0:T(8,128)(2,1)S(1)} %get-tuple-element.15.own_b), channel_id=1, source_target_pairs={{0,28},{4,8},{8,4},{12,16},{16,12},{20,24},{24,20},{28,0},{1,29},{... | collective-permute-start | bytes 884744 | tf_op jit(solution)/shard_map/ppermute | solution.py:320
  22.7 0.0 collective-permute-done.got_a
  22.7 6.7 %collective-permute-done.1.got_b = bf16[9,128,128]{2,1,0:T(8,128)(2,1)S(1)} collective-permute-done((bf16[9,128,128]{2,1,0:T(8,128)(2,1)S(1)}, bf16[9,128,128]{2,1,0:T(8,128)(2,1)S(1)}, u32[]{:S(2)}, u32[]{:S(2)}) %collective-permute-start.1) | collective-permute-done | bytes 294944 | tf_op jit(solution)/shard_map/ppermute | solution.py:320
  29.4 0.0 copy-start.11
  29.4 0.7 %copy-done.11 = bf16[9,128,128]{2,1,0:T(8,128)(2,1)} copy-done((bf16[9,128,128]{2,1,0:T(8,128)(2,1)}, bf16[9,128,128]{2,1,0:T(8,128)(2,1)S(1)}, u32[]{:S(2)}) %copy-start.11) | copy-done | bytes 294936
  30.2 0.0 copy-done.13
  30.2 0.0 copy-start.5
  30.2 2.3 %copy-done.5 = bf16[16,9,128,128]{3,2,1,0:T(8,128)(2,1)S(1)} copy-done((bf16[16,9,128,128]{3,2,1,0:T(8,128)(2,1)S(1)}, bf16[16,9,128,128]{3,2,1,0:T(8,128)(2,1)}, u32[]{:S(2)}) %copy-start.5) | copy-done | bytes 4718616
  32.5 0.0 copy-start.12
  32.5 1.0 %copy-done.12 = bf16[9,128,128]{2,1,0:T(8,128)(2,1)S(1)} copy-done((bf16[9,128,128]{2,1,0:T(8,128)(2,1)S(1)}, bf16[9,128,128]{2,1,0:T(8,128)(2,1)}, u32[]{:S(2)}) %copy-start.12) | copy-done | bytes 294936
  33.5 4.6 %convolve.1.smooth_ref = bf16[16,128,128]{2,1,0:T(8,128)(2,1)S(1)} custom-call(s32[7]{0:T(128)S(1)} %stack.34.flip_ref.info_ref, s32[9,16]{1,0:T(8,128)S(1)} %copy-done.13, bf16[9,128,128]{2,1,0:T(8,128)(2,1)S(1)} %get-tuple-element.14.own_a, bf16[9,128,128]{2,1,0:T(8,128)(2,1)S(1)} %get-tuple-element.15.own_b, ...), custom_call_target="tpu_custom_call" | custom-call | flops 603979776 | bytes 4718592 | tf_op jit(solution)/shard_map/convolve/pallas_call | solution.py:210
  38.1 0.1 collective-permute-start.2
  38.2 1.9 %collective-permute-start.3 = (bf16[128,128]{1,0:T(8,128)(2,1)S(1)}, bf16[128,128]{1,0:T(8,128)(2,1)S(1)}, u32[]{:S(2)}, u32[]{:S(2)}) collective-permute-start(bf16[128,128]{1,0:T(8,128)(2,1)S(1)} %get-tuple-element.19), channel_id=1, source_target_pairs={{0,28},{4,8},{8,4},{12,16},{16,12},{20,24},{24,20},{28,0},{1,29},{... | collective-permute-start | bytes 98312 | tf_op jit(solution)/shard_map/ppermute | solution.py:335
  40.1 0.0 collective-permute-done.2.got_a
  40.1 2.4 %collective-permute-done.3.got_b = bf16[128,128]{1,0:T(8,128)(2,1)S(1)} collective-permute-done((bf16[128,128]{1,0:T(8,128)(2,1)S(1)}, bf16[128,128]{1,0:T(8,128)(2,1)S(1)}, u32[]{:S(2)}, u32[]{:S(2)}) %collective-permute-start.3) | collective-permute-done | bytes 32800 | tf_op jit(solution)/shard_map/ppermute | solution.py:335
  42.5 0.0 copy-done.4
  42.5 2.8 %copy-done.1 = bf16[16,384,512]{2,1,0:T(8,128)(2,1)S(1)} copy-done((bf16[16,384,512]{2,1,0:T(8,128)(2,1)S(1)}, bf16[16,384,512]{2,1,0:T(8,128)(2,1)}, u32[]{:S(2)}) %copy-start.1) | copy-done | bytes 6291480
  45.3 4.9 %back.1 = (bf16[16,16,512]{2,1,0:T(8,128)(2,1)S(1)}, f32[4,16,512]{2,1,0:T(8,128)S(1)}) custom-call(s32[7]{0:T(128)S(1)} %stack.34.flip_ref.info_ref, bf16[16,128,128]{2,1,0:T(8,128)(2,1)S(1)} %convolve.1.smooth_ref, bf16[128,128]{1,0:T(8,128)(2,1)S(1)} %collective-permute-done.2.got_a, bf16[128,128]{1,0:T(8,128)(2,1)S(1)} %collective-permute-done.3.got_b, ...), custom_call_target="tpu_custom_call" | custom-call | flops 805306368 | bytes 6291456 | tf_op jit(solution)/shard_map/back/pallas_call | solution.py:258
  50.2 1.8 %collective-permute-start.4 = (bf16[4,16,512]{2,1,0:T(8,128)(2,1)S(1)}, bf16[4,16,512]{2,1,0:T(8,128)(2,1)S(1)}, u32[]{:S(2)}, u32[]{:S(2)}) collective-permute-start(bf16[4,16,512]{2,1,0:T(8,128)(2,1)S(1)} %get-tuple-element.21), channel_id=1, source_target_pairs={{0,1},{1,2},{2,3},{3,0},{4,5},{5,6},{6,7},{7,4},{8,9},{9,10},{10,1... | collective-permute-start | bytes 196616 | tf_op jit(solution)/shard_map/ppermute | solution.py:342
  52.0 2.6 %collective-permute-start.5 = (bf16[4,16,512]{2,1,0:T(8,128)(2,1)S(1)}, bf16[4,16,512]{2,1,0:T(8,128)(2,1)S(1)}, u32[]{:S(2)}, u32[]{:S(2)}) collective-permute-start(bf16[4,16,512]{2,1,0:T(8,128)(2,1)S(1)} %get-tuple-element.23), channel_id=1, source_target_pairs={{0,2},{1,3},{2,0},{3,1},{4,6},{5,7},{6,4},{7,5},{8,10},{9,11},{10,... | collective-permute-start | bytes 196616 | tf_op jit(solution)/shard_map/ppermute | solution.py:342
  54.6 1.3 %collective-permute-start.6 = (bf16[4,16,512]{2,1,0:T(8,128)(2,1)S(1)}, bf16[4,16,512]{2,1,0:T(8,128)(2,1)S(1)}, u32[]{:S(2)}, u32[]{:S(2)}) collective-permute-start(bf16[4,16,512]{2,1,0:T(8,128)(2,1)S(1)} %get-tuple-element.22), channel_id=1, source_target_pairs={{0,3},{1,0},{2,1},{3,2},{4,7},{5,4},{6,5},{7,6},{8,11},{9,8},{10,9... | collective-permute-start | bytes 196616 | tf_op jit(solution)/shard_map/ppermute | solution.py:342
  55.9 0.6 %collective-permute-done.4 = bf16[4,16,512]{2,1,0:T(8,128)(2,1)S(1)} collective-permute-done((bf16[4,16,512]{2,1,0:T(8,128)(2,1)S(1)}, bf16[4,16,512]{2,1,0:T(8,128)(2,1)S(1)}, u32[]{:S(2)}, u32[]{:S(2)}) %collective-permute-start.4) | collective-permute-done | bytes 65568 | tf_op jit(solution)/shard_map/ppermute | solution.py:342
  56.5 2.5 %collective-permute-done.5 = bf16[4,16,512]{2,1,0:T(8,128)(2,1)S(1)} collective-permute-done((bf16[4,16,512]{2,1,0:T(8,128)(2,1)S(1)}, bf16[4,16,512]{2,1,0:T(8,128)(2,1)S(1)}, u32[]{:S(2)}, u32[]{:S(2)}) %collective-permute-start.5) | collective-permute-done | bytes 65568 | tf_op jit(solution)/shard_map/ppermute | solution.py:342
  59.1 0.2 collective-permute-done.6
  59.3 0.7 %copy.9 = f32[4,2,8,512]{3,2,0,1:T(8,128)} copy(f32[4,2,8,512]{3,2,1,0:T(8,128)S(1)} %multiply_bitcast_fusion) | data formatting | bytes 262144 | tf_op jit(solution)/shard_map/reshape | solution.py:345
  (4 shorter events, 0.1 us)
Async XLA Ops:
  0.0 30.2 %copy-start.13 = (s32[9,16]{1,0:T(8,128)S(1)}, s32[9,16]{1,0:T(8,128)}, u32[]{:S(2)}) copy-start(s32[9,16]{1,0:T(8,128)} %nbr_ref.1) | copy-start | bytes 1732
  0.2 1.6 %copy-start.2 = (bf16[8,16,8192]{2,1,0:T(8,128)(2,1)S(1)}, bf16[8,16,8192]{2,1,0:T(8,128)(2,1)}, u32[]{:S(2)}) copy-start(bf16[8,16,8192]{2,1,0:T(8,128)(2,1)} %anom_ref.5) | copy-start | bytes 6291460
  1.8 1.0 %copy-start.6 = (f32[16,8192]{1,0:T(8,128)S(1)}, f32[16,8192]{1,0:T(8,128)}, u32[]{:S(2)}) copy-start(f32[16,8192]{1,0:T(8,128)} %incr_ref.3) | copy-start | bytes 1572868
  2.8 0.9 %copy-start.8 = (s32[3,8192]{1,0:T(4,128)S(1)}, s32[3,8192]{1,0:T(4,128)}, u32[]{:S(2)}) copy-start(s32[3,8192]{1,0:T(4,128)} %index_ref.3) | copy-start | bytes 294916
  3.7 0.9 %copy-start.10 = (f32[3,8192]{1,0:T(4,128)S(1)}, f32[3,8192]{1,0:T(4,128)}, u32[]{:S(2)}) copy-start(f32[3,8192]{1,0:T(4,128)} %weight_ref.3) | copy-start | bytes 294916
  9.0 1.6 %copy-start.3 = (bf16[8,16,8192]{2,1,0:T(8,128)(2,1)S(1)}, bf16[8,16,8192]{2,1,0:T(8,128)(2,1)}, u32[]{:S(2)}) copy-start(bf16[8,16,8192]{2,1,0:T(8,128)(2,1)} %anom_ref.5) | copy-start | bytes 6291460
  10.6 1.0 %copy-start.7 = (f32[16,8192]{1,0:T(8,128)S(1)}, f32[16,8192]{1,0:T(8,128)}, u32[]{:S(2)}) copy-start(f32[16,8192]{1,0:T(8,128)} %incr_ref.3) | copy-start | bytes 1572868
  11.6 0.9 %copy-start.9 = (s32[3,8192]{1,0:T(4,128)S(1)}, s32[3,8192]{1,0:T(4,128)}, u32[]{:S(2)}) copy-start(s32[3,8192]{1,0:T(4,128)} %index_ref.3) | copy-start | bytes 294916
  12.5 30.0 %copy-start.4 = (bf16[8,16,8192]{2,1,0:T(8,128)(2,1)S(1)}, bf16[8,16,8192]{2,1,0:T(8,128)(2,1)}, u32[]{:S(2)}) copy-start(bf16[8,16,8192]{2,1,0:T(8,128)(2,1)} %anom_ref.5) | copy-start | bytes 6291460
  16.0 2.7 %copy-start = (bf16[16,384,512]{2,1,0:T(8,128)(2,1)}, bf16[16,384,512]{2,1,0:T(8,128)(2,1)S(1)}, u32[]{:S(2)}) copy-start(bf16[16,384,512]{2,1,0:T(8,128)(2,1)S(1)} %get-tuple-element.16.table_ref) | copy-start | bytes 18874372
  18.7 4.0 %collective-permute-start = (bf16[9,128,128]{2,1,0:T(8,128)(2,1)S(1)}, bf16[9,128,128]{2,1,0:T(8,128)(2,1)S(1)}, u32[]{:S(2)}, u32[]{:S(2)}) collective-permute-start(bf16[9,128,128]{2,1,0:T(8,128)(2,1)S(1)} %get-tuple-element.14.own_a), channel_id=1, source_target_pairs={{0,4},{4,0},{8,12},{12,8},{16,20},{20,16},{24,28},{28,24},{1,5},{5... | collective-permute-start | bytes 884744 | tf_op jit(solution)/shard_map/ppermute | solution.py:331
  19.2 10.3 %collective-permute-start.1 = (bf16[9,128,128]{2,1,0:T(8,128)(2,1)S(1)}, bf16[9,128,128]{2,1,0:T(8,128)(2,1)S(1)}, u32[]{:S(2)}, u32[]{:S(2)}) collective-permute-start(bf16[9,128,128]{2,1,0:T(8,128)(2,1)S(1)} %get-tuple-element.15.own_b), channel_id=1, source_target_pairs={{0,28},{4,8},{8,4},{12,16},{16,12},{20,24},{24,20},{28,0},{1,29},{... | collective-permute-start | bytes 884744 | tf_op jit(solution)/shard_map/ppermute | solution.py:320
  29.4 0.7 %copy-start.11 = (bf16[9,128,128]{2,1,0:T(8,128)(2,1)}, bf16[9,128,128]{2,1,0:T(8,128)(2,1)S(1)}, u32[]{:S(2)}) copy-start(bf16[9,128,128]{2,1,0:T(8,128)(2,1)S(1)} %collective-permute-done.1.got_b) | copy-start | bytes 884740
  30.2 2.3 %copy-start.5 = (bf16[16,9,128,128]{3,2,1,0:T(8,128)(2,1)S(1)}, bf16[16,9,128,128]{3,2,1,0:T(8,128)(2,1)}, u32[]{:S(2)}) copy-start(bf16[16,9,128,128]{3,2,1,0:T(8,128)(2,1)} %tiles_ref.1) | copy-start | bytes 14155780
  32.5 1.0 %copy-start.12 = (bf16[9,128,128]{2,1,0:T(8,128)(2,1)S(1)}, bf16[9,128,128]{2,1,0:T(8,128)(2,1)}, u32[]{:S(2)}) copy-start(bf16[9,128,128]{2,1,0:T(8,128)(2,1)} %copy-done.11) | copy-start | bytes 884740
  38.1 2.0 %collective-permute-start.2 = (bf16[128,128]{1,0:T(8,128)(2,1)S(1)}, bf16[128,128]{1,0:T(8,128)(2,1)S(1)}, u32[]{:S(2)}, u32[]{:S(2)}) collective-permute-start(bf16[128,128]{1,0:T(8,128)(2,1)S(1)} %get-tuple-element.20), channel_id=1, source_target_pairs={{0,4},{4,0},{8,12},{12,8},{16,20},{20,16},{24,28},{28,24},{1,5},{5... | collective-permute-start | bytes 98312 | tf_op jit(solution)/shard_map/ppermute | solution.py:334
  38.2 4.3 %collective-permute-start.3 = (bf16[128,128]{1,0:T(8,128)(2,1)S(1)}, bf16[128,128]{1,0:T(8,128)(2,1)S(1)}, u32[]{:S(2)}, u32[]{:S(2)}) collective-permute-start(bf16[128,128]{1,0:T(8,128)(2,1)S(1)} %get-tuple-element.19), channel_id=1, source_target_pairs={{0,28},{4,8},{8,4},{12,16},{16,12},{20,24},{24,20},{28,0},{1,29},{... | collective-permute-start | bytes 98312 | tf_op jit(solution)/shard_map/ppermute | solution.py:335
  42.5 2.8 %copy-start.1 = (bf16[16,384,512]{2,1,0:T(8,128)(2,1)S(1)}, bf16[16,384,512]{2,1,0:T(8,128)(2,1)}, u32[]{:S(2)}) copy-start(bf16[16,384,512]{2,1,0:T(8,128)(2,1)} %copy-done) | copy-start | bytes 18874372
  50.2 6.4 %collective-permute-start.4 = (bf16[4,16,512]{2,1,0:T(8,128)(2,1)S(1)}, bf16[4,16,512]{2,1,0:T(8,128)(2,1)S(1)}, u32[]{:S(2)}, u32[]{:S(2)}) collective-permute-start(bf16[4,16,512]{2,1,0:T(8,128)(2,1)S(1)} %get-tuple-element.21), channel_id=1, source_target_pairs={{0,1},{1,2},{2,3},{3,0},{4,5},{5,6},{6,7},{7,4},{8,9},{9,10},{10,1... | collective-permute-start | bytes 196616 | tf_op jit(solution)/shard_map/ppermute | solution.py:342
  52.0 7.1 %collective-permute-start.5 = (bf16[4,16,512]{2,1,0:T(8,128)(2,1)S(1)}, bf16[4,16,512]{2,1,0:T(8,128)(2,1)S(1)}, u32[]{:S(2)}, u32[]{:S(2)}) collective-permute-start(bf16[4,16,512]{2,1,0:T(8,128)(2,1)S(1)} %get-tuple-element.23), channel_id=1, source_target_pairs={{0,2},{1,3},{2,0},{3,1},{4,6},{5,7},{6,4},{7,5},{8,10},{9,11},{10,... | collective-permute-start | bytes 196616 | tf_op jit(solution)/shard_map/ppermute | solution.py:342
  54.6 4.7 %collective-permute-start.6 = (bf16[4,16,512]{2,1,0:T(8,128)(2,1)S(1)}, bf16[4,16,512]{2,1,0:T(8,128)(2,1)S(1)}, u32[]{:S(2)}, u32[]{:S(2)}) collective-permute-start(bf16[4,16,512]{2,1,0:T(8,128)(2,1)S(1)} %get-tuple-element.22), channel_id=1, source_target_pairs={{0,3},{1,0},{2,1},{3,2},{4,7},{5,4},{6,5},{7,6},{8,11},{9,8},{10,9... | collective-permute-start | bytes 196616 | tf_op jit(solution)/shard_map/ppermute | solution.py:342

commit v2 on v0

v2 whole, which is shorter than its diff:
```python
import functools

import jax
import jax.numpy as jnp
from jax import lax
from jax.experimental import pallas as pl
from jax.experimental.pallas import tpu as pltpu
from jax.sharding import PartitionSpec as P


BLOCK = 128
HI = 128
INTP = 3
RATIO = 4
CHUNK = RATIO * BLOCK
WIN = 3 * BLOCK
REACH = 2 * HI + 32
F32 = jnp.float32
BF16 = jnp.bfloat16
VMEM = pltpu.VMEM
ANY = pl.BlockSpec(memory_space=pl.ANY)
IN_VMEM = pl.BlockSpec(memory_space=pltpu.VMEM)
IN_SMEM = pl.BlockSpec(memory_space=pltpu.SMEM)


def in_hbm(x):
    return pltpu.with_memory_space_constraint(x, pltpu.HBM)


def call(kernel, in_specs, out_specs, out_shape, scratch, flops, aliases=None):
    return pl.pallas_call(
        kernel,
        in_specs=in_specs,
        out_specs=out_specs,
        out_shape=out_shape,
        scratch_shapes=scratch,
        input_output_aliases=aliases or {},
        compiler_params=pltpu.CompilerParams(vmem_limit_bytes=16 * 1024 * 1024),
        cost_estimate=pl.CostEstimate(flops=flops, bytes_accessed=0, transcendentals=0),
    )


def groups(steps, unroll, body):
    unroll = unroll if steps % unroll == 0 else 1

    def group(g, carry):
        for j in range(unroll):
            body(g * unroll + j)
        return carry

    lax.fori_loop(0, steps // unroll, group, 0)


def build_table(local, weight, table_ref):
    i0, i1, i2 = local[0:1], local[1:2], local[2:3]
    w0, w1, w2 = weight[0:1], weight[1:2], weight[2:3]
    zero = jnp.zeros_like(w0)
    w0 = w0 + jnp.where(i1 == i0, w1, zero) + jnp.where(i2 == i0, w2, zero)
    w1 = w1 + jnp.where(i2 == i1, w2, zero)
    rows = REACH // 16
    iota = lax.broadcasted_iota(jnp.int32, (rows, 16, BLOCK), 0) * 16 + lax.broadcasted_iota(
        jnp.int32, (rows, 16, BLOCK), 1
    )
    iota = iota.astype(jnp.int16)
    for s in range(CHUNK // BLOCK):
        cols = slice(s * BLOCK, (s + 1) * BLOCK)
        base = s * BLOCK // RATIO

        def wide(x, kind):
            return jnp.broadcast_to(x[:, cols], (16, BLOCK)).astype(kind)[None]

        table = jnp.zeros((1, 16, BLOCK), BF16)
        for index, value in ((i2, w2), (i1, w1), (i0, w0)):
            table = jnp.where(wide(index - base, jnp.int16) == iota, wide(value, BF16), table)
        table_ref[base : base + REACH, cols] = table.reshape(REACH, BLOCK)
        if base:
            table_ref[0:base, cols] = jnp.zeros((base, BLOCK), BF16)
        if base + REACH < WIN:
            table_ref[base + REACH : WIN, cols] = jnp.zeros((WIN - base - REACH, BLOCK), BF16)


def spread_kernel(steps, done, unroll, chunks, *refs):
    first = done == 0
    if first:
        info_ref, anom_hbm, incr_hbm, index_hbm, weight_hbm = refs[:5]
        table_ref, anom_ref, out_ref, carry_ref = refs[5:9]
        incr_ref, index_ref, weight_ref, acc_ref, anom_sem, incr_sem, some_sem = refs[9:]
    else:
        info_ref, anom_hbm, incr_hbm, index_hbm, weight_hbm, tiles_hbm, carry_ref = refs[:7]
        table_ref, anom_ref, out_ref, tiles_ref = refs[9:13]
        incr_ref, index_ref, weight_ref, acc_ref, anom_sem, incr_sem, some_sem = refs[13:]
    flip = info_ref[0] == 1
    low = jnp.where(flip, chunks - done - steps, done)

    def chunk_of(i):
        return jnp.where(flip, chunks - 1 - done - i, done + i)

    def lanes(c, count=1):
        return pl.ds(pl.multiple_of(c * CHUNK, CHUNK), count * CHUNK)

    index_copy = pltpu.make_async_copy(index_hbm.at[:, lanes(low, steps)], index_ref, some_sem.at[0])
    weight_copy = pltpu.make_async_copy(
        weight_hbm.at[:, lanes(low, steps)], weight_ref, some_sem.at[1]
    )
    index_copy.start()
    weight_copy.start()

    def chunk_copies(i):
        c = chunk_of(i)
        return (
            pltpu.make_async_copy(anom_hbm.at[:, :, lanes(c)], anom_ref.at[c], anom_sem.at[i]),
            pltpu.make_async_copy(incr_hbm.at[:, lanes(c)], incr_ref.at[i], incr_sem.at[i]),
        )

    for i in range(steps):
        for copy in chunk_copies(i):
            copy.start()
    if first:
        acc_ref[...] = jnp.zeros(acc_ref.shape, F32)
    else:
        tiles_copy = pltpu.make_async_copy(tiles_hbm, tiles_ref, some_sem.at[2])
        tiles_copy.start()
        acc_ref[...] = carry_ref[...]
    index_copy.wait()
    weight_copy.wait()
    rows = anom_ref.shape[1] * anom_ref.shape[2]
    total = steps if first else steps + 2

    def group(g, carry):
        acc0, acc1 = acc_ref[0], acc_ref[1]
        steps_here = [g * unroll + j for j in range(unroll)]
        for i in steps_here:
            for copy in chunk_copies(i):
                copy.wait()
        for i in steps_here:
            c = chunk_of(i)
            here = lanes(c - low)
            build_table(index_ref[:, here] - c * BLOCK, weight_ref[:, here], table_ref.at[c])
            weighted = (anom_ref[c].astype(F32) * incr_ref[i][None]).astype(BF16)
            window = lax.dot_general(
                table_ref[c],
                weighted.reshape(rows, CHUNK),
                (((1,), (1,)), ((), ())),
                preferred_element_type=F32,
            )
            near, mid, far = window[:BLOCK], window[BLOCK : 2 * BLOCK], window[2 * BLOCK :]
            ready = acc0 + jnp.where(flip, far, near)
            out_ref[jnp.where(flip, total - 1 - i, i)] = ready.T.astype(BF16)
            acc0 = acc1 + mid
            acc1 = jnp.where(flip, near, far)
        acc_ref[0] = acc0
        acc_ref[1] = acc1
        return carry

    lax.fori_loop(0, steps // unroll, group, 0)
    if first:
        carry_ref[...] = acc_ref[...]
    else:
        out_ref[jnp.where(flip, 1, steps)] = acc_ref[0].T.astype(BF16)
        out_ref[jnp.where(flip, 0, steps + 1)] = acc_ref[1].T.astype(BF16)
        tiles_copy.wait()


def spread_call(steps, done, unroll, info, anomalies, increment, index, weight, extra=()):
    members, fields, columns = anomalies.shape
    rows = members * fields
    chunks = columns // CHUNK
    first = done == 0
    in_specs = [IN_SMEM, ANY, ANY, ANY, ANY]
    out_shape = [
        VMEM((chunks, WIN, CHUNK), BF16),
        VMEM((chunks, members, fields, CHUNK), BF16),
        jax.ShapeDtypeStruct((chunks // 2 + 1, rows, BLOCK), BF16),
    ]
    aliases = {}
    if first:
        out_shape.append(VMEM((2, BLOCK, rows), F32))
    else:
        in_specs += [ANY, IN_VMEM, IN_VMEM, IN_VMEM]
        out_shape.append(VMEM(extra[0].shape, BF16))
        aliases = {7: 0, 8: 1}
    return call(
        functools.partial(spread_kernel, steps, done, unroll, chunks),
        in_specs,
        [IN_VMEM] * 4,
        out_shape,
        [
            VMEM((steps, fields, CHUNK), F32),
            VMEM((INTP, steps * CHUNK), jnp.int32),
            VMEM((INTP, steps * CHUNK), F32),
            VMEM((2, BLOCK, rows), F32),
            pltpu.SemaphoreType.DMA((steps,)),
            pltpu.SemaphoreType.DMA((steps,)),
            pltpu.SemaphoreType.DMA((3,)),
        ],
        2 * rows * steps * WIN * CHUNK,
        aliases,
    )(info, in_hbm(anomalies), in_hbm(increment), in_hbm(index), in_hbm(weight), *extra)


def convolve(wide_ref, tiles_ref, nbr_ref, smooth_ref, b):
    count = tiles_ref.shape[1]
    picked = jnp.concatenate([wide_ref[nbr_ref[n, b]] for n in range(count)], axis=1)
    weights = tiles_ref[b].reshape(count * BLOCK, BLOCK)
    smooth = jnp.dot(picked, weights, preferred_element_type=F32)
    smooth_ref[b + 1] = smooth.astype(BF16)


def conv_early_kernel(
    unroll, info_ref, nbr_ref, own_a, own_b, got_a, tiles_ref, wide_ref, smooth_ref, edge_ref
):
    half = own_a.shape[0]
    reach = half - 1
    blocks = tiles_ref.shape[0]
    top = blocks + reach
    flip = info_ref[0] == 1

    @pl.when(jnp.logical_not(flip))
    def _():
        wide_ref[reach - 1 : reach - 1 + half] = own_b[...]
        wide_ref[reach - 1 + half : top - 1] = own_a[0 : half - 2]
        wide_ref[top - 1 : top + 1] = (
            got_a[0:2].astype(F32) + own_a[half - 2 : half].astype(F32)
        ).astype(BF16)
        wide_ref[top + 1 : top + reach] = got_a[2:half]

    @pl.when(flip)
    def _():
        wide_ref[0 : reach - 1] = got_a[0 : reach - 1]
        wide_ref[reach - 1 : reach + 1] = (
            got_a[reach - 1 : reach + 1].astype(F32) + own_a[0:2].astype(F32)
        ).astype(BF16)
        wide_ref[reach + 1 : reach - 1 + half] = own_a[2:half]
        wide_ref[reach - 1 + half : top + 1] = own_b[...]

    early = blocks - half
    start = jnp.where(flip, 0, half)
    groups(
        early, unroll, lambda i: convolve(wide_ref, tiles_ref, nbr_ref, smooth_ref, start + i)
    )
    edge_ref[...] = smooth_ref[jnp.where(flip, 1, blocks)]


def conv_late_kernel(
    unroll, info_ref, nbr_ref, got_b, tiles_ref, wide_in, smooth_in, wide_ref, smooth_ref, edge_ref
):
    half = got_b.shape[0]
    reach = half - 1
    blocks = tiles_ref.shape[0]
    top = blocks + reach
    flip = info_ref[0] == 1
    present = info_ref[1] == 1
    beyond = jnp.where(present, got_b[...], jnp.zeros(got_b.shape, BF16))

    @pl.when(jnp.logical_not(flip))
    def _():
        wide_ref[0 : reach - 1] = beyond[0 : reach - 1]
        both = wide_ref[reach - 1 : reach + 1].astype(F32) + beyond[reach - 1 :].astype(F32)
        wide_ref[reach - 1] = jnp.where(present, both[0], jnp.zeros_like(both[0])).astype(BF16)
        wide_ref[reach] = both[1].astype(BF16)

    @pl.when(flip)
    def _():
        wide_ref[top + 1 : top + reach] = beyond[2:half]
        both = wide_ref[top - 1 : top + 1].astype(F32) + beyond[0:2].astype(F32)
        wide_ref[top - 1] = both[0].astype(BF16)
        wide_ref[top] = jnp.where(present, both[1], jnp.zeros_like(both[1])).astype(BF16)

    start = jnp.where(flip, blocks - half, 0)
    groups(half, unroll, lambda i: convolve(wide_ref, tiles_ref, nbr_ref, smooth_ref, start + i))
    edge_ref[...] = smooth_ref[jnp.where(flip, blocks, 1)]


def conv_early_call(info, neighbours, own_a, own_b, got_a, tiles):
    blocks, count = tiles.shape[:2]
    half, rows, _ = own_a.shape
    early = blocks - half
    return call(
        functools.partial(conv_early_kernel, early),
        [IN_SMEM, IN_SMEM] + [IN_VMEM] * 4,
        [IN_VMEM] * 3,
        [
            VMEM((blocks + 2 * half - 2, rows, BLOCK), BF16),
            VMEM((blocks + 2, rows, BLOCK), BF16),
            jax.ShapeDtypeStruct((rows, BLOCK), BF16),
        ],
        [],
        2 * rows * early * count * BLOCK * BLOCK,
    )(info, neighbours, own_a, own_b, got_a, tiles)


def conv_late_call(info, neighbours, got_b, tiles, wide, smooth):
    _, count = tiles.shape[:2]
    half, rows, _ = got_b.shape
    return call(
        functools.partial(conv_late_kernel, 3),
        [IN_SMEM, IN_SMEM] + [IN_VMEM] * 4,
        [IN_VMEM] * 3,
        [
            VMEM(wide.shape, BF16),
            VMEM(smooth.shape, BF16),
            jax.ShapeDtypeStruct((rows, BLOCK), BF16),
        ],
        [],
        2 * rows * half * count * BLOCK * BLOCK,
        {4: 0, 5: 1},
    )(info, neighbours, got_b, tiles, wide, smooth)


def back_kernel(part, steps, unroll, per, *refs):
    if part == 0:
        info_ref, got_ref, table_ref, anom_ref, _, smooth_ref, out_ref = refs
    elif part == 1:
        info_ref, table_ref, anom_ref, smooth_ref, _, out_ref = refs
    else:
        info_ref, got_ref, table_ref, anom_ref, _, _, smooth_ref, out_ref = refs
    flip = info_ref[0] == 1
    blocks = table_ref.shape[0]
    if part == 0:
        smooth_ref[jnp.where(flip, 0, blocks + 1)] = got_ref[...]
        start = jnp.where(flip, 0, blocks - steps)
    elif part == 1:
        start = jnp.where(flip, blocks - 1 - steps, 1)
    else:
        got = got_ref[...]
        present = info_ref[1] == 1
        smooth_ref[jnp.where(flip, blocks + 1, 0)] = jnp.where(present, got, jnp.zeros_like(got))
        start = jnp.where(flip, blocks - 1, 0)

    def body(i):
        c = start + i
        lhs = jnp.concatenate([smooth_ref[c], smooth_ref[c + 1], smooth_ref[c + 2]], axis=1)
        returned = jnp.dot(lhs, table_ref[c], preferred_element_type=F32)
        anom = anom_ref[c].astype(F32)
        value = jnp.sum(anom * returned.reshape(anom.shape), axis=0)
        lane = pl.multiple_of(lax.rem(c, per) * CHUNK, CHUNK)
        out_ref[lax.div(c, per), :, pl.ds(lane, CHUNK)] = value.astype(BF16)

    groups(steps, unroll, body)


def back_call(part, steps, unroll, shares, info, got, table, anom, smooth, out=None):
    chunks, members, fields, _ = anom.shape
    per = chunks // shares
    operands = [info] + ([] if part == 1 else [got]) + [table, anom, smooth]
    in_specs = [IN_SMEM] + [IN_VMEM] * (len(operands) - 1)
    out_type = VMEM((shares, fields, per * CHUNK), BF16)
    if part == 2:
        out_type = jax.ShapeDtypeStruct(out_type.shape, BF16)
    smooth_type = VMEM(smooth.shape, BF16)
    last = len(operands) - 1
    if part == 0:
        out_shape, aliases = [smooth_type, out_type], {last: 0}
    elif part == 1:
        operands, in_specs = operands + [out], in_specs + [IN_VMEM]
        out_shape, aliases = [out_type], {last + 1: 0}
    else:
        operands, in_specs = operands + [out], in_specs + [IN_VMEM]
        out_shape, aliases = [smooth_type, out_type], {last: 0, last + 1: 1}
    return call(
        functools.partial(back_kernel, part, steps, unroll, per),
        in_specs,
        [IN_VMEM] * len(out_shape),
        out_shape,
        [],
        2 * members * fields * steps * WIN * CHUNK,
        aliases,
    )(*operands)


def swaps(count):
    inner = [(i, i ^ 1) for i in range(count)]
    outer = [(i, (i + 1) % count if i % 2 else (i - 1) % count) for i in range(count)]
    return inner, outer


def swap(value, pairs):
    return lax.ppermute(value, "space", pairs)


def shards(increment, anomalies, interp_index, interp_weight, neighbour_blocks, tiles):
    members, _, columns = anomalies.shape
    chunks = columns // CHUNK
    space = lax.axis_index("space")
    count = lax.axis_size("space")
    mem = lax.axis_index("mem")
    shares = lax.axis_size("mem")
    assert count % 2 == 0
    flip = space % 2
    inner, outer = swaps(count)
    head = chunks // 2 + 1
    present = jnp.where(flip == 1, space < count - 1, space > 0)
    info = jnp.stack([flip, present.astype(jnp.int32)]).astype(jnp.int32)
    columns_in = (anomalies, increment, interp_index, interp_weight)
    table, anom, own_b, carry = spread_call(head, 0, 3, info, *columns_in)
    got_b = swap(own_b, outer)
    table, anom, own_a, tiles_here = spread_call(
        chunks - head, head, 1, info, *columns_in, (in_hbm(tiles), carry, table, anom)
    )
    got_a = swap(own_a, inner)
    wide, smooth, edge_a = conv_early_call(info, neighbour_blocks, own_a, own_b, got_a, tiles_here)
    halo_a = swap(edge_a, inner)
    smooth, out = back_call(0, chunks - head - 1, 3, shares, info, halo_a, table, anom, smooth)
    wide, smooth, edge_b = conv_late_call(info, neighbour_blocks, got_b, tiles_here, wide, smooth)
    halo_b = swap(edge_b, outer)
    (out,) = back_call(1, head, 3, shares, info, None, table, anom, smooth, out)
    _, pieces = back_call(2, 1, 1, shares, info, halo_b, table, anom, smooth, out)

    def piece_of(share):
        return lax.dynamic_index_in_dim(pieces, share, 0, False)

    total = piece_of(mem).astype(F32)
    for shift in range(1, shares):
        got = lax.ppermute(
            piece_of((mem + shift) % shares),
            "mem",
            [(i, (i + shift) % shares) for i in range(shares)],
        )
        total = total + got.astype(F32)
    return total / (members * shares - 1)


def solution(mesh):
    in_specs = (
        P(None, "space"),
        P("mem", None, "space"),
        P(None, "space"),
        P(None, "space"),
        P(None, "space"),
        P("space", None, None, None),
    )
    out_specs = P(None, ("space", "mem"))
    return jax.shard_map(shards, mesh=mesh, in_specs=in_specs, out_specs=out_specs, check_vma=False)
```

time: 154 us -> 50.4 us (0.33)
  matrix products: 61.8 us -> 0 us
  waiting for transfers between devices: 28.1 us -> 5.85 us
  Pallas kernels: 0 us -> 16.4 us
  other arithmetic: 14.4 us -> 0.77 us
  between operations: 13.7 us -> 0.12 us
  local copies, waits for them, and re-layouts: 22.5 us -> 16.1 us
  starting transfers between devices: 12.6 us -> 10.9 us
    dot_general x4 -> x0, matrix products: 61.8 us -> none  [the longest x1 31.4 us: shards(): jnp.einsum('rcj,cpj->rcp', weighted, table, precision=lax.Precision.HIGHEST)]
    reduce_scatter x1 -> x0, waiting for transfers between devices: 23.6 us -> none  [shards(): lax.psum_scatter(partial_value.astype(jnp.bfloat16), 'mem', scatter_dimen...]
    pallas_call x0 -> x7, Pallas kernels: none -> 16.4 us  [the longest x2 9.27 us: spread_call(): call(functools.partial(spread_kernel, steps, done, unroll, chunks), in_sp...]
    unnamed x8 -> x28, local copies, waits for them, and re-layouts: 6.48 us -> 16 us
    reshape x2 -> x0, local copies, waits for them, and re-layouts: 6.09 us -> none  [the longest x1 5.12 us: shards(): returned.reshape(mem_dev, n_fields, columns)]
    transpose x1 -> x0, local copies, waits for them, and re-layouts: 5.51 us -> none  [shards(): jnp.einsum('rcp,cpj->rcj', windows, table, precision=lax.Precision.HIGHEST)]
    slice x5 -> x0, local copies, waits for them, and re-layouts: 4.05 us -> none  [the longest x1 1.37 us: shards(): pieces[:, :col_blocks]]
    reduce_sum x1 -> x0, other arithmetic: 3.43 us -> none  [shards(): jnp.sum(anomalies.astype(jnp.float32) * returned.reshape(mem_dev, n_field...]
  transfers between devices with their start and end apart: 5 -> 7, of which waited for: 3 -> 5; matrix products, arithmetic and copies ran while one was open for 1% -> 0% of each run, Pallas kernels for 0% -> 9%
where the time goes in v2:
time: 50.4 us; the launch traced here: 50.1 us
  Pallas kernels  16.4 us (33%)
  local copies, waits for them, and re-layouts  16.1 us (32%)
  starting transfers between devices  10.9 us (22%)
  waiting for transfers between devices  5.85 us (12%)
  other arithmetic  0.77 us (2%)
    unnamed x28, local copies, waits for them, and re-layouts  16 us
    pallas_call x2, Pallas kernels, spread_call(): call(functools.partial(spread_kernel, steps, done, unroll, chunks), in_sp...  9.27 us
    ppermute x3, starting transfers between devices, shards(): lax.ppermute(piece_of((mem + shift) % shares), 'mem', [(i, (i + shift) %...  5.56 us
    ppermute x4, starting transfers between devices, swap(): return lax.ppermute(value, 'space', pairs)  5.33 us
    pallas_call x3, Pallas kernels, back_call(): call(functools.partial(back_kernel, part, steps, unroll, per), in_specs,...  3.74 us
    ppermute x3, waiting for transfers between devices, shards(): lax.ppermute(piece_of((mem + shift) % shares), 'mem', [(i, (i + shift) %...  3.32 us
    ppermute x4, waiting for transfers between devices, swap(): return lax.ppermute(value, 'space', pairs)  2.54 us
    pallas_call x1, Pallas kernels, conv_late_call(): call(functools.partial(conv_late_kernel, 3), [IN_SMEM, IN_SMEM] + [IN_VME...  1.94 us
  transfers between devices with their start and end apart: 7, of which 5 were waited for; matrix products, arithmetic and copies ran while one was open for 0% of the time, Pallas kernels for 9%

profile of v2, /device:TPU:0, one launch (start us, length us, event | category | flops | bytes accessed | tf_op | source)
XLA Modules:
  0.0 50.1 jit_solution(3583147847640463325)
XLA Ops:
  0.0 0.1 pad_add_fusion.refs_0_.info_ref
  0.1 4.6 %shard_map.64 = (bf16[16,384,512]{2,1,0:T(8,128)(2,1)S(1)}, bf16[16,8,16,512]{3,2,1,0:T(8,128)(2,1)S(1)}, bf16[9,128,128]{2,1,0:T(8,128)(2,1)S(1)}, f32[2,128,128]{2,1,0:T(8,128)S(1)}) custom-call(s32[2]{0:T(128)S(1)} %pad_add_fusion.refs_0_.info_ref, bf16[8,16,8192]{2,1,0:T(8,128)(2,1)} %refs_1_.3, f32[16,8192]{1,0:T(8,128)} %refs_2_.3, s32[3,8192]{1,0:T(4,128)} %refs_3_.3, ...), custom_call_target="tpu_custom_call" | custom-call | flops 452984832 | tf_op jit(solution)/shard_map/pallas_call | solution.py:182
  4.7 0.0 copy-start.11
  4.7 4.7 %shard_map.65 = (bf16[16,384,512]{2,1,0:T(8,128)(2,1)S(1)}, bf16[16,8,16,512]{3,2,1,0:T(8,128)(2,1)S(1)}, bf16[9,128,128]{2,1,0:T(8,128)(2,1)S(1)}, bf16[16,9,128,128]{3,2,1,0:T(8,128)(2,1)S(1)}) custom-call(s32[2]{0:T(128)S(1)} %pad_add_fusion.refs_0_.info_ref, bf16[8,16,8192]{2,1,0:T(8,128)(2,1)} %refs_1_.3, ...), custom_call_target="tpu_custom_call", output_to_operand_aliasing={{0}: (7, {}), {1}: (8, {})} | custom-call | flops 352321536 | tf_op jit(solution)/shard_map/pallas_call | solution.py:182
  9.4 0.0 copy-start
  9.4 2.6 %copy-done = bf16[16,384,512]{2,1,0:T(8,128)(2,1)} copy-done((bf16[16,384,512]{2,1,0:T(8,128)(2,1)}, bf16[16,384,512]{2,1,0:T(8,128)(2,1)S(1)}, u32[]{:S(2)}) %copy-start) | copy-done | bytes 6291480
  12.0 0.0 copy-start.2
  12.0 1.4 %copy-done.2 = bf16[16,8,16,512]{3,2,1,0:T(8,128)(2,1)} copy-done((bf16[16,8,16,512]{3,2,1,0:T(8,128)(2,1)}, bf16[16,8,16,512]{3,2,1,0:T(8,128)(2,1)S(1)}, u32[]{:S(2)}) %copy-start.2) | copy-done | bytes 2097176
  13.4 0.5 collective-permute-start.1
  13.9 3.5 %collective-permute-start = (bf16[9,128,128]{2,1,0:T(8,128)(2,1)S(1)}, bf16[9,128,128]{2,1,0:T(8,128)(2,1)S(1)}, u32[]{:S(2)}, u32[]{:S(2)}) collective-permute-start(bf16[9,128,128]{2,1,0:T(8,128)(2,1)S(1)} %get-tuple-element.21.own_b), channel_id=1, source_target_pairs={{0,28},{4,8},{8,4},{12,16},{16,12},{20,24},{24,20},{28,0},{1,29},{... | collective-permute-start | bytes 884744 | tf_op jit(solution)/shard_map/ppermute | solution.py:378
  17.5 0.0 collective-permute-done.1.got_a
  17.5 0.0 copy-done.11
  17.5 0.0 slice-start
  17.5 1.5 %shard_map.66 = (bf16[32,128,128]{2,1,0:T(8,128)(2,1)S(1)}, bf16[18,128,128]{2,1,0:T(8,128)(2,1)S(1)}, bf16[128,128]{1,0:T(8,128)(2,1)S(1)}) custom-call(s32[2]{0:T(128)S(1)} %pad_add_fusion.refs_0_.info_ref, s32[9,16]{1,0:T(8,128)S(1)} %copy-done.11, bf16[9,128,128]{2,1,0:T(8,128)(2,1)S(1)} %get-tuple-element.26.own_a, ...), custom_call_target="tpu_custom_call" | custom-call | flops 264241152 | tf_op jit(solution)/shard_map/pallas_call | solution.py:278
  18.9 0.0 copy-start.5
  18.9 2.2 %copy-done.5 = bf16[16,9,128,128]{3,2,1,0:T(8,128)(2,1)} copy-done((bf16[16,9,128,128]{3,2,1,0:T(8,128)(2,1)}, bf16[16,9,128,128]{3,2,1,0:T(8,128)(2,1)S(1)}, u32[]{:S(2)}) %copy-start.5) | copy-done | bytes 4718616
  21.2 0.0 copy-start.7
  21.2 1.0 %copy-done.7 = bf16[32,128,128]{2,1,0:T(8,128)(2,1)} copy-done((bf16[32,128,128]{2,1,0:T(8,128)(2,1)}, bf16[32,128,128]{2,1,0:T(8,128)(2,1)S(1)}, u32[]{:S(2)}) %copy-start.7) | copy-done | bytes 1048600
  22.1 0.0 collective-permute-start.2
  22.1 1.2 %collective-permute-done.2.refs_1_ = bf16[128,128]{1,0:T(8,128)(2,1)S(1)} collective-permute-done((bf16[128,128]{1,0:T(8,128)(2,1)S(1)}, bf16[128,128]{1,0:T(8,128)(2,1)S(1)}, u32[]{:S(2)}, u32[]{:S(2)}) %collective-permute-start.2) | collective-permute-done | bytes 32800 | tf_op jit(solution)/shard_map/ppermute | solution.py:378
  23.3 0.0 copy-start.9
  23.4 0.6 %copy-done.9 = bf16[128,128]{1,0:T(8,128)(2,1)} copy-done((bf16[128,128]{1,0:T(8,128)(2,1)}, bf16[128,128]{1,0:T(8,128)(2,1)S(1)}, u32[]{:S(2)}) %copy-start.9) | copy-done | bytes 32792
  24.0 0.0 copy-start.1
  24.0 2.8 %copy-done.1 = bf16[16,384,512]{2,1,0:T(8,128)(2,1)S(1)} copy-done((bf16[16,384,512]{2,1,0:T(8,128)(2,1)S(1)}, bf16[16,384,512]{2,1,0:T(8,128)(2,1)}, u32[]{:S(2)}) %copy-start.1) | copy-done | bytes 6291480
  26.8 0.0 copy-start.3
  26.8 1.6 %copy-done.3 = bf16[16,8,16,512]{3,2,1,0:T(8,128)(2,1)S(1)} copy-done((bf16[16,8,16,512]{3,2,1,0:T(8,128)(2,1)S(1)}, bf16[16,8,16,512]{3,2,1,0:T(8,128)(2,1)}, u32[]{:S(2)}) %copy-start.3) | copy-done | bytes 2097176
  28.3 0.0 copy-start.10
  28.3 0.8 %copy-done.10 = bf16[128,128]{1,0:T(8,128)(2,1)S(1)} copy-done((bf16[128,128]{1,0:T(8,128)(2,1)S(1)}, bf16[128,128]{1,0:T(8,128)(2,1)}, u32[]{:S(2)}) %copy-start.10) | copy-done | bytes 32792
  29.1 1.3 %shard_map.67 = (bf16[18,128,128]{2,1,0:T(8,128)(2,1)S(1)}, bf16[4,16,2048]{2,1,0:T(8,128)(2,1)S(1)}) custom-call(s32[2]{0:T(128)S(1)} %pad_add_fusion.refs_0_.info_ref, bf16[128,128]{1,0:T(8,128)(2,1)S(1)} %copy-done.10, bf16[16,384,512]{2,1,0:T(8,128)(2,1)S(1)} %copy-done.1, ...), custom_call_target="tpu_custom_call", output_to_operand_aliasing={{0}: (4, {})} | custom-call | flops 301989888 | tf_op jit(solution)/shard_map/pallas_call | solution.py:360
  30.4 0.0 copy-start.4
  30.4 0.0 collective-permute-done.got_b
  30.4 1.0 %copy-done.6 = bf16[16,9,128,128]{3,2,1,0:T(8,128)(2,1)S(1)} copy-done((bf16[16,9,128,128]{3,2,1,0:T(8,128)(2,1)S(1)}, bf16[16,9,128,128]{3,2,1,0:T(8,128)(2,1)}, u32[]{:S(2)}) %copy-start.6) | copy-done | bytes 4718616
  31.4 2.0 %copy-done.8 = bf16[32,128,128]{2,1,0:T(8,128)(2,1)S(1)} copy-done((bf16[32,128,128]{2,1,0:T(8,128)(2,1)S(1)}, bf16[32,128,128]{2,1,0:T(8,128)(2,1)}, u32[]{:S(2)}) %copy-start.8) | copy-done | bytes 1048600
  33.5 1.9 %shard_map.68 = (bf16[32,128,128]{2,1,0:T(8,128)(2,1)S(1)}, bf16[18,128,128]{2,1,0:T(8,128)(2,1)S(1)}, bf16[128,128]{1,0:T(8,128)(2,1)S(1)}) custom-call(s32[2]{0:T(128)S(1)} %pad_add_fusion.refs_0_.info_ref, s32[9,16]{1,0:T(8,128)S(1)} %copy-done.11, ...), custom_call_target="tpu_custom_call", output_to_operand_aliasing={{0}: (4, {}), {1}: (5, {})} | custom-call | flops 339738624 | tf_op jit(solution)/shard_map/pallas_call | solution.py:295
  35.4 1.3 %collective-permute-start.3 = (bf16[128,128]{1,0:T(8,128)(2,1)S(1)}, bf16[128,128]{1,0:T(8,128)(2,1)S(1)}, u32[]{:S(2)}, u32[]{:S(2)}) collective-permute-start(bf16[128,128]{1,0:T(8,128)(2,1)S(1)} %get-tuple-element.33), channel_id=1, source_target_pairs={{0,28},{4,8},{8,4},{12,16},{16,12},{20,24},{24,20},{28,0},{1,29},{... | collective-permute-start | bytes 98312 | tf_op jit(solution)/shard_map/ppermute | solution.py:378
  36.7 0.0 slice-done
  36.7 0.0 slice-done.1
  36.7 0.0 copy-done.4
  36.7 1.7 %shard_map.69.refs_5_ = bf16[4,16,2048]{2,1,0:T(8,128)(2,1)S(1)} custom-call(s32[2]{0:T(128)S(1)} %pad_add_fusion.refs_0_.info_ref, bf16[16,384,512]{2,1,0:T(8,128)(2,1)S(1)} %bitcast.12, bf16[16,8,16,512]{3,2,1,0:T(8,128)(2,1)S(1)} %copy-done.4, bf16[18,128,128]{2,1,0:T(8,128)(2,1)S(1)} %get-tuple-element.34.refs_3_.refs_4_, ...), custom_call_target="tpu_custom_call", output_to_operand_aliasing={{}: (4, {})} | custom-call | flops 452984832 | tf_op jit(solution)/shard_map/pallas_call | solution.py:360
  38.4 1.3 %collective-permute-done.3.refs_1_ = bf16[128,128]{1,0:T(8,128)(2,1)S(1)} collective-permute-done((bf16[128,128]{1,0:T(8,128)(2,1)S(1)}, bf16[128,128]{1,0:T(8,128)(2,1)S(1)}, u32[]{:S(2)}, u32[]{:S(2)}) %collective-permute-start.3) | collective-permute-done | bytes 32800 | tf_op jit(solution)/shard_map/ppermute | solution.py:378
  39.7 0.8 %shard_map.70 = (bf16[18,128,128]{2,1,0:T(8,128)(2,1)S(1)}, bf16[4,16,2048]{2,1,0:T(8,128)(2,1)S(1)}) custom-call(s32[2]{0:T(128)S(1)} %pad_add_fusion.refs_0_.info_ref, bf16[128,128]{1,0:T(8,128)(2,1)S(1)} %collective-permute-done.3.refs_1_, bf16[16,384,512]{2,1,0:T(8,128)(2,1)S(1)} %bitcast.12, ...), custom_call_target="tpu_custom_call", output_to_operand_aliasing={{0}: (4, {}), {1}: (5, {})} | custom-call | flops 50331648 | tf_op jit(solution)/shard_map/pallas_call | solution.py:360
  40.5 1.6 %collective-permute-start.4 = (bf16[16,2048]{1,0:T(8,128)(2,1)S(1)}, bf16[16,2048]{1,0:T(8,128)(2,1)S(1)}, u32[]{:S(2)}, u32[]{:S(2)}) collective-permute-start(bf16[16,2048]{1,0:T(8,128)(2,1)S(1)} %get-tuple-element.37), channel_id=1, source_target_pairs={{0,1},{1,2},{2,3},{3,0},{4,5},{5,6},{6,7},{7,4},{8,9},{9,10},{10,1... | collective-permute-start | bytes 196616 | tf_op jit(solution)/shard_map/ppermute | solution.py:414
  42.1 2.6 %collective-permute-start.5 = (bf16[16,2048]{1,0:T(8,128)(2,1)S(1)}, bf16[16,2048]{1,0:T(8,128)(2,1)S(1)}, u32[]{:S(2)}, u32[]{:S(2)}) collective-permute-start(bf16[16,2048]{1,0:T(8,128)(2,1)S(1)} %get-tuple-element.39), channel_id=1, source_target_pairs={{0,2},{1,3},{2,0},{3,1},{4,6},{5,7},{6,4},{7,5},{8,10},{9,11},{10,... | collective-permute-start | bytes 196616 | tf_op jit(solution)/shard_map/ppermute | solution.py:414
  44.7 1.3 %collective-permute-start.6 = (bf16[16,2048]{1,0:T(8,128)(2,1)S(1)}, bf16[16,2048]{1,0:T(8,128)(2,1)S(1)}, u32[]{:S(2)}, u32[]{:S(2)}) collective-permute-start(bf16[16,2048]{1,0:T(8,128)(2,1)S(1)} %get-tuple-element.38), channel_id=1, source_target_pairs={{0,3},{1,0},{2,1},{3,2},{4,7},{5,4},{6,5},{7,6},{8,11},{9,8},{10,9... | collective-permute-start | bytes 196616 | tf_op jit(solution)/shard_map/ppermute | solution.py:414
  46.1 1.3 %collective-permute-done.4 = bf16[16,2048]{1,0:T(8,128)(2,1)S(1)} collective-permute-done((bf16[16,2048]{1,0:T(8,128)(2,1)S(1)}, bf16[16,2048]{1,0:T(8,128)(2,1)S(1)}, u32[]{:S(2)}, u32[]{:S(2)}) %collective-permute-start.4) | collective-permute-done | bytes 65568 | tf_op jit(solution)/shard_map/ppermute | solution.py:414
  47.4 2.0 %collective-permute-done.5 = bf16[16,2048]{1,0:T(8,128)(2,1)S(1)} collective-permute-done((bf16[16,2048]{1,0:T(8,128)(2,1)S(1)}, bf16[16,2048]{1,0:T(8,128)(2,1)S(1)}, u32[]{:S(2)}, u32[]{:S(2)}) %collective-permute-start.5) | collective-permute-done | bytes 65568 | tf_op jit(solution)/shard_map/ppermute | solution.py:414
  49.3 0.1 collective-permute-done.6
  49.4 0.7 %fusion.2 = f32[16,2048]{1,0:T(8,128)} fusion(bf16[16,2048]{1,0:T(8,128)(2,1)S(1)} %collective-permute-done.6, bf16[16,2048]{1,0:T(8,128)(2,1)S(1)} %collective-permute-done.5, bf16[16,2048]{1,0:T(8,128)(2,1)S(1)} %collective-permute-done.4, bf16[4,16,2048]{2,1,0:T(8,128)(2,1)S(1)} %get-tuple-element.36, s32[]{:T(128)S(6)} %select_n.38), kind=kLoop, calls=%fused_computation.3 | loop fusion | flops 262144 | bytes 393220 | tf_op jit(solution)/shard_map/div | solution.py:420
  (5 shorter events, 0.0 us)
Async XLA Ops:
  4.7 12.8 %copy-start.11 = (s32[9,16]{1,0:T(8,128)S(1)}, s32[9,16]{1,0:T(8,128)}, u32[]{:S(2)}) copy-start(s32[9,16]{1,0:T(8,128)} %nbr_ref.3) | copy-start | bytes 1732
  9.4 2.6 %copy-start = (bf16[16,384,512]{2,1,0:T(8,128)(2,1)}, bf16[16,384,512]{2,1,0:T(8,128)(2,1)S(1)}, u32[]{:S(2)}) copy-start(bf16[16,384,512]{2,1,0:T(8,128)(2,1)S(1)} %get-tuple-element.29.refs_2_.refs_1_) | copy-start | bytes 18874372
  12.0 1.4 %copy-start.2 = (bf16[16,8,16,512]{3,2,1,0:T(8,128)(2,1)}, bf16[16,8,16,512]{3,2,1,0:T(8,128)(2,1)S(1)}, u32[]{:S(2)}) copy-start(bf16[16,8,16,512]{3,2,1,0:T(8,128)(2,1)S(1)} %get-tuple-element.30.refs_3_.refs_2_) | copy-start | bytes 6291460
  13.4 4.0 %collective-permute-start.1 = (bf16[9,128,128]{2,1,0:T(8,128)(2,1)S(1)}, bf16[9,128,128]{2,1,0:T(8,128)(2,1)S(1)}, u32[]{:S(2)}, u32[]{:S(2)}) collective-permute-start(bf16[9,128,128]{2,1,0:T(8,128)(2,1)S(1)} %get-tuple-element.26.own_a), channel_id=1, source_target_pairs={{0,4},{4,0},{8,12},{12,8},{16,20},{20,16},{24,28},{28,24},{1,5},{5... | collective-permute-start | bytes 884744 | tf_op jit(solution)/shard_map/ppermute | solution.py:378
  13.9 16.5 %collective-permute-start = (bf16[9,128,128]{2,1,0:T(8,128)(2,1)S(1)}, bf16[9,128,128]{2,1,0:T(8,128)(2,1)S(1)}, u32[]{:S(2)}, u32[]{:S(2)}) collective-permute-start(bf16[9,128,128]{2,1,0:T(8,128)(2,1)S(1)} %get-tuple-element.21.own_b), channel_id=1, source_target_pairs={{0,28},{4,8},{8,4},{12,16},{16,12},{20,24},{24,20},{28,0},{1,29},{... | collective-permute-start | bytes 884744 | tf_op jit(solution)/shard_map/ppermute | solution.py:378
  17.5 19.2 %slice-start = ((s8[6291456]{0:T(1024)(128)(4,1)}), s8[2097152]{0:T(1024)(128)(4,1)S(1)}, s32[]{:S(2)}) async-start(s8[6291456]{0:T(1024)(128)(4,1)} %bitcast.11), calls=%async_computation | async-start | bytes 4194304
  18.9 2.2 %copy-start.5 = (bf16[16,9,128,128]{3,2,1,0:T(8,128)(2,1)}, bf16[16,9,128,128]{3,2,1,0:T(8,128)(2,1)S(1)}, u32[]{:S(2)}) copy-start(bf16[16,9,128,128]{3,2,1,0:T(8,128)(2,1)S(1)} %get-tuple-element.25.tiles_ref) | copy-start | bytes 14155780
  21.2 1.0 %copy-start.7 = (bf16[32,128,128]{2,1,0:T(8,128)(2,1)}, bf16[32,128,128]{2,1,0:T(8,128)(2,1)S(1)}, u32[]{:S(2)}) copy-start(bf16[32,128,128]{2,1,0:T(8,128)(2,1)S(1)} %get-tuple-element.27.wide_in) | copy-start | bytes 3145732
  22.1 1.2 %collective-permute-start.2 = (bf16[128,128]{1,0:T(8,128)(2,1)S(1)}, bf16[128,128]{1,0:T(8,128)(2,1)S(1)}, u32[]{:S(2)}, u32[]{:S(2)}) collective-permute-start(bf16[128,128]{1,0:T(8,128)(2,1)S(1)} %get-tuple-element.28), channel_id=1, source_target_pairs={{0,4},{4,0},{8,12},{12,8},{16,20},{20,16},{24,28},{28,24},{1,5},{5... | collective-permute-start | bytes 98312 | tf_op jit(solution)/shard_map/ppermute | solution.py:378
  23.3 0.6 %copy-start.9 = (bf16[128,128]{1,0:T(8,128)(2,1)}, bf16[128,128]{1,0:T(8,128)(2,1)S(1)}, u32[]{:S(2)}) copy-start(bf16[128,128]{1,0:T(8,128)(2,1)S(1)} %collective-permute-done.2.refs_1_) | copy-start | bytes 98308
  24.0 2.8 %copy-start.1 = (bf16[16,384,512]{2,1,0:T(8,128)(2,1)S(1)}, bf16[16,384,512]{2,1,0:T(8,128)(2,1)}, u32[]{:S(2)}) copy-start(bf16[16,384,512]{2,1,0:T(8,128)(2,1)} %copy-done) | copy-start | bytes 18874372
  26.8 1.6 %copy-start.3 = (bf16[16,8,16,512]{3,2,1,0:T(8,128)(2,1)S(1)}, bf16[16,8,16,512]{3,2,1,0:T(8,128)(2,1)}, u32[]{:S(2)}) copy-start(bf16[16,8,16,512]{3,2,1,0:T(8,128)(2,1)} %copy-done.2) | copy-start | bytes 6291460
  28.3 0.8 %copy-start.10 = (bf16[128,128]{1,0:T(8,128)(2,1)S(1)}, bf16[128,128]{1,0:T(8,128)(2,1)}, u32[]{:S(2)}) copy-start(bf16[128,128]{1,0:T(8,128)(2,1)} %copy-done.9) | copy-start | bytes 98308
  29.1 2.3 %copy-start.6 = (bf16[16,9,128,128]{3,2,1,0:T(8,128)(2,1)S(1)}, bf16[16,9,128,128]{3,2,1,0:T(8,128)(2,1)}, u32[]{:S(2)}) copy-start(bf16[16,9,128,128]{3,2,1,0:T(8,128)(2,1)} %copy-done.5) | copy-start | bytes 14155780
  29.1 7.6 %slice-start.1 = ((s8[6291456]{0:T(1024)(128)(4,1)}), s8[4194304]{0:T(1024)(128)(4,1)S(1)}, s32[]{:S(2)}) async-start(s8[6291456]{0:T(1024)(128)(4,1)} %bitcast.11), calls=%async_computation.1 | async-start | bytes 8388608
  30.4 6.3 %copy-start.4 = (bf16[16,8,16,512]{3,2,1,0:T(8,128)(2,1)S(1)}, bf16[16,8,16,512]{3,2,1,0:T(8,128)(2,1)}, u32[]{:S(2)}) copy-start(bf16[16,8,16,512]{3,2,1,0:T(8,128)(2,1)} %copy-done.2) | copy-start | bytes 6291460
  31.4 2.0 %copy-start.8 = (bf16[32,128,128]{2,1,0:T(8,128)(2,1)S(1)}, bf16[32,128,128]{2,1,0:T(8,128)(2,1)}, u32[]{:S(2)}) copy-start(bf16[32,128,128]{2,1,0:T(8,128)(2,1)} %copy-done.7) | copy-start | bytes 3145732
  35.4 4.3 %collective-permute-start.3 = (bf16[128,128]{1,0:T(8,128)(2,1)S(1)}, bf16[128,128]{1,0:T(8,128)(2,1)S(1)}, u32[]{:S(2)}, u32[]{:S(2)}) collective-permute-start(bf16[128,128]{1,0:T(8,128)(2,1)S(1)} %get-tuple-element.33), channel_id=1, source_target_pairs={{0,28},{4,8},{8,4},{12,16},{16,12},{20,24},{24,20},{28,0},{1,29},{... | collective-permute-start | bytes 98312 | tf_op jit(solution)/shard_map/ppermute | solution.py:378
  40.5 6.8 %collective-permute-start.4 = (bf16[16,2048]{1,0:T(8,128)(2,1)S(1)}, bf16[16,2048]{1,0:T(8,128)(2,1)S(1)}, u32[]{:S(2)}, u32[]{:S(2)}) collective-permute-start(bf16[16,2048]{1,0:T(8,128)(2,1)S(1)} %get-tuple-element.37), channel_id=1, source_target_pairs={{0,1},{1,2},{2,3},{3,0},{4,5},{5,6},{6,7},{7,4},{8,9},{9,10},{10,1... | collective-permute-start | bytes 196616 | tf_op jit(solution)/shard_map/ppermute | solution.py:414
  42.1 7.2 %collective-permute-start.5 = (bf16[16,2048]{1,0:T(8,128)(2,1)S(1)}, bf16[16,2048]{1,0:T(8,128)(2,1)S(1)}, u32[]{:S(2)}, u32[]{:S(2)}) collective-permute-start(bf16[16,2048]{1,0:T(8,128)(2,1)S(1)} %get-tuple-element.39), channel_id=1, source_target_pairs={{0,2},{1,3},{2,0},{3,1},{4,6},{5,7},{6,4},{7,5},{8,10},{9,11},{10,... | collective-permute-start | bytes 196616 | tf_op jit(solution)/shard_map/ppermute | solution.py:414
  44.7 4.7 %collective-permute-start.6 = (bf16[16,2048]{1,0:T(8,128)(2,1)S(1)}, bf16[16,2048]{1,0:T(8,128)(2,1)S(1)}, u32[]{:S(2)}, u32[]{:S(2)}) collective-permute-start(bf16[16,2048]{1,0:T(8,128)(2,1)S(1)} %get-tuple-element.38), channel_id=1, source_target_pairs={{0,3},{1,0},{2,1},{3,2},{4,7},{5,4},{6,5},{7,6},{8,11},{9,8},{10,9... | collective-permute-start | bytes 196616 | tf_op jit(solution)/shard_map/ppermute | solution.py:414

commit v3 on v2

--- a/solution.py
+++ b/solution.py
@@ -27,7 +27,7 @@
     return pltpu.with_memory_space_constraint(x, pltpu.HBM)
 
 
-def call(kernel, in_specs, out_specs, out_shape, scratch, flops, aliases=None):
+def call(kernel, in_specs, out_specs, out_shape, scratch, aliases=None):
     return pl.pallas_call(
         kernel,
         in_specs=in_specs,
@@ -36,7 +36,7 @@
         scratch_shapes=scratch,
         input_output_aliases=aliases or {},
         compiler_params=pltpu.CompilerParams(vmem_limit_bytes=16 * 1024 * 1024),
-        cost_estimate=pl.CostEstimate(flops=flops, bytes_accessed=0, transcendentals=0),
+        cost_estimate=pl.CostEstimate(flops=0, bytes_accessed=0, transcendentals=0),
     )
 
 
@@ -193,7 +193,6 @@
             pltpu.SemaphoreType.DMA((steps,)),
             pltpu.SemaphoreType.DMA((3,)),
         ],
-        2 * rows * steps * WIN * CHUNK,
         aliases,
     )(info, in_hbm(anomalies), in_hbm(increment), in_hbm(index), in_hbm(weight), *extra)
 
@@ -272,7 +271,7 @@
 
 
 def conv_early_call(info, neighbours, own_a, own_b, got_a, tiles):
-    blocks, count = tiles.shape[:2]
+    blocks, _ = tiles.shape[:2]
     half, rows, _ = own_a.shape
     early = blocks - half
     return call(
@@ -285,13 +284,11 @@
             jax.ShapeDtypeStruct((rows, BLOCK), BF16),
         ],
         [],
-        2 * rows * early * count * BLOCK * BLOCK,
     )(info, neighbours, own_a, own_b, got_a, tiles)
 
 
 def conv_late_call(info, neighbours, got_b, tiles, wide, smooth):
-    _, count = tiles.shape[:2]
-    half, rows, _ = got_b.shape
+    _, rows, _ = got_b.shape
     return call(
         functools.partial(conv_late_kernel, 3),
         [IN_SMEM, IN_SMEM] + [IN_VMEM] * 4,
@@ -302,7 +299,6 @@
             jax.ShapeDtypeStruct((rows, BLOCK), BF16),
         ],
         [],
-        2 * rows * half * count * BLOCK * BLOCK,
         {4: 0, 5: 1},
     )(info, neighbours, got_b, tiles, wide, smooth)
 
@@ -316,6 +312,7 @@
         info_ref, got_ref, table_ref, anom_ref, _, _, smooth_ref, out_ref = refs
     flip = info_ref[0] == 1
     blocks = table_ref.shape[0]
+    shares = out_ref.shape[0]
     if part == 0:
         smooth_ref[jnp.where(flip, 0, blocks + 1)] = got_ref[...]
         start = jnp.where(flip, 0, blocks - steps)
@@ -334,13 +331,15 @@
         anom = anom_ref[c].astype(F32)
         value = jnp.sum(anom * returned.reshape(anom.shape), axis=0)
         lane = pl.multiple_of(lax.rem(c, per) * CHUNK, CHUNK)
-        out_ref[lax.div(c, per), :, pl.ds(lane, CHUNK)] = value.astype(BF16)
+        place = lax.div(c, per) - info_ref[2]
+        place = jnp.where(place < 0, place + shares, place)
+        out_ref[place, :, pl.ds(lane, CHUNK)] = value.astype(BF16)
 
     groups(steps, unroll, body)
 
 
 def back_call(part, steps, unroll, shares, info, got, table, anom, smooth, out=None):
-    chunks, members, fields, _ = anom.shape
+    chunks, _, fields, _ = anom.shape
     per = chunks // shares
     operands = [info] + ([] if part == 1 else [got]) + [table, anom, smooth]
     in_specs = [IN_SMEM] + [IN_VMEM] * (len(operands) - 1)
@@ -363,7 +362,6 @@
         [IN_VMEM] * len(out_shape),
         out_shape,
         [],
-        2 * members * fields * steps * WIN * CHUNK,
         aliases,
     )(*operands)
 
@@ -386,11 +384,11 @@
     mem = lax.axis_index("mem")
     shares = lax.axis_size("mem")
     assert count % 2 == 0
-    flip = space % 2
+    flip = space & 1
     inner, outer = swaps(count)
     head = chunks // 2 + 1
     present = jnp.where(flip == 1, space < count - 1, space > 0)
-    info = jnp.stack([flip, present.astype(jnp.int32)]).astype(jnp.int32)
+    info = jnp.stack([flip, present.astype(jnp.int32), mem]).astype(jnp.int32)
     columns_in = (anomalies, increment, interp_index, interp_weight)
     table, anom, own_b, carry = spread_call(head, 0, 3, info, *columns_in)
     got_b = swap(own_b, outer)
@@ -406,13 +404,10 @@
     (out,) = back_call(1, head, 3, shares, info, None, table, anom, smooth, out)
     _, pieces = back_call(2, 1, 1, shares, info, halo_b, table, anom, smooth, out)
 
-    def piece_of(share):
-        return lax.dynamic_index_in_dim(pieces, share, 0, False)
-
-    total = piece_of(mem).astype(F32)
+    total = pieces[0].astype(F32)
     for shift in range(1, shares):
         got = lax.ppermute(
-            piece_of((mem + shift) % shares),
+            pieces[shift],
             "mem",
             [(i, (i + shift) % shares) for i in range(shares)],
         )

time: 50.4 us -> 37.5 us (0.74)
  local copies, waits for them, and re-layouts: 16.1 us -> 0.02 us
  waiting for transfers between devices: 5.85 us -> 7.86 us
  starting transfers between devices: 10.9 us -> 12.2 us
    unnamed x28 -> x2, local copies, waits for them, and re-layouts: 16 us -> 0.01 us
    ppermute x4, waiting for transfers between devices: 2.54 us -> 4.67 us  [swap(): return lax.ppermute(value, 'space', pairs)]
    ppermute x4, starting transfers between devices: 5.33 us -> 6.14 us  [swap(): return lax.ppermute(value, 'space', pairs)]
  transfers between devices with their start and end apart: 7 -> 7, of which waited for: 5 -> 6; matrix products, arithmetic and copies ran while one was open for 0% -> 0% of each run, Pallas kernels for 9% -> 12%
where the time goes in v3:
time: 37.5 us; the launch traced here: 37.3 us
  Pallas kernels  16.4 us (44%)
  starting transfers between devices  12.2 us (33%)
  waiting for transfers between devices  7.86 us (21%)
  other arithmetic  0.77 us (2%)
    pallas_call x2, Pallas kernels, spread_call(): call(functools.partial(spread_kernel, steps, done, unroll, chunks), in_sp...  9.27 us
    ppermute x4, starting transfers between devices, swap(): return lax.ppermute(value, 'space', pairs)  6.14 us
    ppermute x3, starting transfers between devices, shards(): lax.ppermute(pieces[shift], 'mem', [(i, (i + shift) % shares) for i in ra...  6.05 us
    ppermute x4, waiting for transfers between devices, swap(): return lax.ppermute(value, 'space', pairs)  4.67 us
    pallas_call x3, Pallas kernels, back_call(): call(functools.partial(back_kernel, part, steps, unroll, per), in_specs,...  3.76 us
    ppermute x3, waiting for transfers between devices, shards(): lax.ppermute(pieces[shift], 'mem', [(i, (i + shift) % shares) for i in ra...  3.19 us
    pallas_call x1, Pallas kernels, conv_late_call(): call(functools.partial(conv_late_kernel, 3), [IN_SMEM, IN_SMEM] + [IN_VME...  1.95 us
    pallas_call x1, Pallas kernels, conv_early_call(): call(functools.partial(conv_early_kernel, early), [IN_SMEM, IN_SMEM] + [I...  1.45 us
  transfers between devices with their start and end apart: 7, of which 6 were waited for; matrix products, arithmetic and copies ran while one was open for 0% of the time, Pallas kernels for 12%

profile of v3, /device:TPU:0, one launch (start us, length us, event | category | flops | bytes accessed | tf_op | source)
XLA Modules:
  0.0 37.3 jit_solution(15888880219637811122)
XLA Ops:
  0.0 0.1 pad_add_fusion.refs_0_.info_ref
  0.1 4.6 %shard_map.64 = (bf16[16,384,512]{2,1,0:T(8,128)(2,1)S(1)}, bf16[16,8,16,512]{3,2,1,0:T(8,128)(2,1)S(1)}, bf16[9,128,128]{2,1,0:T(8,128)(2,1)S(1)}, f32[2,128,128]{2,1,0:T(8,128)S(1)}) custom-call(s32[3]{0:T(128)S(1)} %pad_add_fusion.refs_0_.info_ref, bf16[8,16,8192]{2,1,0:T(8,128)(2,1)} %refs_1_.3, f32[16,8192]{1,0:T(8,128)} %refs_2_.3, s32[3,8192]{1,0:T(4,128)} %refs_3_.3, ...), custom_call_target="tpu_custom_call" | custom-call | tf_op jit(solution)/shard_map/pallas_call | solution.py:182
  4.7 0.0 copy-start
  4.7 4.7 %shard_map.65 = (bf16[16,384,512]{2,1,0:T(8,128)(2,1)S(1)}, bf16[16,8,16,512]{3,2,1,0:T(8,128)(2,1)S(1)}, bf16[9,128,128]{2,1,0:T(8,128)(2,1)S(1)}, bf16[16,9,128,128]{3,2,1,0:T(8,128)(2,1)S(1)}) custom-call(s32[3]{0:T(128)S(1)} %pad_add_fusion.refs_0_.info_ref, bf16[8,16,8192]{2,1,0:T(8,128)(2,1)} %refs_1_.3, ...), custom_call_target="tpu_custom_call", output_to_operand_aliasing={{0}: (7, {}), {1}: (8, {})} | custom-call | tf_op jit(solution)/shard_map/pallas_call | solution.py:182
  9.4 0.6 %collective-permute-start.1 = (bf16[9,128,128]{2,1,0:T(8,128)(2,1)S(1)}, bf16[9,128,128]{2,1,0:T(8,128)(2,1)S(1)}, u32[]{:S(2)}, u32[]{:S(2)}) collective-permute-start(bf16[9,128,128]{2,1,0:T(8,128)(2,1)S(1)} %get-tuple-element.26.own_a), channel_id=1, source_target_pairs={{0,4},{4,0},{8,12},{12,8},{16,20},{20,16},{24,28},{28,24},{1,5},{5... | collective-permute-start | bytes 884744 | tf_op jit(solution)/shard_map/ppermute | solution.py:376
  9.9 3.5 %collective-permute-start = (bf16[9,128,128]{2,1,0:T(8,128)(2,1)S(1)}, bf16[9,128,128]{2,1,0:T(8,128)(2,1)S(1)}, u32[]{:S(2)}, u32[]{:S(2)}) collective-permute-start(bf16[9,128,128]{2,1,0:T(8,128)(2,1)S(1)} %get-tuple-element.21.own_b), channel_id=1, source_target_pairs={{0,28},{4,8},{8,4},{12,16},{16,12},{20,24},{24,20},{28,0},{1,29},{... | collective-permute-start | bytes 884744 | tf_op jit(solution)/shard_map/ppermute | solution.py:376
  13.5 0.0 collective-permute-done.1.got_a
  13.5 0.0 copy-done
  13.5 1.5 %shard_map.66 = (bf16[32,128,128]{2,1,0:T(8,128)(2,1)S(1)}, bf16[18,128,128]{2,1,0:T(8,128)(2,1)S(1)}, bf16[128,128]{1,0:T(8,128)(2,1)S(1)}) custom-call(s32[3]{0:T(128)S(1)} %pad_add_fusion.refs_0_.info_ref, s32[9,16]{1,0:T(8,128)S(1)} %copy-done, bf16[9,128,128]{2,1,0:T(8,128)(2,1)S(1)} %get-tuple-element.26.own_a, ...), custom_call_target="tpu_custom_call" | custom-call | tf_op jit(solution)/shard_map/pallas_call | solution.py:277
  14.9 0.1 collective-permute-start.2
  15.0 1.2 %collective-permute-done.2.refs_1_ = bf16[128,128]{1,0:T(8,128)(2,1)S(1)} collective-permute-done((bf16[128,128]{1,0:T(8,128)(2,1)S(1)}, bf16[128,128]{1,0:T(8,128)(2,1)S(1)}, u32[]{:S(2)}, u32[]{:S(2)}) %collective-permute-start.2) | collective-permute-done | bytes 32800 | tf_op jit(solution)/shard_map/ppermute | solution.py:376
  16.2 1.3 %shard_map.67 = (bf16[18,128,128]{2,1,0:T(8,128)(2,1)S(1)}, bf16[4,16,2048]{2,1,0:T(8,128)(2,1)S(1)}) custom-call(s32[3]{0:T(128)S(1)} %pad_add_fusion.refs_0_.info_ref, bf16[128,128]{1,0:T(8,128)(2,1)S(1)} %collective-permute-done.2.refs_1_, bf16[16,384,512]{2,1,0:T(8,128)(2,1)S(1)} %get-tuple-element.29.refs_2_.refs_1_, ...), custom_call_target="tpu_custom_call", output_to_operand_aliasing={{0}: (4, {})} | custom-call | tf_op jit(solution)/shard_map/pallas_call | solution.py:359
  17.5 2.7 %collective-permute-done.got_b = bf16[9,128,128]{2,1,0:T(8,128)(2,1)S(1)} collective-permute-done((bf16[9,128,128]{2,1,0:T(8,128)(2,1)S(1)}, bf16[9,128,128]{2,1,0:T(8,128)(2,1)S(1)}, u32[]{:S(2)}, u32[]{:S(2)}) %collective-permute-start) | collective-permute-done | bytes 294944 | tf_op jit(solution)/shard_map/ppermute | solution.py:376
  20.2 1.9 %shard_map.68 = (bf16[32,128,128]{2,1,0:T(8,128)(2,1)S(1)}, bf16[18,128,128]{2,1,0:T(8,128)(2,1)S(1)}, bf16[128,128]{1,0:T(8,128)(2,1)S(1)}) custom-call(s32[3]{0:T(128)S(1)} %pad_add_fusion.refs_0_.info_ref, s32[9,16]{1,0:T(8,128)S(1)} %copy-done, ...), custom_call_target="tpu_custom_call", output_to_operand_aliasing={{0}: (4, {}), {1}: (5, {})} | custom-call | tf_op jit(solution)/shard_map/pallas_call | solution.py:292
  22.2 2.0 %collective-permute-start.3 = (bf16[128,128]{1,0:T(8,128)(2,1)S(1)}, bf16[128,128]{1,0:T(8,128)(2,1)S(1)}, u32[]{:S(2)}, u32[]{:S(2)}) collective-permute-start(bf16[128,128]{1,0:T(8,128)(2,1)S(1)} %get-tuple-element.33), channel_id=1, source_target_pairs={{0,28},{4,8},{8,4},{12,16},{16,12},{20,24},{24,20},{28,0},{1,29},{... | collective-permute-start | bytes 98312 | tf_op jit(solution)/shard_map/ppermute | solution.py:376
  24.1 1.7 %shard_map.69.refs_5_ = bf16[4,16,2048]{2,1,0:T(8,128)(2,1)S(1)} custom-call(s32[3]{0:T(128)S(1)} %pad_add_fusion.refs_0_.info_ref, bf16[16,384,512]{2,1,0:T(8,128)(2,1)S(1)} %get-tuple-element.29.refs_2_.refs_1_, bf16[16,8,16,512]{3,2,1,0:T(8,128)(2,1)S(1)} %get-tuple-element.30.refs_3_.refs_2_, ...), custom_call_target="tpu_custom_call", output_to_operand_aliasing={{}: (4, {})} | custom-call | tf_op jit(solution)/shard_map/pallas_call | solution.py:359
  25.8 0.8 %collective-permute-done.3.refs_1_ = bf16[128,128]{1,0:T(8,128)(2,1)S(1)} collective-permute-done((bf16[128,128]{1,0:T(8,128)(2,1)S(1)}, bf16[128,128]{1,0:T(8,128)(2,1)S(1)}, u32[]{:S(2)}, u32[]{:S(2)}) %collective-permute-start.3) | collective-permute-done | bytes 32800 | tf_op jit(solution)/shard_map/ppermute | solution.py:376
  26.6 0.8 %shard_map.70 = (bf16[18,128,128]{2,1,0:T(8,128)(2,1)S(1)}, bf16[4,16,2048]{2,1,0:T(8,128)(2,1)S(1)}) custom-call(s32[3]{0:T(128)S(1)} %pad_add_fusion.refs_0_.info_ref, bf16[128,128]{1,0:T(8,128)(2,1)S(1)} %collective-permute-done.3.refs_1_, ...), custom_call_target="tpu_custom_call", output_to_operand_aliasing={{0}: (4, {}), {1}: (5, {})} | custom-call | tf_op jit(solution)/shard_map/pallas_call | solution.py:359
  27.4 2.1 %collective-permute-start.4 = (bf16[16,2048]{1,0:T(8,128)(2,1)S(1)}, bf16[16,2048]{1,0:T(8,128)(2,1)S(1)}, u32[]{:S(2)}, u32[]{:S(2)}) collective-permute-start(bf16[16,2048]{1,0:T(8,128)(2,1)S(1)} %get-tuple-element.37), channel_id=1, source_target_pairs={{0,1},{1,2},{2,3},{3,0},{4,5},{5,6},{6,7},{7,4},{8,9},{9,10},{10,1... | collective-permute-start | bytes 196616 | tf_op jit(solution)/shard_map/ppermute | solution.py:409
  29.5 2.6 %collective-permute-start.5 = (bf16[16,2048]{1,0:T(8,128)(2,1)S(1)}, bf16[16,2048]{1,0:T(8,128)(2,1)S(1)}, u32[]{:S(2)}, u32[]{:S(2)}) collective-permute-start(bf16[16,2048]{1,0:T(8,128)(2,1)S(1)} %get-tuple-element.39), channel_id=1, source_target_pairs={{0,2},{1,3},{2,0},{3,1},{4,6},{5,7},{6,4},{7,5},{8,10},{9,11},{10,... | collective-permute-start | bytes 196616 | tf_op jit(solution)/shard_map/ppermute | solution.py:409
  32.1 1.3 %collective-permute-start.6 = (bf16[16,2048]{1,0:T(8,128)(2,1)S(1)}, bf16[16,2048]{1,0:T(8,128)(2,1)S(1)}, u32[]{:S(2)}, u32[]{:S(2)}) collective-permute-start(bf16[16,2048]{1,0:T(8,128)(2,1)S(1)} %get-tuple-element.38), channel_id=1, source_target_pairs={{0,3},{1,0},{2,1},{3,2},{4,7},{5,4},{6,5},{7,6},{8,11},{9,8},{10,9... | collective-permute-start | bytes 196616 | tf_op jit(solution)/shard_map/ppermute | solution.py:409
  33.5 1.0 %collective-permute-done.4 = bf16[16,2048]{1,0:T(8,128)(2,1)S(1)} collective-permute-done((bf16[16,2048]{1,0:T(8,128)(2,1)S(1)}, bf16[16,2048]{1,0:T(8,128)(2,1)S(1)}, u32[]{:S(2)}, u32[]{:S(2)}) %collective-permute-start.4) | collective-permute-done | bytes 65568 | tf_op jit(solution)/shard_map/ppermute | solution.py:409
  34.5 1.8 %collective-permute-done.5 = bf16[16,2048]{1,0:T(8,128)(2,1)S(1)} collective-permute-done((bf16[16,2048]{1,0:T(8,128)(2,1)S(1)}, bf16[16,2048]{1,0:T(8,128)(2,1)S(1)}, u32[]{:S(2)}, u32[]{:S(2)}) %collective-permute-start.5) | collective-permute-done | bytes 65568 | tf_op jit(solution)/shard_map/ppermute | solution.py:409
  36.3 0.3 collective-permute-done.6
  36.6 0.7 %fusion.2 = f32[16,2048]{1,0:T(8,128)} fusion(bf16[16,2048]{1,0:T(8,128)(2,1)S(1)} %collective-permute-done.6, bf16[16,2048]{1,0:T(8,128)(2,1)S(1)} %collective-permute-done.5, bf16[16,2048]{1,0:T(8,128)(2,1)S(1)} %collective-permute-done.4, bf16[4,16,2048]{2,1,0:T(8,128)(2,1)S(1)} %get-tuple-element.36), kind=kLoop, calls=%fused_computation.3 | loop fusion | flops 262144 | bytes 393216 | tf_op jit(solution)/shard_map/div | solution.py:415
  (1 shorter events, 0.0 us)
Async XLA Ops:
  4.7 8.8 %copy-start = (s32[9,16]{1,0:T(8,128)S(1)}, s32[9,16]{1,0:T(8,128)}, u32[]{:S(2)}) copy-start(s32[9,16]{1,0:T(8,128)} %nbr_ref.3) | copy-start | bytes 1732
  9.4 4.1 %collective-permute-start.1 = (bf16[9,128,128]{2,1,0:T(8,128)(2,1)S(1)}, bf16[9,128,128]{2,1,0:T(8,128)(2,1)S(1)}, u32[]{:S(2)}, u32[]{:S(2)}) collective-permute-start(bf16[9,128,128]{2,1,0:T(8,128)(2,1)S(1)} %get-tuple-element.26.own_a), channel_id=1, source_target_pairs={{0,4},{4,0},{8,12},{12,8},{16,20},{20,16},{24,28},{28,24},{1,5},{5... | collective-permute-start | bytes 884744 | tf_op jit(solution)/shard_map/ppermute | solution.py:376
  9.9 10.3 %collective-permute-start = (bf16[9,128,128]{2,1,0:T(8,128)(2,1)S(1)}, bf16[9,128,128]{2,1,0:T(8,128)(2,1)S(1)}, u32[]{:S(2)}, u32[]{:S(2)}) collective-permute-start(bf16[9,128,128]{2,1,0:T(8,128)(2,1)S(1)} %get-tuple-element.21.own_b), channel_id=1, source_target_pairs={{0,28},{4,8},{8,4},{12,16},{16,12},{20,24},{24,20},{28,0},{1,29},{... | collective-permute-start | bytes 884744 | tf_op jit(solution)/shard_map/ppermute | solution.py:376
  14.9 1.3 %collective-permute-start.2 = (bf16[128,128]{1,0:T(8,128)(2,1)S(1)}, bf16[128,128]{1,0:T(8,128)(2,1)S(1)}, u32[]{:S(2)}, u32[]{:S(2)}) collective-permute-start(bf16[128,128]{1,0:T(8,128)(2,1)S(1)} %get-tuple-element.28), channel_id=1, source_target_pairs={{0,4},{4,0},{8,12},{12,8},{16,20},{20,16},{24,28},{28,24},{1,5},{5... | collective-permute-start | bytes 98312 | tf_op jit(solution)/shard_map/ppermute | solution.py:376
  22.2 4.4 %collective-permute-start.3 = (bf16[128,128]{1,0:T(8,128)(2,1)S(1)}, bf16[128,128]{1,0:T(8,128)(2,1)S(1)}, u32[]{:S(2)}, u32[]{:S(2)}) collective-permute-start(bf16[128,128]{1,0:T(8,128)(2,1)S(1)} %get-tuple-element.33), channel_id=1, source_target_pairs={{0,28},{4,8},{8,4},{12,16},{16,12},{20,24},{24,20},{28,0},{1,29},{... | collective-permute-start | bytes 98312 | tf_op jit(solution)/shard_map/ppermute | solution.py:376
  27.4 7.1 %collective-permute-start.4 = (bf16[16,2048]{1,0:T(8,128)(2,1)S(1)}, bf16[16,2048]{1,0:T(8,128)(2,1)S(1)}, u32[]{:S(2)}, u32[]{:S(2)}) collective-permute-start(bf16[16,2048]{1,0:T(8,128)(2,1)S(1)} %get-tuple-element.37), channel_id=1, source_target_pairs={{0,1},{1,2},{2,3},{3,0},{4,5},{5,6},{6,7},{7,4},{8,9},{9,10},{10,1... | collective-permute-start | bytes 196616 | tf_op jit(solution)/shard_map/ppermute | solution.py:409
  29.5 6.8 %collective-permute-start.5 = (bf16[16,2048]{1,0:T(8,128)(2,1)S(1)}, bf16[16,2048]{1,0:T(8,128)(2,1)S(1)}, u32[]{:S(2)}, u32[]{:S(2)}) collective-permute-start(bf16[16,2048]{1,0:T(8,128)(2,1)S(1)} %get-tuple-element.39), channel_id=1, source_target_pairs={{0,2},{1,3},{2,0},{3,1},{4,6},{5,7},{6,4},{7,5},{8,10},{9,11},{10,... | collective-permute-start | bytes 196616 | tf_op jit(solution)/shard_map/ppermute | solution.py:409
  32.1 4.5 %collective-permute-start.6 = (bf16[16,2048]{1,0:T(8,128)(2,1)S(1)}, bf16[16,2048]{1,0:T(8,128)(2,1)S(1)}, u32[]{:S(2)}, u32[]{:S(2)}) collective-permute-start(bf16[16,2048]{1,0:T(8,128)(2,1)S(1)} %get-tuple-element.38), channel_id=1, source_target_pairs={{0,3},{1,0},{2,1},{3,2},{4,7},{5,4},{6,5},{7,6},{8,11},{9,8},{10,9... | collective-permute-start | bytes 196616 | tf_op jit(solution)/shard_map/ppermute | solution.py:409

commit v4 on v3

v4 whole, which is shorter than its diff:
```python
import functools

import jax
import jax.numpy as jnp
from jax import lax
from jax.experimental import pallas as pl
from jax.experimental.pallas import tpu as pltpu
from jax.sharding import PartitionSpec as P


BLOCK = 128
HI = 128
RATIO = 4
CHUNK = RATIO * BLOCK
WIN = 3 * BLOCK
REACH = 2 * HI + 32
F32 = jnp.float32
BF16 = jnp.bfloat16
FIRST_UNROLL = 9
REST_UNROLL = 7
VMEM = pltpu.VMEM
ANY = pl.BlockSpec(memory_space=pl.ANY)
IN_VMEM = pl.BlockSpec(memory_space=pltpu.VMEM)
IN_SMEM = pl.BlockSpec(memory_space=pltpu.SMEM)


def is_present():
    space = lax.axis_index("space")
    last = lax.axis_size("space") - 1
    return jnp.where((space & 1) == 1, space < last, space > 0)


def in_hbm(x):
    return pltpu.with_memory_space_constraint(x, pltpu.HBM)


def call(kernel, in_specs, out_specs, out_shape, scratch, aliases=None):
    return pl.pallas_call(
        kernel,
        in_specs=in_specs,
        out_specs=out_specs,
        out_shape=out_shape,
        scratch_shapes=scratch,
        input_output_aliases=aliases or {},
        compiler_params=pltpu.CompilerParams(vmem_limit_bytes=16 * 1024 * 1024),
        cost_estimate=pl.CostEstimate(flops=0, bytes_accessed=0, transcendentals=0),
    )


def groups(steps, unroll, body):
    unroll = unroll if steps % unroll == 0 else 1

    def group(g, carry):
        for j in range(unroll):
            body(g * unroll + j)
        return carry

    lax.fori_loop(0, steps // unroll, group, 0)


def build_table(local, weight):
    i0, i1, i2 = local[0:1], local[1:2], local[2:3]
    w0, w1, w2 = weight[0:1], weight[1:2], weight[2:3]
    zero = jnp.zeros_like(w0)
    w0 = w0 + jnp.where(i1 == i0, w1, zero) + jnp.where(i2 == i0, w2, zero)
    w1 = w1 + jnp.where(i2 == i1, w2, zero)
    rows = REACH // 16
    iota = lax.broadcasted_iota(jnp.int32, (rows, 16, BLOCK), 0) * 16 + lax.broadcasted_iota(
        jnp.int32, (rows, 16, BLOCK), 1
    )
    iota = iota.astype(jnp.int16)
    parts = []
    for s in range(CHUNK // BLOCK):
        cols = slice(s * BLOCK, (s + 1) * BLOCK)
        base = s * BLOCK // RATIO

        def wide(x, kind):
            return jnp.broadcast_to(x[:, cols], (16, BLOCK)).astype(kind)[None]

        table = jnp.zeros((1, 16, BLOCK), BF16)
        for index, value in ((i2, w2), (i1, w1), (i0, w0)):
            table = jnp.where(wide(index - base, jnp.int16) == iota, wide(value, BF16), table)
        pieces = [table.reshape(REACH, BLOCK)]
        if base:
            pieces.insert(0, jnp.zeros((base, BLOCK), BF16))
        if base + REACH < WIN:
            pieces.append(jnp.zeros((WIN - base - REACH, BLOCK), BF16))
        parts.append(jnp.concatenate(pieces, axis=0))
    return jnp.concatenate(parts, axis=1)


def is_flipped():
    return (lax.axis_index("space") & 1) == 1


def spread_kernel(steps, done, unroll, chunks, *refs):
    first = done == 0
    if first:
        anom_hbm, incr_hbm, index_hbm, weight_hbm, nbr_hbm = refs[:5]
        table_ref, out_ref, carry_ref = refs[5:8]
        anom_ref, incr_ref, index_ref, weight_ref, nbr_ref = refs[8:13]
        acc_ref, anom_sem, incr_sem, some_sem = refs[13:]
    else:
        anom_ref, incr_ref, index_ref, weight_ref, tiles_hbm, carry_ref = refs[:6]
        table_ref, out_ref, tiles_ref, acc_ref, tiles_sem = refs[7:]
        tiles_copy = pltpu.make_async_copy(tiles_hbm, tiles_ref, tiles_sem)
        tiles_copy.start()
    flip = is_flipped()

    def chunk_of(step):
        return jnp.where(flip, chunks - 1 - step, step)

    def lanes(c):
        return pl.ds(pl.multiple_of(c * CHUNK, CHUNK), CHUNK)

    def chunk_copies(step):
        c = chunk_of(step)
        return (
            pltpu.make_async_copy(anom_hbm.at[:, :, lanes(c)], anom_ref.at[c], anom_sem.at[step]),
            pltpu.make_async_copy(incr_hbm.at[:, lanes(c)], incr_ref.at[c], incr_sem.at[step]),
        )

    if first:
        copies = [
            pltpu.make_async_copy(source, target, some_sem.at[k])
            for k, (source, target) in enumerate(
                (
                    (index_hbm, index_ref),
                    (weight_hbm, weight_ref),
                    (nbr_hbm, nbr_ref),
                )
            )
        ]
        for copy in copies[:2]:
            copy.start()
        for step in range(chunks):
            for copy in chunk_copies(step):
                copy.start()
        for copy in copies[2:]:
            copy.start()
        acc_ref[...] = jnp.zeros(acc_ref.shape, F32)
        for copy in copies[:2]:
            copy.wait()
    else:
        acc_ref[...] = carry_ref[...]
    rows = anom_ref.shape[1] * anom_ref.shape[2]
    total = steps if first else steps + 2

    def group(g, carry):
        acc0, acc1 = acc_ref[0], acc_ref[1]
        here = [g * unroll + j for j in range(unroll)]
        if first:
            for i in here:
                for copy in chunk_copies(i):
                    copy.wait()
        for i in here:
            c = chunk_of(done + i)
            table = build_table(index_ref[:, lanes(c)] - c * BLOCK, weight_ref[:, lanes(c)])
            table_ref[c] = table
            weighted = (anom_ref[c].astype(F32) * incr_ref[c][None]).astype(BF16)
            window = lax.dot_general(
                table,
                weighted.reshape(rows, CHUNK),
                (((1,), (1,)), ((), ())),
                preferred_element_type=F32,
            )
            near, mid, far = window[:BLOCK], window[BLOCK : 2 * BLOCK], window[2 * BLOCK :]
            ready = acc0 + jnp.where(flip, far, near)
            out_ref[jnp.where(flip, total - 1 - i, i)] = ready.T.astype(BF16)
            acc0 = acc1 + mid
            acc1 = jnp.where(flip, near, far)
        acc_ref[0] = acc0
        acc_ref[1] = acc1
        return carry

    lax.fori_loop(0, steps // unroll, group, 0)
    if first:
        carry_ref[...] = acc_ref[...]
        for step in range(steps, chunks):
            for copy in chunk_copies(step):
                copy.wait()
        for copy in copies[2:]:
            copy.wait()
    else:
        out_ref[jnp.where(flip, 1, steps)] = acc_ref[0].T.astype(BF16)
        out_ref[jnp.where(flip, 0, steps + 1)] = acc_ref[1].T.astype(BF16)
        tiles_copy.wait()


def spread_first_call(steps, unroll, increment, anomalies, index, weight, neighbours):
    members, fields, columns = anomalies.shape
    rows = members * fields
    chunks = columns // CHUNK
    return call(
        functools.partial(spread_kernel, steps, 0, unroll, chunks),
        [ANY] * 5,
        [IN_VMEM] * 7 + [IN_SMEM],
        [
            VMEM((chunks, WIN, CHUNK), BF16),
            jax.ShapeDtypeStruct((steps, rows, BLOCK), BF16),
            VMEM((2, BLOCK, rows), F32),
            VMEM((chunks, members, fields, CHUNK), BF16),
            VMEM((chunks, fields, CHUNK), F32),
            VMEM(index.shape, jnp.int32),
            VMEM(weight.shape, F32),
            pltpu.SMEM(neighbours.shape, jnp.int32),
        ],
        [
            VMEM((2, BLOCK, rows), F32),
            pltpu.SemaphoreType.DMA((chunks,)),
            pltpu.SemaphoreType.DMA((chunks,)),
            pltpu.SemaphoreType.DMA((3,)),
        ],
    )(*(in_hbm(x) for x in (anomalies, increment, index, weight, neighbours)))


def spread_rest_call(steps, unroll, table, carry, columns, tiles):
    chunks = table.shape[0]
    rows = carry.shape[2]
    return call(
        functools.partial(spread_kernel, steps, chunks - steps, unroll, chunks),
        [IN_VMEM] * 4 + [ANY] + [IN_VMEM] * 2,
        [IN_VMEM] * 3,
        [
            VMEM(table.shape, BF16),
            jax.ShapeDtypeStruct((steps + 2, rows, BLOCK), BF16),
            VMEM(tiles.shape, BF16),
        ],
        [VMEM((2, BLOCK, rows), F32), pltpu.SemaphoreType.DMA(())],
        {6: 0},
    )(*columns, in_hbm(tiles), carry, table)


def convolve(wide_ref, tiles_ref, nbr_ref, b):
    count = tiles_ref.shape[1]
    picked = jnp.concatenate([wide_ref[nbr_ref[n, b]] for n in range(count)], axis=1)
    weights = tiles_ref[b].reshape(count * BLOCK, BLOCK)
    return jnp.dot(picked, weights, preferred_element_type=F32).astype(BF16)


def edge_early_kernel(nbr_ref, own_a, own_b, got_a, tiles_ref, wide_ref, smooth_ref, edge_ref):
    half = own_a.shape[0]
    reach = half - 1
    blocks = tiles_ref.shape[0]
    top = blocks + reach
    flip = is_flipped()

    @pl.when(jnp.logical_not(flip))
    def _():
        wide_ref[reach - 1 : reach - 1 + half] = own_b[...]
        wide_ref[reach - 1 + half : top - 1] = own_a[0 : half - 2]
        wide_ref[top - 1 : top + 1] = (
            got_a[0:2].astype(F32) + own_a[half - 2 : half].astype(F32)
        ).astype(BF16)
        wide_ref[top + 1 : top + reach] = got_a[2:half]

    @pl.when(flip)
    def _():
        wide_ref[0 : reach - 1] = got_a[0 : reach - 1]
        wide_ref[reach - 1 : reach + 1] = (
            got_a[reach - 1 : reach + 1].astype(F32) + own_a[0:2].astype(F32)
        ).astype(BF16)
        wide_ref[reach + 1 : reach - 1 + half] = own_a[2:half]
        wide_ref[reach - 1 + half : top + 1] = own_b[...]

    b = jnp.where(flip, 0, blocks - 1)
    edge = convolve(wide_ref, tiles_ref, nbr_ref, b)
    smooth_ref[b + 1] = edge
    edge_ref[...] = edge


def edge_late_kernel(
    nbr_ref, got_b, tiles_ref, wide_in, smooth_in, wide_ref, smooth_ref, edge_ref
):
    half = got_b.shape[0]
    reach = half - 1
    blocks = tiles_ref.shape[0]
    top = blocks + reach
    flip = is_flipped()
    present = is_present()
    beyond = jnp.where(present, got_b[...], jnp.zeros(got_b.shape, BF16))

    @pl.when(jnp.logical_not(flip))
    def _():
        wide_ref[0 : reach - 1] = beyond[0 : reach - 1]
        both = wide_ref[reach - 1 : reach + 1].astype(F32) + beyond[reach - 1 :].astype(F32)
        wide_ref[reach - 1] = jnp.where(present, both[0], jnp.zeros_like(both[0])).astype(BF16)
        wide_ref[reach] = both[1].astype(BF16)

    @pl.when(flip)
    def _():
        wide_ref[top + 1 : top + reach] = beyond[2:half]
        both = wide_ref[top - 1 : top + 1].astype(F32) + beyond[0:2].astype(F32)
        wide_ref[top - 1] = both[0].astype(BF16)
        wide_ref[top] = jnp.where(present, both[1], jnp.zeros_like(both[1])).astype(BF16)

    b = jnp.where(flip, blocks - 1, 0)
    edge = convolve(wide_ref, tiles_ref, nbr_ref, b)
    smooth_ref[b + 1] = edge
    edge_ref[...] = edge


def rest_kernel(early, steps, unroll, nbr_ref, wide_ref, tiles_ref, smooth_in, smooth_ref):
    blocks = tiles_ref.shape[0]
    flip = is_flipped()
    if early:
        start = jnp.where(flip, 1, blocks - 1 - steps)
    else:
        start = jnp.where(flip, blocks - 1 - steps, 1)

    def body(i):
        b = start + i
        smooth_ref[b + 1] = convolve(wide_ref, tiles_ref, nbr_ref, b)

    groups(steps, unroll, body)


def edge_early_call(neighbours, own_a, own_b, got_a, tiles):
    blocks = tiles.shape[0]
    half, rows, _ = own_a.shape
    return call(
        edge_early_kernel,
        [IN_SMEM] + [IN_VMEM] * 4,
        [IN_VMEM] * 3,
        [
            VMEM((blocks + 2 * half - 2, rows, BLOCK), BF16),
            VMEM((blocks + 2, rows, BLOCK), BF16),
            jax.ShapeDtypeStruct((rows, BLOCK), BF16),
        ],
        [],
    )(neighbours, own_a, own_b, got_a, tiles)


def edge_late_call(neighbours, got_b, tiles, wide, smooth):
    _, rows, _ = got_b.shape
    return call(
        edge_late_kernel,
        [IN_SMEM] + [IN_VMEM] * 4,
        [IN_VMEM] * 3,
        [
            VMEM(wide.shape, BF16),
            VMEM(smooth.shape, BF16),
            jax.ShapeDtypeStruct((rows, BLOCK), BF16),
        ],
        [],
        {3: 0, 4: 1},
    )(neighbours, got_b, tiles, wide, smooth)


def rest_call(early, steps, unroll, neighbours, wide, tiles, smooth):
    return call(
        functools.partial(rest_kernel, early, steps, unroll),
        [IN_SMEM] + [IN_VMEM] * 3,
        [IN_VMEM],
        [VMEM(smooth.shape, BF16)],
        [],
        {3: 0},
    )(neighbours, wide, tiles, smooth)[0]


def back_kernel(part, steps, unroll, per, *refs):
    if part == 0:
        got_ref, table_ref, anom_ref, _, smooth_ref, out_ref = refs
    elif part == 1:
        table_ref, anom_ref, smooth_ref, _, out_ref = refs
    else:
        got_ref, table_ref, anom_ref, _, _, smooth_ref, out_ref = refs
    flip = is_flipped()
    blocks = table_ref.shape[0]
    shares = out_ref.shape[0]
    if part == 0:
        smooth_ref[jnp.where(flip, 0, blocks + 1)] = got_ref[...]
        start = jnp.where(flip, 0, blocks - steps)
    elif part == 1:
        start = jnp.where(flip, blocks - 1 - steps, 1)
    else:
        got = got_ref[...]
        present = is_present()
        smooth_ref[jnp.where(flip, blocks + 1, 0)] = jnp.where(present, got, jnp.zeros_like(got))
        start = jnp.where(flip, blocks - 1, 0)

    def body(i):
        c = start + i
        lhs = jnp.concatenate([smooth_ref[c], smooth_ref[c + 1], smooth_ref[c + 2]], axis=1)
        returned = jnp.dot(lhs, table_ref[c], preferred_element_type=F32)
        anom = anom_ref[c].astype(F32)
        value = jnp.sum(anom * returned.reshape(anom.shape), axis=0)
        lane = pl.multiple_of(lax.rem(c, per) * CHUNK, CHUNK)
        place = lax.div(c, per) - lax.axis_index("mem")
        place = jnp.where(place < 0, place + shares, place)
        out_ref[place, :, pl.ds(lane, CHUNK)] = value.astype(BF16)

    groups(steps, unroll, body)


def back_call(part, steps, unroll, shares, got, table, anom, smooth, out=None):
    chunks, _, fields, _ = anom.shape
    per = chunks // shares
    operands = ([] if part == 1 else [got]) + [table, anom, smooth]
    in_specs = [IN_VMEM] * len(operands)
    out_type = VMEM((shares, fields, per * CHUNK), BF16)
    if part == 2:
        out_type = jax.ShapeDtypeStruct(out_type.shape, BF16)
    smooth_type = VMEM(smooth.shape, BF16)
    last = len(operands) - 1
    if part == 0:
        out_shape, aliases = [smooth_type, out_type], {last: 0}
    elif part == 1:
        operands, in_specs = operands + [out], in_specs + [IN_VMEM]
        out_shape, aliases = [out_type], {last + 1: 0}
    else:
        operands, in_specs = operands + [out], in_specs + [IN_VMEM]
        out_shape, aliases = [smooth_type, out_type], {last: 0, last + 1: 1}
    return call(
        functools.partial(back_kernel, part, steps, unroll, per),
        in_specs,
        [IN_VMEM] * len(out_shape),
        out_shape,
        [],
        aliases,
    )(*operands)


def swaps(count, shares):
    inner, outer = [], []
    for i in range(count):
        far = i + 1 if i % 2 else i - 1
        for m in range(shares):
            here = i * shares + m
            inner.append((here, (i ^ 1) * shares + m))
            outer.append((here, far * shares + m if 0 <= far < count else i * shares + (m ^ 1)))
    return inner, outer


def swap(value, pairs):
    return lax.ppermute(value, ("space", "mem"), pairs)


def shards(increment, anomalies, interp_index, interp_weight, neighbour_blocks, tiles):
    members, _, columns = anomalies.shape
    chunks = columns // CHUNK
    count = lax.axis_size("space")
    shares = lax.axis_size("mem")
    assert count % 2 == 0 and shares % 2 == 0
    inner, outer = swaps(count, shares)
    head = chunks // 2 + 1
    table, own_b, carry, anom, *columns_here, neighbours = spread_first_call(
        head,
        FIRST_UNROLL,
        increment,
        anomalies,
        interp_index,
        interp_weight,
        neighbour_blocks,
    )
    got_b = swap(own_b, outer)
    table, own_a, tiles = spread_rest_call(
        chunks - head, REST_UNROLL, table, carry, (anom, *columns_here), tiles
    )
    got_a = swap(own_a, inner)
    early = chunks - head - 1
    wide, smooth, edge_a = edge_early_call(neighbours, own_a, own_b, got_a, tiles)
    halo_a = swap(edge_a, inner)
    smooth = rest_call(True, early, 3, neighbours, wide, tiles, smooth)
    smooth, out = back_call(0, early, 3, shares, halo_a, table, anom, smooth)
    wide, smooth, edge_b = edge_late_call(neighbours, got_b, tiles, wide, smooth)
    halo_b = swap(edge_b, outer)
    smooth = rest_call(False, head - 1, 4, neighbours, wide, tiles, smooth)
    (out,) = back_call(1, head, 3, shares, None, table, anom, smooth, out)
    _, pieces = back_call(2, 1, 1, shares, halo_b, table, anom, smooth, out)
    total = pieces[0].astype(F32)
    for shift in range(1, shares):
        got = lax.ppermute(
            pieces[shift],
            "mem",
            [(i, (i + shift) % shares) for i in range(shares)],
        )
        total = total + got.astype(F32)
    return total / (members * shares - 1)


def solution(mesh):
    in_specs = (
        P(None, "space"),
        P("mem", None, "space"),
        P(None, "space"),
        P(None, "space"),
        P(None, "space"),
        P("space", None, None, None),
    )
    out_specs = P(None, ("space", "mem"))
    return jax.shard_map(shards, mesh=mesh, in_specs=in_specs, out_specs=out_specs, check_vma=False)
```

time: 37.5 us -> 30.8 us (0.82)
  the two profiles are of different devices: /device:TPU:0 before, /device:TPU:4 now
where the time goes in v4:
time: 30.8 us; the launch traced here: 30.6 us
  Pallas kernels  10.9 us (35%)
  starting transfers between devices  9.83 us (32%)
  waiting for transfers between devices  9.07 us (29%)
  other arithmetic  0.69 us (2%)
    ppermute x4, waiting for transfers between devices, swap(): return lax.ppermute(value, ('space', 'mem'), pairs)  6.15 us
    ppermute x3, starting transfers between devices, shards(): lax.ppermute(pieces[shift], 'mem', [(i, (i + shift) % shares) for i in ra...  6.13 us
    ppermute x4, starting transfers between devices, swap(): return lax.ppermute(value, ('space', 'mem'), pairs)  3.7 us
    pallas_call x1, Pallas kernels, spread_first_call(): call(functools.partial(spread_kernel, steps, 0, unroll, chunks), [ANY] *...  3.42 us
    pallas_call x1, Pallas kernels, spread_rest_call(): call(functools.partial(spread_kernel, steps, chunks - steps, unroll, chun...  3.1 us
    ppermute x3, waiting for transfers between devices, shards(): lax.ppermute(pieces[shift], 'mem', [(i, (i + shift) % shares) for i in ra...  2.92 us
    pallas_call x3, Pallas kernels, back_call(): call(functools.partial(back_kernel, part, steps, unroll, per), in_specs,...  2.13 us
    pallas_call x2, Pallas kernels, rest_call(): call(functools.partial(rest_kernel, early, steps, unroll), [IN_SMEM] + [I...  1.68 us
  transfers between devices with their start and end apart: 7, of which 6 were waited for; matrix products, arithmetic and copies ran while one was open for 0% of the time, Pallas kernels for 13%

profile of v4, /device:TPU:4, one launch (start us, length us, event | category | flops | bytes accessed | tf_op | source)
XLA Modules:
  0.0 30.6 jit_solution(3605552266221044393)
XLA Ops:
  0.0 3.4 %shard_map.64 = (bf16[16,384,512]{2,1,0:T(8,128)(2,1)S(1)}, bf16[9,128,128]{2,1,0:T(8,128)(2,1)S(1)}, f32[2,128,128]{2,1,0:T(8,128)S(1)}, bf16[16,8,16,512]{3,2,...) custom-call(bf16[8,16,8192]{2,1,0:T(8,128)(2,1)} %refs_0_.1, ...), custom_call_target="tpu_custom_call" | custom-call | tf_op jit(solution)/shard_map/pallas_call | solution.py:194
  3.4 3.1 %shard_map.65 = (bf16[16,384,512]{2,1,0:T(8,128)(2,1)S(1)}, bf16[9,128,128]{2,1,0:T(8,128)(2,1)S(1)}, bf16[16,9,128,128]{3,2,1,0:T(8,128)(2,1)S(1)}) custom-call(bf16[16,8,16,512]{3,2,1,0:T(8,128)(2,1)S(1)} %get-tuple-element.27.refs_0_.refs_2_.refs_1_, f32[16,16,512]{2,1,0:T(8,128)S(1)} %get-tuple-element.28.refs_1_, ...), custom_call_target="tpu_custom_call", output_to_operand_aliasing={{0}: (6, {})} | custom-call | tf_op jit(solution)/shard_map/pallas_call | solution.py:220
  6.5 0.1 collective-permute-start.1
  6.6 1.5 %collective-permute-start = (bf16[9,128,128]{2,1,0:T(8,128)(2,1)S(1)}, bf16[9,128,128]{2,1,0:T(8,128)(2,1)S(1)}, u32[]{:S(2)}, u32[]{:S(2)}) collective-permute-start(bf16[9,128,128]{2,1,0:T(8,128)(2,1)S(1)} %get-tuple-element.26.own_b), channel_id=1, source_target_pairs={{0,1},{1,0},{2,3},{3,2},{4,8},{5,9},{6,10},{7,11},{8,4},{9,5},{10,... | collective-permute-start | bytes 884744 | tf_op jit(solution)/shard_map/ppermute | solution.py:436
  8.2 0.0 collective-permute-done.1.got_a
  8.2 0.3 shard_map.66
  8.5 0.2 collective-permute-start.2
  8.7 0.8 %shard_map.67.refs_3_ = bf16[18,128,128]{2,1,0:T(8,128)(2,1)S(1)} custom-call(s32[9,16]{1,0:T(8,128)S(4)} %get-tuple-element.25.nbr_ref, bf16[32,128,128]{2,1,0:T(8,128)(2,1)S(1)} %get-tuple-element.35.wide_ref.wide_in, bf16[16,9,128,128]{3,2,1,0:T(8,128)(2,1)S(1)} %get-tuple-element.33.tiles_ref, ...), custom_call_target="tpu_custom_call", output_to_operand_aliasing={{}: (3, {})} | custom-call | tf_op jit(solution)/shard_map/pallas_call | solution.py:351
  9.4 0.3 %collective-permute-done.2.refs_0_ = bf16[128,128]{1,0:T(8,128)(2,1)S(1)} collective-permute-done((bf16[128,128]{1,0:T(8,128)(2,1)S(1)}, bf16[128,128]{1,0:T(8,128)(2,1)S(1)}, u32[]{:S(2)}, u32[]{:S(2)}) %collective-permute-start.2) | collective-permute-done | bytes 32800 | tf_op jit(solution)/shard_map/ppermute | solution.py:436
  9.8 0.7 %shard_map.68 = (bf16[18,128,128]{2,1,0:T(8,128)(2,1)S(1)}, bf16[4,16,2048]{2,1,0:T(8,128)(2,1)S(1)}) custom-call(bf16[128,128]{1,0:T(8,128)(2,1)S(1)} %collective-permute-done.2.refs_0_, bf16[16,384,512]{2,1,0:T(8,128)(2,1)S(1)} %get-tuple-element.37.refs_1_.refs_0_, ...), custom_call_target="tpu_custom_call", output_to_operand_aliasing={{0}: (3, {})} | custom-call | tf_op jit(solution)/shard_map/pallas_call | solution.py:414
  10.5 5.5 %collective-permute-done.got_b = bf16[9,128,128]{2,1,0:T(8,128)(2,1)S(1)} collective-permute-done((bf16[9,128,128]{2,1,0:T(8,128)(2,1)S(1)}, bf16[9,128,128]{2,1,0:T(8,128)(2,1)S(1)}, u32[]{:S(2)}, u32[]{:S(2)}) %collective-permute-start) | collective-permute-done | bytes 294944 | tf_op jit(solution)/shard_map/ppermute | solution.py:436
  16.0 0.3 %shard_map.69 = (bf16[32,128,128]{2,1,0:T(8,128)(2,1)S(1)}, bf16[18,128,128]{2,1,0:T(8,128)(2,1)S(1)}, bf16[128,128]{1,0:T(8,128)(2,1)S(1)}) custom-call(s32[9,16]{1,0:T(8,128)S(4)} %get-tuple-element.25.nbr_ref, bf16[9,128,128]{2,1,0:T(8,128)(2,1)S(1)} %collective-permute-done.got_b, ...), custom_call_target="tpu_custom_call", output_to_operand_aliasing={{0}: (3, {}), {1}: (4, {})} | custom-call | tf_op jit(solution)/shard_map/pallas_call | solution.py:336
  16.3 1.9 %collective-permute-start.3 = (bf16[128,128]{1,0:T(8,128)(2,1)S(1)}, bf16[128,128]{1,0:T(8,128)(2,1)S(1)}, u32[]{:S(2)}, u32[]{:S(2)}) collective-permute-start(bf16[128,128]{1,0:T(8,128)(2,1)S(1)} %get-tuple-element.40), channel_id=1, source_target_pairs={{0,1},{1,0},{2,3},{3,2},{4,8},{5,9},{6,10},{7,11},{8,4},{9,5},{10,... | collective-permute-start | bytes 98312 | tf_op jit(solution)/shard_map/ppermute | solution.py:436
  18.2 0.9 %shard_map.70.refs_2_.refs_3_ = bf16[18,128,128]{2,1,0:T(8,128)(2,1)S(1)} custom-call(s32[9,16]{1,0:T(8,128)S(4)} %get-tuple-element.25.nbr_ref, bf16[32,128,128]{2,1,0:T(8,128)(2,1)S(1)} %get-tuple-element.41.wide_ref, bf16[16,9,128,128]{3,2,1,0:T(8,128)(2,1)S(1)} %get-tuple-element.33.tiles_ref, ...), custom_call_target="tpu_custom_call", output_to_operand_aliasing={{}: (3, {})} | custom-call | tf_op jit(solution)/shard_map/pallas_call | solution.py:351
  19.1 1.1 %shard_map.71.refs_4_ = bf16[4,16,2048]{2,1,0:T(8,128)(2,1)S(1)} custom-call(bf16[16,384,512]{2,1,0:T(8,128)(2,1)S(1)} %get-tuple-element.37.refs_1_.refs_0_, bf16[16,8,16,512]{3,2,1,0:T(8,128)(2,1)S(1)} %get-tuple-element.27.refs_0_.refs_2_.refs_1_, bf16[18,128,128]{2,1,0:T(8,128)(2,1)S(1)} %shard_map.70.refs_2_.refs_3_, ...), custom_call_target="tpu_custom_call", output_to_operand_aliasing={{}: (3, {})} | custom-call | tf_op jit(solution)/shard_map/pallas_call | solution.py:414
  20.3 0.3 %collective-permute-done.3.refs_0_ = bf16[128,128]{1,0:T(8,128)(2,1)S(1)} collective-permute-done((bf16[128,128]{1,0:T(8,128)(2,1)S(1)}, bf16[128,128]{1,0:T(8,128)(2,1)S(1)}, u32[]{:S(2)}, u32[]{:S(2)}) %collective-permute-start.3) | collective-permute-done | bytes 32800 | tf_op jit(solution)/shard_map/ppermute | solution.py:436
  20.6 0.2 shard_map.72
  20.9 2.2 %collective-permute-start.4 = (bf16[16,2048]{1,0:T(8,128)(2,1)S(1)}, bf16[16,2048]{1,0:T(8,128)(2,1)S(1)}, u32[]{:S(2)}, u32[]{:S(2)}) collective-permute-start(bf16[16,2048]{1,0:T(8,128)(2,1)S(1)} %get-tuple-element.45), channel_id=1, source_target_pairs={{0,1},{1,2},{2,3},{3,0},{4,5},{5,6},{6,7},{7,4},{8,9},{9,10},{10,1... | collective-permute-start | bytes 196616 | tf_op jit(solution)/shard_map/ppermute | solution.py:473
  23.1 2.6 %collective-permute-start.5 = (bf16[16,2048]{1,0:T(8,128)(2,1)S(1)}, bf16[16,2048]{1,0:T(8,128)(2,1)S(1)}, u32[]{:S(2)}, u32[]{:S(2)}) collective-permute-start(bf16[16,2048]{1,0:T(8,128)(2,1)S(1)} %get-tuple-element.47), channel_id=1, source_target_pairs={{0,2},{1,3},{2,0},{3,1},{4,6},{5,7},{6,4},{7,5},{8,10},{9,11},{10,... | collective-permute-start | bytes 196616 | tf_op jit(solution)/shard_map/ppermute | solution.py:473
  25.7 1.3 %collective-permute-start.6 = (bf16[16,2048]{1,0:T(8,128)(2,1)S(1)}, bf16[16,2048]{1,0:T(8,128)(2,1)S(1)}, u32[]{:S(2)}, u32[]{:S(2)}) collective-permute-start(bf16[16,2048]{1,0:T(8,128)(2,1)S(1)} %get-tuple-element.46), channel_id=1, source_target_pairs={{0,3},{1,0},{2,1},{3,2},{4,7},{5,4},{6,5},{7,6},{8,11},{9,8},{10,9... | collective-permute-start | bytes 196616 | tf_op jit(solution)/shard_map/ppermute | solution.py:473
  27.0 0.7 %collective-permute-done.4 = bf16[16,2048]{1,0:T(8,128)(2,1)S(1)} collective-permute-done((bf16[16,2048]{1,0:T(8,128)(2,1)S(1)}, bf16[16,2048]{1,0:T(8,128)(2,1)S(1)}, u32[]{:S(2)}, u32[]{:S(2)}) %collective-permute-start.4) | collective-permute-done | bytes 65568 | tf_op jit(solution)/shard_map/ppermute | solution.py:473
  27.8 0.8 %collective-permute-done.5 = bf16[16,2048]{1,0:T(8,128)(2,1)S(1)} collective-permute-done((bf16[16,2048]{1,0:T(8,128)(2,1)S(1)}, bf16[16,2048]{1,0:T(8,128)(2,1)S(1)}, u32[]{:S(2)}, u32[]{:S(2)}) %collective-permute-start.5) | collective-permute-done | bytes 65568 | tf_op jit(solution)/shard_map/ppermute | solution.py:473
  28.5 1.4 %collective-permute-done.6 = bf16[16,2048]{1,0:T(8,128)(2,1)S(1)} collective-permute-done((bf16[16,2048]{1,0:T(8,128)(2,1)S(1)}, bf16[16,2048]{1,0:T(8,128)(2,1)S(1)}, u32[]{:S(2)}, u32[]{:S(2)}) %collective-permute-start.6) | collective-permute-done | bytes 65568 | tf_op jit(solution)/shard_map/ppermute | solution.py:473
  29.9 0.7 %fusion.2 = f32[16,2048]{1,0:T(8,128)} fusion(bf16[16,2048]{1,0:T(8,128)(2,1)S(1)} %collective-permute-done.6, bf16[16,2048]{1,0:T(8,128)(2,1)S(1)} %collective-permute-done.5, bf16[16,2048]{1,0:T(8,128)(2,1)S(1)} %collective-permute-done.4, bf16[4,16,2048]{2,1,0:T(8,128)(2,1)S(1)} %get-tuple-element.44), kind=kLoop, calls=%fused_computation.3 | loop fusion | flops 262144 | bytes 393216 | tf_op jit(solution)/shard_map/div | solution.py:479
  (1 shorter events, 0.0 us)
Async XLA Ops:
  6.5 1.6 %collective-permute-start.1 = (bf16[9,128,128]{2,1,0:T(8,128)(2,1)S(1)}, bf16[9,128,128]{2,1,0:T(8,128)(2,1)S(1)}, u32[]{:S(2)}, u32[]{:S(2)}) collective-permute-start(bf16[9,128,128]{2,1,0:T(8,128)(2,1)S(1)} %get-tuple-element.34.own_a), channel_id=1, source_target_pairs={{0,4},{1,5},{2,6},{3,7},{4,0},{5,1},{6,2},{7,3},{8,12},{9,13},{10,... | collective-permute-start | bytes 884744 | tf_op jit(solution)/shard_map/ppermute | solution.py:436
  6.6 9.4 %collective-permute-start = (bf16[9,128,128]{2,1,0:T(8,128)(2,1)S(1)}, bf16[9,128,128]{2,1,0:T(8,128)(2,1)S(1)}, u32[]{:S(2)}, u32[]{:S(2)}) collective-permute-start(bf16[9,128,128]{2,1,0:T(8,128)(2,1)S(1)} %get-tuple-element.26.own_b), channel_id=1, source_target_pairs={{0,1},{1,0},{2,3},{3,2},{4,8},{5,9},{6,10},{7,11},{8,4},{9,5},{10,... | collective-permute-start | bytes 884744 | tf_op jit(solution)/shard_map/ppermute | solution.py:436
  8.5 1.3 %collective-permute-start.2 = (bf16[128,128]{1,0:T(8,128)(2,1)S(1)}, bf16[128,128]{1,0:T(8,128)(2,1)S(1)}, u32[]{:S(2)}, u32[]{:S(2)}) collective-permute-start(bf16[128,128]{1,0:T(8,128)(2,1)S(1)} %get-tuple-element.36), channel_id=1, source_target_pairs={{0,4},{1,5},{2,6},{3,7},{4,0},{5,1},{6,2},{7,3},{8,12},{9,13},{10,... | collective-permute-start | bytes 98312 | tf_op jit(solution)/shard_map/ppermute | solution.py:436
  16.3 4.3 %collective-permute-start.3 = (bf16[128,128]{1,0:T(8,128)(2,1)S(1)}, bf16[128,128]{1,0:T(8,128)(2,1)S(1)}, u32[]{:S(2)}, u32[]{:S(2)}) collective-permute-start(bf16[128,128]{1,0:T(8,128)(2,1)S(1)} %get-tuple-element.40), channel_id=1, source_target_pairs={{0,1},{1,0},{2,3},{3,2},{4,8},{5,9},{6,10},{7,11},{8,4},{9,5},{10,... | collective-permute-start | bytes 98312 | tf_op jit(solution)/shard_map/ppermute | solution.py:436
  20.9 6.9 %collective-permute-start.4 = (bf16[16,2048]{1,0:T(8,128)(2,1)S(1)}, bf16[16,2048]{1,0:T(8,128)(2,1)S(1)}, u32[]{:S(2)}, u32[]{:S(2)}) collective-permute-start(bf16[16,2048]{1,0:T(8,128)(2,1)S(1)} %get-tuple-element.45), channel_id=1, source_target_pairs={{0,1},{1,2},{2,3},{3,0},{4,5},{5,6},{6,7},{7,4},{8,9},{9,10},{10,1... | collective-permute-start | bytes 196616 | tf_op jit(solution)/shard_map/ppermute | solution.py:473
  23.1 5.4 %collective-permute-start.5 = (bf16[16,2048]{1,0:T(8,128)(2,1)S(1)}, bf16[16,2048]{1,0:T(8,128)(2,1)S(1)}, u32[]{:S(2)}, u32[]{:S(2)}) collective-permute-start(bf16[16,2048]{1,0:T(8,128)(2,1)S(1)} %get-tuple-element.47), channel_id=1, source_target_pairs={{0,2},{1,3},{2,0},{3,1},{4,6},{5,7},{6,4},{7,5},{8,10},{9,11},{10,... | collective-permute-start | bytes 196616 | tf_op jit(solution)/shard_map/ppermute | solution.py:473
  25.7 4.3 %collective-permute-start.6 = (bf16[16,2048]{1,0:T(8,128)(2,1)S(1)}, bf16[16,2048]{1,0:T(8,128)(2,1)S(1)}, u32[]{:S(2)}, u32[]{:S(2)}) collective-permute-start(bf16[16,2048]{1,0:T(8,128)(2,1)S(1)} %get-tuple-element.46), channel_id=1, source_target_pairs={{0,3},{1,0},{2,1},{3,2},{4,7},{5,4},{6,5},{7,6},{8,11},{9,8},{10,9... | collective-permute-start | bytes 196616 | tf_op jit(solution)/shard_map/ppermute | solution.py:473

commit v5 on v4

v5 whole, which is shorter than its diff:
```python
import functools

import jax
import jax.numpy as jnp
from jax import lax
from jax.experimental import pallas as pl
from jax.experimental.pallas import tpu as pltpu
from jax.sharding import PartitionSpec as P


BLOCK = 128
HI = 128
RATIO = 4
CHUNK = RATIO * BLOCK
WIN = 3 * BLOCK
REACH = 2 * HI + 32
F32 = jnp.float32
BF16 = jnp.bfloat16
NEAR = 5
VMEM = pltpu.VMEM
ANY = pl.BlockSpec(memory_space=pl.ANY)
IN_VMEM = pl.BlockSpec(memory_space=pltpu.VMEM)
IN_SMEM = pl.BlockSpec(memory_space=pltpu.SMEM)


def is_present():
    space = lax.axis_index("space")
    last = lax.axis_size("space") - 1
    return jnp.where((space & 1) == 1, space < last, space > 0)


def in_hbm(x):
    return pltpu.with_memory_space_constraint(x, pltpu.HBM)


def call(kernel, in_specs, out_specs, out_shape, scratch, aliases=None):
    return pl.pallas_call(
        kernel,
        in_specs=in_specs,
        out_specs=out_specs,
        out_shape=out_shape,
        scratch_shapes=scratch,
        input_output_aliases=aliases or {},
        compiler_params=pltpu.CompilerParams(vmem_limit_bytes=16 * 1024 * 1024),
        cost_estimate=pl.CostEstimate(flops=0, bytes_accessed=0, transcendentals=0),
    )


def groups(steps, unroll, body):
    unroll = unroll if steps % unroll == 0 else 1

    def group(g, carry):
        for j in range(unroll):
            body(g * unroll + j)
        return carry

    lax.fori_loop(0, steps // unroll, group, 0)


def build_table(local, weight):
    i0, i1, i2 = local[0:1], local[1:2], local[2:3]
    w0, w1, w2 = weight[0:1], weight[1:2], weight[2:3]
    zero = jnp.zeros_like(w0)
    w0 = w0 + jnp.where(i1 == i0, w1, zero) + jnp.where(i2 == i0, w2, zero)
    w1 = w1 + jnp.where(i2 == i1, w2, zero)
    rows = REACH // 16
    iota = lax.broadcasted_iota(jnp.int32, (rows, 16, BLOCK), 0) * 16 + lax.broadcasted_iota(
        jnp.int32, (rows, 16, BLOCK), 1
    )
    iota = iota.astype(jnp.int16)
    parts = []
    for s in range(CHUNK // BLOCK):
        cols = slice(s * BLOCK, (s + 1) * BLOCK)
        base = s * BLOCK // RATIO

        def wide(x, kind):
            return jnp.broadcast_to(x[:, cols], (16, BLOCK)).astype(kind)[None]

        table = jnp.zeros((1, 16, BLOCK), BF16)
        for index, value in ((i2, w2), (i1, w1), (i0, w0)):
            table = jnp.where(wide(index - base, jnp.int16) == iota, wide(value, BF16), table)
        pieces = [table.reshape(REACH, BLOCK)]
        if base:
            pieces.insert(0, jnp.zeros((base, BLOCK), BF16))
        if base + REACH < WIN:
            pieces.append(jnp.zeros((WIN - base - REACH, BLOCK), BF16))
        parts.append(jnp.concatenate(pieces, axis=0))
    return jnp.concatenate(parts, axis=1)


def is_flipped():
    return (lax.axis_index("space") & 1) == 1


def spread_kernel(steps, done, chunks, *refs):
    first, last = done == 0, done + steps == chunks
    if first:
        anom_hbm, incr_hbm, index_hbm, weight_hbm, nbr_hbm = refs[:5]
        table_ref, out_ref, carry_ref = refs[5:8]
        anom_ref, incr_ref, index_ref, weight_ref, nbr_ref = refs[8:13]
        anom_sem, incr_sem, some_sem = refs[13:]
    else:
        anom_ref, incr_ref, index_ref, weight_ref, carry_in = refs[:5]
        table_ref, out_ref = refs[6:8]
        carry_ref = refs[-1]
    flip = is_flipped()

    def chunk_of(step):
        return jnp.where(flip, chunks - 1 - step, step)

    def lanes(c):
        return pl.ds(pl.multiple_of(c * CHUNK, CHUNK), CHUNK)

    if first:
        copies = [
            pltpu.make_async_copy(source, target, some_sem.at[k])
            for k, (source, target) in enumerate(
                ((index_hbm, index_ref), (weight_hbm, weight_ref), (nbr_hbm, nbr_ref))
            )
        ]
        columns = []
        for k, (begin, end) in enumerate(((0, steps), (steps, chunks))):
            low = jnp.where(flip, chunks - end, begin)
            here = pl.ds(pl.multiple_of(low * CHUNK, CHUNK), (end - begin) * CHUNK)
            columns.append(
                (
                    pltpu.make_async_copy(
                        anom_hbm.at[:, :, here], anom_ref.at[:, :, here], anom_sem.at[k]
                    ),
                    pltpu.make_async_copy(
                        incr_hbm.at[:, here], incr_ref.at[:, here], incr_sem.at[k]
                    ),
                )
            )
        for copy in (*copies[:2], *columns[0], *columns[1], copies[2]):
            copy.start()
        acc0 = acc1 = jnp.zeros(carry_ref.shape[1:], F32)
        for copy in copies[:2]:
            copy.wait()
    else:
        acc0, acc1 = carry_in[0], carry_in[1]
    rows = anom_ref.shape[0] * anom_ref.shape[1]
    total = out_ref.shape[0]

    def table_of(i):
        c = chunk_of(done + i)
        table = build_table(index_ref[:, lanes(c)] - c * BLOCK, weight_ref[:, lanes(c)])
        table_ref[c] = table
        return table

    before = steps if first else 0
    if first:
        for i in range(before):
            table_of(i)
        for copy in columns[0]:
            copy.wait()
    for i in range(steps):
        c = chunk_of(done + i)
        table = table_ref[c] if i < before else table_of(i)
        weighted = (anom_ref[:, :, lanes(c)].astype(F32) * incr_ref[:, lanes(c)][None]).astype(BF16)
        window = lax.dot_general(
            table,
            weighted.reshape(rows, CHUNK),
            (((1,), (1,)), ((), ())),
            preferred_element_type=F32,
        )
        near, mid, far = window[:BLOCK], window[BLOCK : 2 * BLOCK], window[2 * BLOCK :]
        ready = acc0 + jnp.where(flip, far, near)
        out_ref[jnp.where(flip, total - 1 - i, i)] = ready.T.astype(BF16)
        acc0 = acc1 + mid
        acc1 = jnp.where(flip, near, far)
    if last:
        out_ref[jnp.where(flip, 1, steps)] = acc0.T.astype(BF16)
        out_ref[jnp.where(flip, 0, steps + 1)] = acc1.T.astype(BF16)
    else:
        carry_ref[0] = acc0
        carry_ref[1] = acc1
    if first:
        for copy in (*columns[1], copies[2]):
            copy.wait()


def spread_first_call(steps, increment, anomalies, index, weight, neighbours):
    members, fields, columns = anomalies.shape
    rows = members * fields
    chunks = columns // CHUNK
    return call(
        functools.partial(spread_kernel, steps, 0, chunks),
        [ANY] * 5,
        [IN_VMEM] * 7 + [IN_SMEM],
        [
            VMEM((chunks, WIN, CHUNK), BF16),
            jax.ShapeDtypeStruct((steps, rows, BLOCK), BF16),
            VMEM((2, BLOCK, rows), F32),
            VMEM(anomalies.shape, BF16),
            VMEM(increment.shape, F32),
            VMEM(index.shape, jnp.int32),
            VMEM(weight.shape, F32),
            pltpu.SMEM(neighbours.shape, jnp.int32),
        ],
        [
            pltpu.SemaphoreType.DMA((2,)),
            pltpu.SemaphoreType.DMA((2,)),
            pltpu.SemaphoreType.DMA((3,)),
        ],
    )(*(in_hbm(x) for x in (anomalies, increment, index, weight, neighbours)))


def spread_more_call(done, steps, table, carry, columns):
    chunks = table.shape[0]
    rows = carry.shape[2]
    last = done + steps == chunks
    out_shape = [
        VMEM(table.shape, BF16),
        jax.ShapeDtypeStruct((steps + 2 * last, rows, BLOCK), BF16),
    ]
    if not last:
        out_shape.append(VMEM(carry.shape, F32))
    return call(
        functools.partial(spread_kernel, steps, done, chunks),
        [IN_VMEM] * 6,
        [IN_VMEM] * len(out_shape),
        out_shape,
        [],
        {5: 0},
    )(*columns, carry, table)


def convolve(wide_ref, tiles_ref, nbr_ref, b):
    count = tiles_ref.shape[1]
    picked = jnp.concatenate([wide_ref[nbr_ref[n, b]] for n in range(count)], axis=1)
    weights = tiles_ref[b].reshape(count * BLOCK, BLOCK)
    return jnp.dot(picked, weights, preferred_element_type=F32).astype(BF16)


def edge_early_kernel(
    nbr_ref, own_a, own_near, own_far, got_a, tiles_ref, wide_ref, smooth_ref, edge_ref
):
    half = own_a.shape[0]
    near = own_near.shape[0]
    reach = half - 1
    blocks = tiles_ref.shape[0]
    top = blocks + reach
    flip = is_flipped()

    @pl.when(jnp.logical_not(flip))
    def _():
        wide_ref[reach - 1 : reach - 1 + near] = own_near[...]
        wide_ref[reach - 1 + near : reach - 1 + half] = own_far[...]
        wide_ref[reach - 1 + half : top - 1] = own_a[0 : half - 2]
        wide_ref[top - 1 : top + 1] = (
            got_a[0:2].astype(F32) + own_a[half - 2 : half].astype(F32)
        ).astype(BF16)
        wide_ref[top + 1 : top + reach] = got_a[2:half]

    @pl.when(flip)
    def _():
        wide_ref[0 : reach - 1] = got_a[0 : reach - 1]
        wide_ref[reach - 1 : reach + 1] = (
            got_a[reach - 1 : reach + 1].astype(F32) + own_a[0:2].astype(F32)
        ).astype(BF16)
        wide_ref[reach + 1 : reach - 1 + half] = own_a[2:half]
        wide_ref[reach - 1 + half : top + 1 - near] = own_far[...]
        wide_ref[top + 1 - near : top + 1] = own_near[...]

    b = jnp.where(flip, 0, blocks - 1)
    edge = convolve(wide_ref, tiles_ref, nbr_ref, b)
    smooth_ref[b + 1] = edge
    edge_ref[...] = edge


def edge_late_kernel(
    nbr_ref, got_near, got_far, tiles_ref, wide_in, smooth_in, wide_ref, smooth_ref, edge_ref
):
    near = got_near.shape[0]
    half = near + got_far.shape[0]
    reach = half - 1
    blocks = tiles_ref.shape[0]
    top = blocks + reach
    flip = is_flipped()
    present = is_present()

    def there(value):
        return jnp.where(present, value, jnp.zeros_like(value))

    @pl.when(jnp.logical_not(flip))
    def _():
        wide_ref[0 : half - near] = there(got_far[...])
        wide_ref[half - near : reach - 1] = there(got_near[0 : near - 2])
        both = wide_ref[reach - 1 : reach + 1].astype(F32) + there(got_near[near - 2 :].astype(F32))
        wide_ref[reach - 1] = there(both[0]).astype(BF16)
        wide_ref[reach] = both[1].astype(BF16)

    @pl.when(flip)
    def _():
        both = wide_ref[top - 1 : top + 1].astype(F32) + there(got_near[0:2].astype(F32))
        wide_ref[top - 1] = both[0].astype(BF16)
        wide_ref[top] = there(both[1]).astype(BF16)
        wide_ref[top + 1 : top - 1 + near] = there(got_near[2:near])
        wide_ref[top - 1 + near : top + reach] = there(got_far[...])

    b = jnp.where(flip, blocks - 1, 0)
    edge = convolve(wide_ref, tiles_ref, nbr_ref, b)
    smooth_ref[b + 1] = edge
    edge_ref[...] = edge


def rest_kernel(early, steps, unroll, nbr_ref, wide_ref, tiles_ref, smooth_in, smooth_ref):
    blocks = tiles_ref.shape[0]
    flip = is_flipped()
    if early:
        start = jnp.where(flip, 1, blocks - 1 - steps)
    else:
        start = jnp.where(flip, blocks - 1 - steps, 1)

    def body(i):
        b = start + i
        smooth_ref[b + 1] = convolve(wide_ref, tiles_ref, nbr_ref, b)

    groups(steps, unroll, body)


def edge_early_call(neighbours, own_a, own_near, own_far, got_a, tiles):
    blocks = tiles.shape[0]
    half, rows, _ = own_a.shape
    return call(
        edge_early_kernel,
        [IN_SMEM] + [IN_VMEM] * 5,
        [IN_VMEM] * 3,
        [
            VMEM((blocks + 2 * half - 2, rows, BLOCK), BF16),
            VMEM((blocks + 2, rows, BLOCK), BF16),
            jax.ShapeDtypeStruct((rows, BLOCK), BF16),
        ],
        [],
    )(neighbours, own_a, own_near, own_far, got_a, tiles)


def edge_late_call(neighbours, got_near, got_far, tiles, wide, smooth):
    _, rows, _ = got_near.shape
    return call(
        edge_late_kernel,
        [IN_SMEM] + [IN_VMEM] * 5,
        [IN_VMEM] * 3,
        [
            VMEM(wide.shape, BF16),
            VMEM(smooth.shape, BF16),
            jax.ShapeDtypeStruct((rows, BLOCK), BF16),
        ],
        [],
        {4: 0, 5: 1},
    )(neighbours, got_near, got_far, tiles, wide, smooth)


def rest_call(early, steps, unroll, neighbours, wide, tiles, smooth):
    return call(
        functools.partial(rest_kernel, early, steps, unroll),
        [IN_SMEM] + [IN_VMEM] * 3,
        [IN_VMEM],
        [VMEM(smooth.shape, BF16)],
        [],
        {3: 0},
    )(neighbours, wide, tiles, smooth)[0]


def back_kernel(part, steps, unroll, per, *refs):
    if part == 0:
        got_ref, table_ref, anom_ref, _, smooth_ref, out_ref = refs
    elif part == 1:
        table_ref, anom_ref, smooth_ref, _, out_ref = refs
    else:
        got_ref, table_ref, anom_ref, _, _, smooth_ref, out_ref = refs
    flip = is_flipped()
    blocks = table_ref.shape[0]
    shares = out_ref.shape[0]
    if part == 0:
        smooth_ref[jnp.where(flip, 0, blocks + 1)] = got_ref[...]
        start = jnp.where(flip, 0, blocks - steps)
    elif part == 1:
        start = jnp.where(flip, blocks - 1 - steps, 1)
    else:
        got = got_ref[...]
        present = is_present()
        smooth_ref[jnp.where(flip, blocks + 1, 0)] = jnp.where(present, got, jnp.zeros_like(got))
        start = jnp.where(flip, blocks - 1, 0)

    def body(i):
        c = start + i
        lhs = jnp.concatenate([smooth_ref[c], smooth_ref[c + 1], smooth_ref[c + 2]], axis=1)
        returned = jnp.dot(lhs, table_ref[c], preferred_element_type=F32)
        here = pl.ds(pl.multiple_of(c * CHUNK, CHUNK), CHUNK)
        anom = anom_ref[:, :, here].astype(F32)
        value = jnp.sum(anom * returned.reshape(anom.shape), axis=0)
        lane = pl.multiple_of(lax.rem(c, per) * CHUNK, CHUNK)
        place = lax.div(c, per) - lax.axis_index("mem")
        place = jnp.where(place < 0, place + shares, place)
        out_ref[place, :, pl.ds(lane, CHUNK)] = value.astype(BF16)

    groups(steps, unroll, body)


def back_call(part, steps, unroll, shares, got, table, anom, smooth, out=None):
    chunks, fields = table.shape[0], anom.shape[1]
    per = chunks // shares
    operands = ([] if part == 1 else [got]) + [table, anom, smooth]
    in_specs = [IN_VMEM] * len(operands)
    out_type = VMEM((shares, fields, per * CHUNK), BF16)
    if part == 2:
        out_type = jax.ShapeDtypeStruct(out_type.shape, BF16)
    smooth_type = VMEM(smooth.shape, BF16)
    last = len(operands) - 1
    if part == 0:
        out_shape, aliases = [smooth_type, out_type], {last: 0}
    elif part == 1:
        operands, in_specs = operands + [out], in_specs + [IN_VMEM]
        out_shape, aliases = [out_type], {last + 1: 0}
    else:
        operands, in_specs = operands + [out], in_specs + [IN_VMEM]
        out_shape, aliases = [smooth_type, out_type], {last: 0, last + 1: 1}
    return call(
        functools.partial(back_kernel, part, steps, unroll, per),
        in_specs,
        [IN_VMEM] * len(out_shape),
        out_shape,
        [],
        aliases,
    )(*operands)


def swaps(count, shares):
    inner, outer = [], []
    for i in range(count):
        far = i + 1 if i % 2 else i - 1
        for m in range(shares):
            here = i * shares + m
            inner.append((here, (i ^ 1) * shares + m))
            outer.append((here, far * shares + m if 0 <= far < count else i * shares + (m ^ 1)))
    return inner, outer


def swap(value, pairs):
    return lax.ppermute(value, ("space", "mem"), pairs)


def shards(increment, anomalies, interp_index, interp_weight, neighbour_blocks, tiles):
    members, _, columns = anomalies.shape
    chunks = columns // CHUNK
    count = lax.axis_size("space")
    shares = lax.axis_size("mem")
    assert count % 2 == 0 and shares % 2 == 0
    inner, outer = swaps(count, shares)
    head = chunks // 2 + 1
    table, own_near, carry, anom, *columns_here, neighbours = spread_first_call(
        NEAR, increment, anomalies, interp_index, interp_weight, neighbour_blocks
    )
    columns_here = (anom, *columns_here)
    got_near = swap(own_near, outer)
    table, own_far, carry = spread_more_call(NEAR, head - NEAR, table, carry, columns_here)
    got_far = swap(own_far, outer)
    table, own_a = spread_more_call(head, chunks - head, table, carry, columns_here)
    got_a = swap(own_a, inner)
    early = chunks - head - 1
    wide, smooth, edge_a = edge_early_call(
        neighbours, own_a, own_near, own_far, got_a, tiles
    )
    halo_a = swap(edge_a, inner)
    smooth = rest_call(True, early, early, neighbours, wide, tiles, smooth)
    smooth, out = back_call(0, early, early, shares, halo_a, table, anom, smooth)
    wide, smooth, edge_b = edge_late_call(neighbours, got_near, got_far, tiles, wide, smooth)
    halo_b = swap(edge_b, outer)
    smooth = rest_call(False, head - 1, head - 1, neighbours, wide, tiles, smooth)
    (out,) = back_call(1, head, head, shares, None, table, anom, smooth, out)
    _, pieces = back_call(2, 1, 1, shares, halo_b, table, anom, smooth, out)
    total = pieces[0].astype(F32)
    for shift in range(1, shares):
        pairs = [(i, (i + shift) % shares) for i in range(shares)]
        got = lax.ppermute(pieces[shift], "mem", pairs)
        total = total + got.astype(F32)
    return total / (members * shares - 1)


def solution(mesh):
    in_specs = (
        P(None, "space"),
        P("mem", None, "space"),
        P(None, "space"),
        P(None, "space"),
        P(None, "space"),
        P("space", None, None, None),
    )
    out_specs = P(None, ("space", "mem"))
    return jax.shard_map(shards, mesh=mesh, in_specs=in_specs, out_specs=out_specs, check_vma=False)
```

time: 30.8 us -> 29.1 us (0.945)
  the two profiles are of different devices: /device:TPU:4 before, /device:TPU:0 now
where the time goes in v5:
time: 29.1 us; the launch traced here: 28.6 us
  waiting for transfers between devices  10.1 us (35%)
  starting transfers between devices  10 us (34%)
  Pallas kernels  7.61 us (26%)
  other arithmetic  0.69 us (2%)
    ppermute x3, waiting for transfers between devices, shards(): got = lax.ppermute(pieces[shift], 'mem', pairs)  6.24 us
    ppermute x5, starting transfers between devices, swap(): return lax.ppermute(value, ('space', 'mem'), pairs)  5.18 us
    ppermute x3, starting transfers between devices, shards(): got = lax.ppermute(pieces[shift], 'mem', pairs)  4.85 us
    ppermute x5, waiting for transfers between devices, swap(): return lax.ppermute(value, ('space', 'mem'), pairs)  3.85 us
    pallas_call x1, Pallas kernels, spread_first_call(): call(functools.partial(spread_kernel, steps, 0, chunks), [ANY] * 5, [IN_V...  2.21 us
    pallas_call x2, Pallas kernels, spread_more_call(): call(functools.partial(spread_kernel, steps, done, chunks), [IN_VMEM] * 6...  1.81 us
    pallas_call x3, Pallas kernels, back_call(): call(functools.partial(back_kernel, part, steps, unroll, per), in_specs,...  1.61 us
    pallas_call x2, Pallas kernels, rest_call(): call(functools.partial(rest_kernel, early, steps, unroll), [IN_SMEM] + [I...  1.37 us
  transfers between devices with their start and end apart: 8, of which 6 were waited for; matrix products, arithmetic and copies ran while one was open for 0% of the time, Pallas kernels for 11%

profile of v5, /device:TPU:0, one launch (start us, length us, event | category | flops | bytes accessed | tf_op | source)
XLA Modules:
  0.0 28.6 jit_solution(3919095426598693215)
XLA Ops:
  0.0 2.2 %shard_map.64 = (bf16[16,384,512]{2,1,0:T(8,128)(2,1)S(1)}, bf16[5,128,128]{2,1,0:T(8,128)(2,1)S(1)}, f32[2,128,128]{2,1,0:T(8,128)S(1)}, bf16[8,16,8192]{2,1,0:...) custom-call(bf16[8,16,8192]{2,1,0:T(8,128)(2,1)} %refs_0_.1, ...), custom_call_target="tpu_custom_call" | custom-call | tf_op jit(solution)/shard_map/pallas_call | solution.py:187
  2.2 0.7 %shard_map.65 = (bf16[16,384,512]{2,1,0:T(8,128)(2,1)S(1)}, bf16[4,128,128]{2,1,0:T(8,128)(2,1)S(1)}, f32[2,128,128]{2,1,0:T(8,128)S(1)}) custom-call(bf16[8,16,8192]{2,1,0:T(8,128)(2,1)S(1)} %get-tuple-element.29.refs_0_.refs_2_.refs_1_, f32[16,8192]{1,0:T(8,128)S(1)} %get-tuple-element.30.refs_1_, ...), custom_call_target="tpu_custom_call", output_to_operand_aliasing={{0}: (5, {})} | custom-call | tf_op jit(solution)/shard_map/pallas_call | solution.py:219
  2.9 0.0 slice-start
  3.0 0.0 slice-start.1
  3.0 1.1 %shard_map.66 = (bf16[16,384,512]{2,1,0:T(8,128)(2,1)S(1)}, bf16[9,128,128]{2,1,0:T(8,128)(2,1)S(1)}) custom-call(bf16[8,16,8192]{2,1,0:T(8,128)(2,1)S(1)} %get-tuple-element.29.refs_0_.refs_2_.refs_1_, f32[16,8192]{1,0:T(8,128)S(1)} %get-tuple-element.30.refs_1_, s32[3,8192]{1,0:T(4,128)S(1)} %get-tuple-element.31.refs_2_, ...), custom_call_target="tpu_custom_call", output_to_operand_aliasing={{0}: (5, {})} | custom-call | tf_op jit(solution)/shard_map/pallas_call | solution.py:219
  4.1 0.6 %collective-permute-start.2 = (bf16[9,128,128]{2,1,0:T(8,128)(2,1)S(1)}, bf16[9,128,128]{2,1,0:T(8,128)(2,1)S(1)}, u32[]{:S(2)}, u32[]{:S(2)}) collective-permute-start(bf16[9,128,128]{2,1,0:T(8,128)(2,1)S(1)} %get-tuple-element.38.own_a), channel_id=1, source_target_pairs={{0,4},{1,5},{2,6},{3,7},{4,0},{5,1},{6,2},{7,3},{8,12},{9,13},{10,... | collective-permute-start | bytes 884744 | tf_op jit(solution)/shard_map/ppermute | solution.py:442
  4.6 2.6 %collective-permute-start = (bf16[5,128,128]{2,1,0:T(8,128)(2,1)S(1)}, bf16[5,128,128]{2,1,0:T(8,128)(2,1)S(1)}, u32[]{:S(2)}, u32[]{:S(2)}) collective-permute-start(bf16[5,128,128]{2,1,0:T(8,128)(2,1)S(1)} %get-tuple-element.28.own_near), channel_id=1, source_target_pairs={{0,1},{1,0},{2,3},{3,2},{4,8},{5,9},{6,10},{7,11},{8,4},{9,5},{10,... | collective-permute-start | bytes 491528 | tf_op jit(solution)/shard_map/ppermute | solution.py:442
  7.2 0.1 collective-permute-start.1
  7.3 0.0 collective-permute-done.2.got_a
  7.3 0.0 slice-done
  7.3 0.0 slice-done.1
  7.3 0.3 %shard_map.67 = (bf16[32,128,128]{2,1,0:T(8,128)(2,1)S(1)}, bf16[18,128,128]{2,1,0:T(8,128)(2,1)S(1)}, bf16[128,128]{1,0:T(8,128)(2,1)S(1)}) custom-call(s32[9,16]{1,0:T(8,128)S(4)} %get-tuple-element.27.nbr_ref, bf16[9,128,128]{2,1,0:T(8,128)(2,1)S(1)} %get-tuple-element.38.own_a, bf16[5,128,128]{2,1,0:T(8,128)(2,1)S(1)} %get-tuple-element.28.own_near, ...), custom_call_target="tpu_custom_call" | custom-call | tf_op jit(solution)/shard_map/pallas_call | solution.py:326
  7.7 0.1 collective-permute-start.3
  7.7 0.6 %shard_map.68.refs_3_ = bf16[18,128,128]{2,1,0:T(8,128)(2,1)S(1)} custom-call(s32[9,16]{1,0:T(8,128)S(4)} %get-tuple-element.27.nbr_ref, bf16[32,128,128]{2,1,0:T(8,128)(2,1)S(1)} %get-tuple-element.39.wide_ref.wide_in, bf16[16,9,128,128]{3,2,1,0:T(8,128)(2,1)S(1)} %bitcast.10, ...), custom_call_target="tpu_custom_call", output_to_operand_aliasing={{}: (3, {})} | custom-call | tf_op jit(solution)/shard_map/pallas_call | solution.py:356
  8.4 0.6 %collective-permute-done.3.refs_0_ = bf16[128,128]{1,0:T(8,128)(2,1)S(1)} collective-permute-done((bf16[128,128]{1,0:T(8,128)(2,1)S(1)}, bf16[128,128]{1,0:T(8,128)(2,1)S(1)}, u32[]{:S(2)}, u32[]{:S(2)}) %collective-permute-start.3) | collective-permute-done | bytes 32800 | tf_op jit(solution)/shard_map/ppermute | solution.py:442
  8.9 0.6 %shard_map.69 = (bf16[18,128,128]{2,1,0:T(8,128)(2,1)S(1)}, bf16[4,16,2048]{2,1,0:T(8,128)(2,1)S(1)}) custom-call(bf16[128,128]{1,0:T(8,128)(2,1)S(1)} %collective-permute-done.3.refs_0_, bf16[16,384,512]{2,1,0:T(8,128)(2,1)S(1)} %get-tuple-element.41.refs_1_.refs_0_, ...), custom_call_target="tpu_custom_call", output_to_operand_aliasing={{0}: (3, {})} | custom-call | tf_op jit(solution)/shard_map/pallas_call | solution.py:420
  9.5 2.7 %collective-permute-done.1.got_far = bf16[4,128,128]{2,1,0:T(8,128)(2,1)S(1)} collective-permute-done((bf16[4,128,128]{2,1,0:T(8,128)(2,1)S(1)}, bf16[4,128,128]{2,1,0:T(8,128)(2,1)S(1)}, u32[]{:S(2)}, u32[]{:S(2)}) %collective-permute-start.1) | collective-permute-done | bytes 131104 | tf_op jit(solution)/shard_map/ppermute | solution.py:442
  12.2 0.0 collective-permute-done.got_near
  12.2 0.3 %shard_map.70 = (bf16[32,128,128]{2,1,0:T(8,128)(2,1)S(1)}, bf16[18,128,128]{2,1,0:T(8,128)(2,1)S(1)}, bf16[128,128]{1,0:T(8,128)(2,1)S(1)}) custom-call(s32[9,16]{1,0:T(8,128)S(4)} %get-tuple-element.27.nbr_ref, bf16[5,128,128]{2,1,0:T(8,128)(2,1)S(1)} %collective-permute-done.got_near, ...), custom_call_target="tpu_custom_call", output_to_operand_aliasing={{0}: (4, {}), {1}: (5, {})} | custom-call | tf_op jit(solution)/shard_map/pallas_call | solution.py:341
  12.5 1.8 %collective-permute-start.4 = (bf16[128,128]{1,0:T(8,128)(2,1)S(1)}, bf16[128,128]{1,0:T(8,128)(2,1)S(1)}, u32[]{:S(2)}, u32[]{:S(2)}) collective-permute-start(bf16[128,128]{1,0:T(8,128)(2,1)S(1)} %get-tuple-element.44), channel_id=1, source_target_pairs={{0,1},{1,0},{2,3},{3,2},{4,8},{5,9},{6,10},{7,11},{8,4},{9,5},{10,... | collective-permute-start | bytes 98312 | tf_op jit(solution)/shard_map/ppermute | solution.py:442
  14.3 0.8 %shard_map.71.refs_2_.refs_3_ = bf16[18,128,128]{2,1,0:T(8,128)(2,1)S(1)} custom-call(s32[9,16]{1,0:T(8,128)S(4)} %get-tuple-element.27.nbr_ref, bf16[32,128,128]{2,1,0:T(8,128)(2,1)S(1)} %get-tuple-element.45.wide_ref, bf16[16,9,128,128]{3,2,1,0:T(8,128)(2,1)S(1)} %bitcast.10, ...), custom_call_target="tpu_custom_call", output_to_operand_aliasing={{}: (3, {})} | custom-call | tf_op jit(solution)/shard_map/pallas_call | solution.py:356
  15.1 0.8 %shard_map.72.refs_4_ = bf16[4,16,2048]{2,1,0:T(8,128)(2,1)S(1)} custom-call(bf16[16,384,512]{2,1,0:T(8,128)(2,1)S(1)} %get-tuple-element.41.refs_1_.refs_0_, bf16[8,16,8192]{2,1,0:T(8,128)(2,1)S(1)} %get-tuple-element.29.refs_0_.refs_2_.refs_1_, bf16[18,128,128]{2,1,0:T(8,128)(2,1)S(1)} %shard_map.71.refs_2_.refs_3_, ...), custom_call_target="tpu_custom_call", output_to_operand_aliasing={{}: (3, {})} | custom-call | tf_op jit(solution)/shard_map/pallas_call | solution.py:420
  15.9 0.6 %collective-permute-done.4.refs_0_ = bf16[128,128]{1,0:T(8,128)(2,1)S(1)} collective-permute-done((bf16[128,128]{1,0:T(8,128)(2,1)S(1)}, bf16[128,128]{1,0:T(8,128)(2,1)S(1)}, u32[]{:S(2)}, u32[]{:S(2)}) %collective-permute-start.4) | collective-permute-done | bytes 32800 | tf_op jit(solution)/shard_map/ppermute | solution.py:442
  16.5 0.2 shard_map.73
  16.8 1.8 %collective-permute-start.5 = (bf16[16,2048]{1,0:T(8,128)(2,1)S(1)}, bf16[16,2048]{1,0:T(8,128)(2,1)S(1)}, u32[]{:S(2)}, u32[]{:S(2)}) collective-permute-start(bf16[16,2048]{1,0:T(8,128)(2,1)S(1)} %get-tuple-element.49), channel_id=1, source_target_pairs={{0,1},{1,2},{2,3},{3,0},{4,5},{5,6},{6,7},{7,4},{8,9},{9,10},{10,1... | collective-permute-start | bytes 196616 | tf_op jit(solution)/shard_map/ppermute | solution.py:477
  18.6 2.1 %collective-permute-start.7 = (bf16[16,2048]{1,0:T(8,128)(2,1)S(1)}, bf16[16,2048]{1,0:T(8,128)(2,1)S(1)}, u32[]{:S(2)}, u32[]{:S(2)}) collective-permute-start(bf16[16,2048]{1,0:T(8,128)(2,1)S(1)} %get-tuple-element.50), channel_id=1, source_target_pairs={{0,3},{1,0},{2,1},{3,2},{4,7},{5,4},{6,5},{7,6},{8,11},{9,8},{10,9... | collective-permute-start | bytes 196616 | tf_op jit(solution)/shard_map/ppermute | solution.py:477
  20.7 0.9 %collective-permute-start.6 = (bf16[16,2048]{1,0:T(8,128)(2,1)S(1)}, bf16[16,2048]{1,0:T(8,128)(2,1)S(1)}, u32[]{:S(2)}, u32[]{:S(2)}) collective-permute-start(bf16[16,2048]{1,0:T(8,128)(2,1)S(1)} %get-tuple-element.51), channel_id=1, source_target_pairs={{0,2},{1,3},{2,0},{3,1},{4,6},{5,7},{6,4},{7,5},{8,10},{9,11},{10,... | collective-permute-start | bytes 196616 | tf_op jit(solution)/shard_map/ppermute | solution.py:477
  21.6 1.4 %collective-permute-done.5 = bf16[16,2048]{1,0:T(8,128)(2,1)S(1)} collective-permute-done((bf16[16,2048]{1,0:T(8,128)(2,1)S(1)}, bf16[16,2048]{1,0:T(8,128)(2,1)S(1)}, u32[]{:S(2)}, u32[]{:S(2)}) %collective-permute-start.5) | collective-permute-done | bytes 65568 | tf_op jit(solution)/shard_map/ppermute | solution.py:477
  23.0 1.8 %collective-permute-done.7 = bf16[16,2048]{1,0:T(8,128)(2,1)S(1)} collective-permute-done((bf16[16,2048]{1,0:T(8,128)(2,1)S(1)}, bf16[16,2048]{1,0:T(8,128)(2,1)S(1)}, u32[]{:S(2)}, u32[]{:S(2)}) %collective-permute-start.7) | collective-permute-done | bytes 65568 | tf_op jit(solution)/shard_map/ppermute | solution.py:477
  24.8 3.0 %collective-permute-done.6 = bf16[16,2048]{1,0:T(8,128)(2,1)S(1)} collective-permute-done((bf16[16,2048]{1,0:T(8,128)(2,1)S(1)}, bf16[16,2048]{1,0:T(8,128)(2,1)S(1)}, u32[]{:S(2)}, u32[]{:S(2)}) %collective-permute-start.6) | collective-permute-done | bytes 65568 | tf_op jit(solution)/shard_map/ppermute | solution.py:477
  27.9 0.7 %fusion.2 = f32[16,2048]{1,0:T(8,128)} fusion(bf16[16,2048]{1,0:T(8,128)(2,1)S(1)} %collective-permute-done.7, bf16[16,2048]{1,0:T(8,128)(2,1)S(1)} %collective-permute-done.6, bf16[16,2048]{1,0:T(8,128)(2,1)S(1)} %collective-permute-done.5, bf16[4,16,2048]{2,1,0:T(8,128)(2,1)S(1)} %get-tuple-element.48), kind=kLoop, calls=%fused_computation.3 | loop fusion | flops 262144 | bytes 393216 | tf_op jit(solution)/shard_map/div | solution.py:479
  (2 shorter events, 0.0 us)
Async XLA Ops:
  2.9 4.4 %slice-start = ((s8[4718592]{0:T(1024)(128)(4,1)}), s8[4194304]{0:T(1024)(128)(4,1)S(1)}, s32[]{:S(2)}) async-start(s8[4718592]{0:T(1024)(128)(4,1)} %bitcast.9), calls=%async_computation | async-start | bytes 8388608
  3.0 4.4 %slice-start.1 = ((s8[4718592]{0:T(1024)(128)(4,1)}), s8[524288]{0:T(1024)(128)(4,1)S(1)}, s32[]{:S(2)}) async-start(s8[4718592]{0:T(1024)(128)(4,1)} %bitcast.9), calls=%async_computation.1 | async-start | bytes 1048576
  4.1 3.3 %collective-permute-start.2 = (bf16[9,128,128]{2,1,0:T(8,128)(2,1)S(1)}, bf16[9,128,128]{2,1,0:T(8,128)(2,1)S(1)}, u32[]{:S(2)}, u32[]{:S(2)}) collective-permute-start(bf16[9,128,128]{2,1,0:T(8,128)(2,1)S(1)} %get-tuple-element.38.own_a), channel_id=1, source_target_pairs={{0,4},{1,5},{2,6},{3,7},{4,0},{5,1},{6,2},{7,3},{8,12},{9,13},{10,... | collective-permute-start | bytes 884744 | tf_op jit(solution)/shard_map/ppermute | solution.py:442
  4.6 7.6 %collective-permute-start = (bf16[5,128,128]{2,1,0:T(8,128)(2,1)S(1)}, bf16[5,128,128]{2,1,0:T(8,128)(2,1)S(1)}, u32[]{:S(2)}, u32[]{:S(2)}) collective-permute-start(bf16[5,128,128]{2,1,0:T(8,128)(2,1)S(1)} %get-tuple-element.28.own_near), channel_id=1, source_target_pairs={{0,1},{1,0},{2,3},{3,2},{4,8},{5,9},{6,10},{7,11},{8,4},{9,5},{10,... | collective-permute-start | bytes 491528 | tf_op jit(solution)/shard_map/ppermute | solution.py:442
  7.2 5.0 %collective-permute-start.1 = (bf16[4,128,128]{2,1,0:T(8,128)(2,1)S(1)}, bf16[4,128,128]{2,1,0:T(8,128)(2,1)S(1)}, u32[]{:S(2)}, u32[]{:S(2)}) collective-permute-start(bf16[4,128,128]{2,1,0:T(8,128)(2,1)S(1)} %get-tuple-element.35.own_far), channel_id=1, source_target_pairs={{0,1},{1,0},{2,3},{3,2},{4,8},{5,9},{6,10},{7,11},{8,4},{9,5},{10,... | collective-permute-start | bytes 393224 | tf_op jit(solution)/shard_map/ppermute | solution.py:442
  7.7 1.3 %collective-permute-start.3 = (bf16[128,128]{1,0:T(8,128)(2,1)S(1)}, bf16[128,128]{1,0:T(8,128)(2,1)S(1)}, u32[]{:S(2)}, u32[]{:S(2)}) collective-permute-start(bf16[128,128]{1,0:T(8,128)(2,1)S(1)} %get-tuple-element.40), channel_id=1, source_target_pairs={{0,4},{1,5},{2,6},{3,7},{4,0},{5,1},{6,2},{7,3},{8,12},{9,13},{10,... | collective-permute-start | bytes 98312 | tf_op jit(solution)/shard_map/ppermute | solution.py:442
  12.5 4.0 %collective-permute-start.4 = (bf16[128,128]{1,0:T(8,128)(2,1)S(1)}, bf16[128,128]{1,0:T(8,128)(2,1)S(1)}, u32[]{:S(2)}, u32[]{:S(2)}) collective-permute-start(bf16[128,128]{1,0:T(8,128)(2,1)S(1)} %get-tuple-element.44), channel_id=1, source_target_pairs={{0,1},{1,0},{2,3},{3,2},{4,8},{5,9},{6,10},{7,11},{8,4},{9,5},{10,... | collective-permute-start | bytes 98312 | tf_op jit(solution)/shard_map/ppermute | solution.py:442
  16.8 6.2 %collective-permute-start.5 = (bf16[16,2048]{1,0:T(8,128)(2,1)S(1)}, bf16[16,2048]{1,0:T(8,128)(2,1)S(1)}, u32[]{:S(2)}, u32[]{:S(2)}) collective-permute-start(bf16[16,2048]{1,0:T(8,128)(2,1)S(1)} %get-tuple-element.49), channel_id=1, source_target_pairs={{0,1},{1,2},{2,3},{3,0},{4,5},{5,6},{6,7},{7,4},{8,9},{9,10},{10,1... | collective-permute-start | bytes 196616 | tf_op jit(solution)/shard_map/ppermute | solution.py:477
  18.6 6.2 %collective-permute-start.7 = (bf16[16,2048]{1,0:T(8,128)(2,1)S(1)}, bf16[16,2048]{1,0:T(8,128)(2,1)S(1)}, u32[]{:S(2)}, u32[]{:S(2)}) collective-permute-start(bf16[16,2048]{1,0:T(8,128)(2,1)S(1)} %get-tuple-element.50), channel_id=1, source_target_pairs={{0,3},{1,0},{2,1},{3,2},{4,7},{5,4},{6,5},{7,6},{8,11},{9,8},{10,9... | collective-permute-start | bytes 196616 | tf_op jit(solution)/shard_map/ppermute | solution.py:477
  20.7 7.2 %collective-permute-start.6 = (bf16[16,2048]{1,0:T(8,128)(2,1)S(1)}, bf16[16,2048]{1,0:T(8,128)(2,1)S(1)}, u32[]{:S(2)}, u32[]{:S(2)}) collective-permute-start(bf16[16,2048]{1,0:T(8,128)(2,1)S(1)} %get-tuple-element.51), channel_id=1, source_target_pairs={{0,2},{1,3},{2,0},{3,1},{4,6},{5,7},{6,4},{7,5},{8,10},{9,11},{10,... | collective-permute-start | bytes 196616 | tf_op jit(solution)/shard_map/ppermute | solution.py:477

commit v6 on v5

--- a/solution.py
+++ b/solution.py
@@ -16,7 +16,7 @@
 REACH = 2 * HI + 32
 F32 = jnp.float32
 BF16 = jnp.bfloat16
-NEAR = 5
+NEAR = 4
 VMEM = pltpu.VMEM
 ANY = pl.BlockSpec(memory_space=pl.ANY)
 IN_VMEM = pl.BlockSpec(memory_space=pltpu.VMEM)
@@ -44,17 +44,6 @@
         compiler_params=pltpu.CompilerParams(vmem_limit_bytes=16 * 1024 * 1024),
         cost_estimate=pl.CostEstimate(flops=0, bytes_accessed=0, transcendentals=0),
     )
-
-
-def groups(steps, unroll, body):
-    unroll = unroll if steps % unroll == 0 else 1
-
-    def group(g, carry):
-        for j in range(unroll):
-            body(g * unroll + j)
-        return carry
-
-    lax.fori_loop(0, steps // unroll, group, 0)
 
 
 def build_table(local, weight):
@@ -305,19 +294,73 @@
     edge_ref[...] = edge
 
 
-def rest_kernel(early, steps, unroll, nbr_ref, wide_ref, tiles_ref, smooth_in, smooth_ref):
+def back_chunk(smooth_ref, table_ref, anom_ref, out_ref, c):
+    shares = out_ref.shape[0]
+    per = table_ref.shape[0] // shares
+    lhs = jnp.concatenate([smooth_ref[c], smooth_ref[c + 1], smooth_ref[c + 2]], axis=1)
+    returned = jnp.dot(lhs, table_ref[c], preferred_element_type=F32)
+    here = pl.ds(pl.multiple_of(c * CHUNK, CHUNK), CHUNK)
+    anom = anom_ref[:, :, here].astype(F32)
+    value = jnp.sum(anom * returned.reshape(anom.shape), axis=0)
+    place = lax.div(c, per) - lax.axis_index("mem")
+    place = jnp.where(place < 0, place + shares, place)
+    lane = pl.multiple_of(lax.rem(c, per) * CHUNK, CHUNK)
+    out_ref[place, :, pl.ds(lane, CHUNK)] = value.astype(BF16)
+
+
+def early_kernel(
+    steps, nbr_ref, wide_ref, tiles_ref, table_ref, anom_ref, smooth_in, smooth_ref, out_ref
+):
     blocks = tiles_ref.shape[0]
     flip = is_flipped()
-    if early:
-        start = jnp.where(flip, 1, blocks - 1 - steps)
-    else:
-        start = jnp.where(flip, blocks - 1 - steps, 1)
-
-    def body(i):
-        b = start + i
-        smooth_ref[b + 1] = convolve(wide_ref, tiles_ref, nbr_ref, b)
-
-    groups(steps, unroll, body)
+    start = jnp.where(flip, 1, blocks - 1 - steps)
+    for i in range(steps):
+        smooth_ref[start + i + 1] = convolve(wide_ref, tiles_ref, nbr_ref, start + i)
+    start = jnp.where(flip, 1, blocks - steps)
+    for i in range(steps - 1):
+        back_chunk(smooth_ref, table_ref, anom_ref, out_ref, start + i)
+
+
+def late_kernel(
+    steps,
+    nbr_ref,
+    halo_ref,
+    wide_ref,
+    tiles_ref,
+    table_ref,
+    anom_ref,
+    smooth_in,
+    out_in,
+    smooth_ref,
+    out_ref,
+    main_ref,
+):
+    blocks = tiles_ref.shape[0]
+    flip = is_flipped()
+    start = jnp.where(flip, blocks - 1 - steps, 1)
+    for i in range(steps):
+        smooth_ref[start + i + 1] = convolve(wide_ref, tiles_ref, nbr_ref, start + i)
+    smooth_ref[jnp.where(flip, 0, blocks + 1)] = halo_ref[...]
+    back_chunk(smooth_ref, table_ref, anom_ref, out_ref, jnp.where(flip, 0, blocks - 1))
+    start = jnp.where(flip, blocks - 2 - steps, 1)
+    for i in range(steps + 1):
+        back_chunk(smooth_ref, table_ref, anom_ref, out_ref, start + i)
+    width = main_ref.shape[1]
+    here = pl.ds(pl.multiple_of(jnp.where(flip, 0, CHUNK), CHUNK), width)
+    main_ref[...] = out_ref[out_ref.shape[0] // 2, :, here]
+
+
+def last_kernel(
+    halo_ref, table_ref, anom_ref, smooth_in, out_in, smooth_ref, out_ref, edge_ref
+):
+    blocks = table_ref.shape[0]
+    flip = is_flipped()
+    halo = halo_ref[...]
+    smooth_ref[jnp.where(flip, blocks + 1, 0)] = jnp.where(is_present(), halo, jnp.zeros_like(halo))
+    back_chunk(smooth_ref, table_ref, anom_ref, out_ref, jnp.where(flip, blocks - 1, 0))
+    shares, _, columns = out_ref.shape
+    here = pl.ds(pl.multiple_of(jnp.where(flip, columns - CHUNK, 0), CHUNK), CHUNK)
+    edge_ref[...] = out_ref[shares // 2, :, here]
 
 
 def edge_early_call(neighbours, own_a, own_near, own_far, got_a, tiles):
@@ -352,79 +395,46 @@
     )(neighbours, got_near, got_far, tiles, wide, smooth)
 
 
-def rest_call(early, steps, unroll, neighbours, wide, tiles, smooth):
-    return call(
-        functools.partial(rest_kernel, early, steps, unroll),
-        [IN_SMEM] + [IN_VMEM] * 3,
-        [IN_VMEM],
-        [VMEM(smooth.shape, BF16)],
+def early_call(steps, shares, neighbours, wide, tiles, table, anom, smooth):
+    _, fields, columns = anom.shape
+    return call(
+        functools.partial(early_kernel, steps),
+        [IN_SMEM] + [IN_VMEM] * 5,
+        [IN_VMEM] * 2,
+        [VMEM(smooth.shape, BF16), VMEM((shares, fields, columns // shares), BF16)],
         [],
-        {3: 0},
-    )(neighbours, wide, tiles, smooth)[0]
-
-
-def back_kernel(part, steps, unroll, per, *refs):
-    if part == 0:
-        got_ref, table_ref, anom_ref, _, smooth_ref, out_ref = refs
-    elif part == 1:
-        table_ref, anom_ref, smooth_ref, _, out_ref = refs
-    else:
-        got_ref, table_ref, anom_ref, _, _, smooth_ref, out_ref = refs
-    flip = is_flipped()
-    blocks = table_ref.shape[0]
-    shares = out_ref.shape[0]
-    if part == 0:
-        smooth_ref[jnp.where(flip, 0, blocks + 1)] = got_ref[...]
-        start = jnp.where(flip, 0, blocks - steps)
-    elif part == 1:
-        start = jnp.where(flip, blocks - 1 - steps, 1)
-    else:
-        got = got_ref[...]
-        present = is_present()
-        smooth_ref[jnp.where(flip, blocks + 1, 0)] = jnp.where(present, got, jnp.zeros_like(got))
-        start = jnp.where(flip, blocks - 1, 0)
-
-    def body(i):
-        c = start + i
-        lhs = jnp.concatenate([smooth_ref[c], smooth_ref[c + 1], smooth_ref[c + 2]], axis=1)
-        returned = jnp.dot(lhs, table_ref[c], preferred_element_type=F32)
-        here = pl.ds(pl.multiple_of(c * CHUNK, CHUNK), CHUNK)
-        anom = anom_ref[:, :, here].astype(F32)
-        value = jnp.sum(anom * returned.reshape(anom.shape), axis=0)
-        lane = pl.multiple_of(lax.rem(c, per) * CHUNK, CHUNK)
-        place = lax.div(c, per) - lax.axis_index("mem")
-        place = jnp.where(place < 0, place + shares, place)
-        out_ref[place, :, pl.ds(lane, CHUNK)] = value.astype(BF16)
-
-    groups(steps, unroll, body)
-
-
-def back_call(part, steps, unroll, shares, got, table, anom, smooth, out=None):
-    chunks, fields = table.shape[0], anom.shape[1]
-    per = chunks // shares
-    operands = ([] if part == 1 else [got]) + [table, anom, smooth]
-    in_specs = [IN_VMEM] * len(operands)
-    out_type = VMEM((shares, fields, per * CHUNK), BF16)
-    if part == 2:
-        out_type = jax.ShapeDtypeStruct(out_type.shape, BF16)
-    smooth_type = VMEM(smooth.shape, BF16)
-    last = len(operands) - 1
-    if part == 0:
-        out_shape, aliases = [smooth_type, out_type], {last: 0}
-    elif part == 1:
-        operands, in_specs = operands + [out], in_specs + [IN_VMEM]
-        out_shape, aliases = [out_type], {last + 1: 0}
-    else:
-        operands, in_specs = operands + [out], in_specs + [IN_VMEM]
-        out_shape, aliases = [smooth_type, out_type], {last: 0, last + 1: 1}
-    return call(
-        functools.partial(back_kernel, part, steps, unroll, per),
-        in_specs,
-        [IN_VMEM] * len(out_shape),
-        out_shape,
+        {5: 0},
+    )(neighbours, wide, tiles, table, anom, smooth)
+
+
+def late_call(steps, neighbours, halo, wide, tiles, table, anom, smooth, out):
+    return call(
+        functools.partial(late_kernel, steps),
+        [IN_SMEM] + [IN_VMEM] * 7,
+        [IN_VMEM] * 3,
+        [
+            VMEM(smooth.shape, BF16),
+            VMEM(out.shape, BF16),
+            jax.ShapeDtypeStruct((out.shape[1], out.shape[2] - CHUNK), BF16),
+        ],
         [],
-        aliases,
-    )(*operands)
+        {6: 0, 7: 1},
+    )(neighbours, halo, wide, tiles, table, anom, smooth, out)
+
+
+def last_call(halo, table, anom, smooth, out):
+    return call(
+        last_kernel,
+        [IN_VMEM] * 5,
+        [IN_VMEM] * 3,
+        [
+            VMEM(smooth.shape, BF16),
+            jax.ShapeDtypeStruct(out.shape, BF16),
+            jax.ShapeDtypeStruct((out.shape[1], CHUNK), BF16),
+        ],
+        [],
+        {3: 0, 4: 1},
+    )(halo, table, anom, smooth, out)
 
 
 def swaps(count, shares):
@@ -442,12 +452,16 @@
     return lax.ppermute(value, ("space", "mem"), pairs)
 
 
+def pass_on(value, shift, shares):
+    return lax.ppermute(value, "mem", [(i, (i + shift) % shares) for i in range(shares)])
+
+
 def shards(increment, anomalies, interp_index, interp_weight, neighbour_blocks, tiles):
     members, _, columns = anomalies.shape
     chunks = columns // CHUNK
     count = lax.axis_size("space")
     shares = lax.axis_size("mem")
-    assert count % 2 == 0 and shares % 2 == 0
+    assert count % 2 == 0 and shares % 2 == 0 and chunks > shares
     inner, outer = swaps(count, shares)
     head = chunks // 2 + 1
     table, own_near, carry, anom, *columns_here, neighbours = spread_first_call(
@@ -464,17 +478,26 @@
         neighbours, own_a, own_near, own_far, got_a, tiles
     )
     halo_a = swap(edge_a, inner)
-    smooth = rest_call(True, early, early, neighbours, wide, tiles, smooth)
-    smooth, out = back_call(0, early, early, shares, halo_a, table, anom, smooth)
+    smooth, out = early_call(early, shares, neighbours, wide, tiles, table, anom, smooth)
     wide, smooth, edge_b = edge_late_call(neighbours, got_near, got_far, tiles, wide, smooth)
     halo_b = swap(edge_b, outer)
-    smooth = rest_call(False, head - 1, head - 1, neighbours, wide, tiles, smooth)
-    (out,) = back_call(1, head, head, shares, None, table, anom, smooth, out)
-    _, pieces = back_call(2, 1, 1, shares, halo_b, table, anom, smooth, out)
+    smooth, out, main = late_call(
+        head - 1, neighbours, halo_a, wide, tiles, table, anom, smooth, out
+    )
+    half = shares // 2
+    main = pass_on(main, half, shares)
+    _, pieces, edge = last_call(halo_b, table, anom, smooth, out)
     total = pieces[0].astype(F32)
     for shift in range(1, shares):
-        pairs = [(i, (i + shift) % shares) for i in range(shares)]
-        got = lax.ppermute(pieces[shift], "mem", pairs)
+        piece = edge if shift == half else pieces[shift]
+        got = pass_on(piece, shift, shares)
+        if shift == half:
+            flip = is_flipped()
+            got = jnp.where(
+                flip,
+                jnp.concatenate([main, got], axis=1),
+                jnp.concatenate([got, main], axis=1),
+            )
         total = total + got.astype(F32)
     return total / (members * shares - 1)
 

time: 29.1 us -> 29 us (level)
  starting transfers between devices: 10 us -> 12 us
  waiting for transfers between devices: 10.1 us -> 8.3 us
    ppermute x3 -> x4, waiting for transfers between devices: 6.24 us -> 4.26 us  [pass_on(): lax.ppermute(value, 'mem', [(i, (i + shift) % shares) for i in range(shar...]
    ppermute x3 -> x4, starting transfers between devices: 4.85 us -> 6.82 us  [pass_on(): lax.ppermute(value, 'mem', [(i, (i + shift) % shares) for i in range(shar...]
    pallas_call x5 -> x3, Pallas kernels: 2.99 us -> 2.81 us  [the longest x1 1.6 us: late_call(): call(functools.partial(late_kernel, steps), [IN_SMEM] + [IN_VMEM] * 7, [I...]
  transfers between devices with their start and end apart: 8 -> 9, of which waited for: 6 -> 3; matrix products, arithmetic and copies ran while one was open for 0% -> 0% of each run, Pallas kernels for 11% -> 11%
where the time goes in v6:
time: 29 us; the launch traced here: 28.5 us
  starting transfers between devices  12 us (41%)
  waiting for transfers between devices  8.3 us (29%)
  Pallas kernels  7.34 us (25%)
  other arithmetic  0.7 us (2%)
    ppermute x4, starting transfers between devices, pass_on(): lax.ppermute(value, 'mem', [(i, (i + shift) % shares) for i in range(shar...  6.82 us
    ppermute x5, starting transfers between devices, swap(): return lax.ppermute(value, ('space', 'mem'), pairs)  5.18 us
    ppermute x4, waiting for transfers between devices, pass_on(): lax.ppermute(value, 'mem', [(i, (i + shift) % shares) for i in range(shar...  4.26 us
    ppermute x5, waiting for transfers between devices, swap(): return lax.ppermute(value, ('space', 'mem'), pairs)  4.04 us
    pallas_call x1, Pallas kernels, spread_first_call(): call(functools.partial(spread_kernel, steps, 0, chunks), [ANY] * 5, [IN_V...  2.03 us
    pallas_call x2, Pallas kernels, spread_more_call(): call(functools.partial(spread_kernel, steps, done, chunks), [IN_VMEM] * 6...  1.89 us
    pallas_call x1, Pallas kernels, late_call(): call(functools.partial(late_kernel, steps), [IN_SMEM] + [IN_VMEM] * 7, [I...  1.6 us
    pallas_call x1, Pallas kernels, early_call(): call(functools.partial(early_kernel, steps), [IN_SMEM] + [IN_VMEM] * 5, [...  0.98 us
  transfers between devices with their start and end apart: 9, of which 3 were waited for; matrix products, arithmetic and copies ran while one was open for 0% of the time, Pallas kernels for 11%

profile of v6, /device:TPU:0, one launch (start us, length us, event | category | flops | bytes accessed | tf_op | source)
XLA Modules:
  0.0 28.5 jit_solution(17499037717594984099)
XLA Ops:
  0.0 2.0 %shard_map.64 = (bf16[16,384,512]{2,1,0:T(8,128)(2,1)S(1)}, bf16[4,128,128]{2,1,0:T(8,128)(2,1)S(1)}, f32[2,128,128]{2,1,0:T(8,128)S(1)}, bf16[8,16,8192]{2,1,0:...) custom-call(bf16[8,16,8192]{2,1,0:T(8,128)(2,1)} %refs_0_.1, ...), custom_call_target="tpu_custom_call" | custom-call | tf_op jit(solution)/shard_map/pallas_call | solution.py:176
  2.0 0.8 %shard_map.65 = (bf16[16,384,512]{2,1,0:T(8,128)(2,1)S(1)}, bf16[5,128,128]{2,1,0:T(8,128)(2,1)S(1)}, f32[2,128,128]{2,1,0:T(8,128)S(1)}) custom-call(bf16[8,16,8192]{2,1,0:T(8,128)(2,1)S(1)} %get-tuple-element.33.refs_0_.anom_ref, f32[16,8192]{1,0:T(8,128)S(1)} %get-tuple-element.34.refs_1_, ...), custom_call_target="tpu_custom_call", output_to_operand_aliasing={{0}: (5, {})} | custom-call | tf_op jit(solution)/shard_map/pallas_call | solution.py:208
  2.8 0.0 slice-start
  2.9 0.0 slice-start.1
  2.9 1.1 %shard_map.66 = (bf16[16,384,512]{2,1,0:T(8,128)(2,1)S(1)}, bf16[9,128,128]{2,1,0:T(8,128)(2,1)S(1)}) custom-call(bf16[8,16,8192]{2,1,0:T(8,128)(2,1)S(1)} %get-tuple-element.33.refs_0_.anom_ref, f32[16,8192]{1,0:T(8,128)S(1)} %get-tuple-element.34.refs_1_, s32[3,8192]{1,0:T(4,128)S(1)} %get-tuple-element.35.refs_2_, ...), custom_call_target="tpu_custom_call", output_to_operand_aliasing={{0}: (5, {})} | custom-call | tf_op jit(solution)/shard_map/pallas_call | solution.py:208
  4.0 0.6 %collective-permute-start.2 = (bf16[9,128,128]{2,1,0:T(8,128)(2,1)S(1)}, bf16[9,128,128]{2,1,0:T(8,128)(2,1)S(1)}, u32[]{:S(2)}, u32[]{:S(2)}) collective-permute-start(bf16[9,128,128]{2,1,0:T(8,128)(2,1)S(1)} %get-tuple-element.42.own_a), channel_id=1, source_target_pairs={{0,4},{1,5},{2,6},{3,7},{4,0},{5,1},{6,2},{7,3},{8,12},{9,13},{10,... | collective-permute-start | bytes 884744 | tf_op jit(solution)/shard_map/ppermute | solution.py:452
  4.5 2.6 %collective-permute-start.1 = (bf16[5,128,128]{2,1,0:T(8,128)(2,1)S(1)}, bf16[5,128,128]{2,1,0:T(8,128)(2,1)S(1)}, u32[]{:S(2)}, u32[]{:S(2)}) collective-permute-start(bf16[5,128,128]{2,1,0:T(8,128)(2,1)S(1)} %get-tuple-element.39.own_far), channel_id=1, source_target_pairs={{0,1},{1,0},{2,3},{3,2},{4,8},{5,9},{6,10},{7,11},{8,4},{9,5},{10,... | collective-permute-start | bytes 491528 | tf_op jit(solution)/shard_map/ppermute | solution.py:452
  7.2 0.1 collective-permute-start
  7.2 0.0 collective-permute-done.2.got_a
  7.2 0.0 slice-done
  7.2 0.0 slice-done.1
  7.3 0.3 %shard_map.67 = (bf16[32,128,128]{2,1,0:T(8,128)(2,1)S(1)}, bf16[18,128,128]{2,1,0:T(8,128)(2,1)S(1)}, bf16[128,128]{1,0:T(8,128)(2,1)S(1)}) custom-call(s32[9,16]{1,0:T(8,128)S(4)} %get-tuple-element.31.nbr_ref, bf16[9,128,128]{2,1,0:T(8,128)(2,1)S(1)} %get-tuple-element.42.own_a, bf16[4,128,128]{2,1,0:T(8,128)(2,1)S(1)} %get-tuple-element.32.own_near, ...), custom_call_target="tpu_custom_call" | custom-call | tf_op jit(solution)/shard_map/pallas_call | solution.py:369
  7.6 0.1 collective-permute-start.4
  7.7 1.0 %shard_map.68 = (bf16[18,128,128]{2,1,0:T(8,128)(2,1)S(1)}, bf16[4,16,2048]{2,1,0:T(8,128)(2,1)S(1)}) custom-call(s32[9,16]{1,0:T(8,128)S(4)} %get-tuple-element.31.nbr_ref, bf16[32,128,128]{2,1,0:T(8,128)(2,1)S(1)} %get-tuple-element.43.wide_ref.wide_in, bf16[16,9,128,128]{3,2,1,0:T(8,128)(2,1)S(1)} %bitcast.8, ...), custom_call_target="tpu_custom_call", output_to_operand_aliasing={{0}: (5, {})} | custom-call | tf_op jit(solution)/shard_map/pallas_call | solution.py:400
  8.6 3.5 %collective-permute-done.got_near = bf16[4,128,128]{2,1,0:T(8,128)(2,1)S(1)} collective-permute-done((bf16[4,128,128]{2,1,0:T(8,128)(2,1)S(1)}, bf16[4,128,128]{2,1,0:T(8,128)(2,1)S(1)}, u32[]{:S(2)}, u32[]{:S(2)}) %collective-permute-start) | collective-permute-done | bytes 131104 | tf_op jit(solution)/shard_map/ppermute | solution.py:452
  12.1 0.0 collective-permute-done.1.got_far
  12.1 0.3 %shard_map.69 = (bf16[32,128,128]{2,1,0:T(8,128)(2,1)S(1)}, bf16[18,128,128]{2,1,0:T(8,128)(2,1)S(1)}, bf16[128,128]{1,0:T(8,128)(2,1)S(1)}) custom-call(s32[9,16]{1,0:T(8,128)S(4)} %get-tuple-element.31.nbr_ref, bf16[4,128,128]{2,1,0:T(8,128)(2,1)S(1)} %collective-permute-done.got_near, ...), custom_call_target="tpu_custom_call", output_to_operand_aliasing={{0}: (4, {}), {1}: (5, {})} | custom-call | tf_op jit(solution)/shard_map/pallas_call | solution.py:384
  12.4 1.8 %collective-permute-start.3 = (bf16[128,128]{1,0:T(8,128)(2,1)S(1)}, bf16[128,128]{1,0:T(8,128)(2,1)S(1)}, u32[]{:S(2)}, u32[]{:S(2)}) collective-permute-start(bf16[128,128]{1,0:T(8,128)(2,1)S(1)} %get-tuple-element.47), channel_id=1, source_target_pairs={{0,1},{1,0},{2,3},{3,2},{4,8},{5,9},{6,10},{7,11},{8,4},{9,5},{10,... | collective-permute-start | bytes 98312 | tf_op jit(solution)/shard_map/ppermute | solution.py:452
  14.3 0.0 collective-permute-done.4.halo_ref
  14.3 1.6 %shard_map.70 = (bf16[18,128,128]{2,1,0:T(8,128)(2,1)S(1)}, bf16[4,16,2048]{2,1,0:T(8,128)(2,1)S(1)}, bf16[16,1536]{1,0:T(8,128)(2,1)S(1)}) custom-call(s32[9,16]{1,0:T(8,128)S(4)} %get-tuple-element.31.nbr_ref, bf16[128,128]{1,0:T(8,128)(2,1)S(1)} %collective-permute-done.4.halo_ref, ...), custom_call_target="tpu_custom_call", output_to_operand_aliasing={{0}: (6, {}), {1}: (7, {})} | custom-call | tf_op jit(solution)/shard_map/pallas_call | solution.py:411
  15.9 0.5 %collective-permute-done.3.halo_ref = bf16[128,128]{1,0:T(8,128)(2,1)S(1)} collective-permute-done((bf16[128,128]{1,0:T(8,128)(2,1)S(1)}, bf16[128,128]{1,0:T(8,128)(2,1)S(1)}, u32[]{:S(2)}, u32[]{:S(2)}) %collective-permute-start.3) | collective-permute-done | bytes 32800 | tf_op jit(solution)/shard_map/ppermute | solution.py:452
  16.4 0.2 shard_map.71
  16.7 1.8 %collective-permute-start.5 = (bf16[16,2048]{1,0:T(8,128)(2,1)S(1)}, bf16[16,2048]{1,0:T(8,128)(2,1)S(1)}, u32[]{:S(2)}, u32[]{:S(2)}) collective-permute-start(bf16[16,2048]{1,0:T(8,128)(2,1)S(1)} %get-tuple-element.57), channel_id=1, source_target_pairs={{0,1},{1,2},{2,3},{3,0},{4,5},{5,6},{6,7},{7,4},{8,9},{9,10},{10,1... | collective-permute-start | bytes 196616 | tf_op jit(solution)/shard_map/ppermute | solution.py:456
  18.5 2.1 %collective-permute-start.8 = (bf16[16,2048]{1,0:T(8,128)(2,1)S(1)}, bf16[16,2048]{1,0:T(8,128)(2,1)S(1)}, u32[]{:S(2)}, u32[]{:S(2)}) collective-permute-start(bf16[16,2048]{1,0:T(8,128)(2,1)S(1)} %get-tuple-element.58), channel_id=1, source_target_pairs={{0,3},{1,0},{2,1},{3,2},{4,7},{5,4},{6,5},{7,6},{8,11},{9,8},{10,9... | collective-permute-start | bytes 196616 | tf_op jit(solution)/shard_map/ppermute | solution.py:456
  20.6 1.0 %collective-permute-start.6 = (bf16[16,1536]{1,0:T(8,128)(2,1)S(1)}, bf16[16,1536]{1,0:T(8,128)(2,1)S(1)}, u32[]{:S(2)}, u32[]{:S(2)}) collective-permute-start(bf16[16,1536]{1,0:T(8,128)(2,1)S(1)} %get-tuple-element.55), channel_id=1, source_target_pairs={{0,2},{1,3},{2,0},{3,1},{4,6},{5,7},{6,4},{7,5},{8,10},{9,11},{10,... | collective-permute-start | bytes 147464 | tf_op jit(solution)/shard_map/ppermute | solution.py:456
  21.5 2.0 %collective-permute-start.7 = (bf16[16,512]{1,0:T(8,128)(2,1)S(1)}, bf16[16,512]{1,0:T(8,128)(2,1)S(1)}, u32[]{:S(2)}, u32[]{:S(2)}) collective-permute-start(bf16[16,512]{1,0:T(8,128)(2,1)S(1)} %get-tuple-element.56), channel_id=1, source_target_pairs={{0,2},{1,3},{2,0},{3,1},{4,6},{5,7},{6,4},{7,5},{8,10},{9,11},{10,... | collective-permute-start | bytes 49160 | tf_op jit(solution)/shard_map/ppermute | solution.py:456
  23.5 4.3 %collective-permute-done.7 = bf16[16,512]{1,0:T(8,128)(2,1)S(1)} collective-permute-done((bf16[16,512]{1,0:T(8,128)(2,1)S(1)}, bf16[16,512]{1,0:T(8,128)(2,1)S(1)}, u32[]{:S(2)}, u32[]{:S(2)}) %collective-permute-start.7) | collective-permute-done | bytes 16416 | tf_op jit(solution)/shard_map/ppermute | solution.py:456
  27.7 0.0 collective-permute-done.6
  27.8 0.0 collective-permute-done.5
  27.8 0.0 collective-permute-done.8
  27.8 0.7 %fusion.2 = f32[16,2048]{1,0:T(8,128)} fusion(bf16[16,2048]{1,0:T(8,128)(2,1)S(1)} %collective-permute-done.8, bf16[16,2048]{1,0:T(8,128)(2,1)S(1)} %collective-permute-done.5, bf16[16,512]{1,0:T(8,128)(2,1)S(1)} %collective-permute-done.7, bf16[16,1536]{1,0:T(8,128)(2,1)S(1)} %collective-permute-done.6, bf16[4,16,2048]{2,1,0:T(8,128)(2,1)S(1)} %get-tuple-element.54, ...), kind=kLoop, calls=%fused_computation.3 | loop fusion | flops 557056 | bytes 393217 | tf_op jit(solution)/shard_map/div | solution.py:502
  (2 shorter events, 0.0 us)
Async XLA Ops:
  2.8 4.4 %slice-start = ((s8[4718592]{0:T(1024)(128)(4,1)}), s8[4194304]{0:T(1024)(128)(4,1)S(1)}, s32[]{:S(2)}) async-start(s8[4718592]{0:T(1024)(128)(4,1)} %bitcast.7), calls=%async_computation | async-start | bytes 8388608
  2.9 4.4 %slice-start.1 = ((s8[4718592]{0:T(1024)(128)(4,1)}), s8[524288]{0:T(1024)(128)(4,1)S(1)}, s32[]{:S(2)}) async-start(s8[4718592]{0:T(1024)(128)(4,1)} %bitcast.7), calls=%async_computation.1 | async-start | bytes 1048576
  4.0 3.3 %collective-permute-start.2 = (bf16[9,128,128]{2,1,0:T(8,128)(2,1)S(1)}, bf16[9,128,128]{2,1,0:T(8,128)(2,1)S(1)}, u32[]{:S(2)}, u32[]{:S(2)}) collective-permute-start(bf16[9,128,128]{2,1,0:T(8,128)(2,1)S(1)} %get-tuple-element.42.own_a), channel_id=1, source_target_pairs={{0,4},{1,5},{2,6},{3,7},{4,0},{5,1},{6,2},{7,3},{8,12},{9,13},{10,... | collective-permute-start | bytes 884744 | tf_op jit(solution)/shard_map/ppermute | solution.py:452
  4.5 7.6 %collective-permute-start.1 = (bf16[5,128,128]{2,1,0:T(8,128)(2,1)S(1)}, bf16[5,128,128]{2,1,0:T(8,128)(2,1)S(1)}, u32[]{:S(2)}, u32[]{:S(2)}) collective-permute-start(bf16[5,128,128]{2,1,0:T(8,128)(2,1)S(1)} %get-tuple-element.39.own_far), channel_id=1, source_target_pairs={{0,1},{1,0},{2,3},{3,2},{4,8},{5,9},{6,10},{7,11},{8,4},{9,5},{10,... | collective-permute-start | bytes 491528 | tf_op jit(solution)/shard_map/ppermute | solution.py:452
  7.2 5.0 %collective-permute-start = (bf16[4,128,128]{2,1,0:T(8,128)(2,1)S(1)}, bf16[4,128,128]{2,1,0:T(8,128)(2,1)S(1)}, u32[]{:S(2)}, u32[]{:S(2)}) collective-permute-start(bf16[4,128,128]{2,1,0:T(8,128)(2,1)S(1)} %get-tuple-element.32.own_near), channel_id=1, source_target_pairs={{0,1},{1,0},{2,3},{3,2},{4,8},{5,9},{6,10},{7,11},{8,4},{9,5},{10,... | collective-permute-start | bytes 393224 | tf_op jit(solution)/shard_map/ppermute | solution.py:452
  7.6 6.7 %collective-permute-start.4 = (bf16[128,128]{1,0:T(8,128)(2,1)S(1)}, bf16[128,128]{1,0:T(8,128)(2,1)S(1)}, u32[]{:S(2)}, u32[]{:S(2)}) collective-permute-start(bf16[128,128]{1,0:T(8,128)(2,1)S(1)} %get-tuple-element.48), channel_id=1, source_target_pairs={{0,4},{1,5},{2,6},{3,7},{4,0},{5,1},{6,2},{7,3},{8,12},{9,13},{10,... | collective-permute-start | bytes 98312 | tf_op jit(solution)/shard_map/ppermute | solution.py:452
  12.4 4.0 %collective-permute-start.3 = (bf16[128,128]{1,0:T(8,128)(2,1)S(1)}, bf16[128,128]{1,0:T(8,128)(2,1)S(1)}, u32[]{:S(2)}, u32[]{:S(2)}) collective-permute-start(bf16[128,128]{1,0:T(8,128)(2,1)S(1)} %get-tuple-element.47), channel_id=1, source_target_pairs={{0,1},{1,0},{2,3},{3,2},{4,8},{5,9},{6,10},{7,11},{8,4},{9,5},{10,... | collective-permute-start | bytes 98312 | tf_op jit(solution)/shard_map/ppermute | solution.py:452
  16.7 11.1 %collective-permute-start.5 = (bf16[16,2048]{1,0:T(8,128)(2,1)S(1)}, bf16[16,2048]{1,0:T(8,128)(2,1)S(1)}, u32[]{:S(2)}, u32[]{:S(2)}) collective-permute-start(bf16[16,2048]{1,0:T(8,128)(2,1)S(1)} %get-tuple-element.57), channel_id=1, source_target_pairs={{0,1},{1,2},{2,3},{3,0},{4,5},{5,6},{6,7},{7,4},{8,9},{9,10},{10,1... | collective-permute-start | bytes 196616 | tf_op jit(solution)/shard_map/ppermute | solution.py:456
  18.5 9.3 %collective-permute-start.8 = (bf16[16,2048]{1,0:T(8,128)(2,1)S(1)}, bf16[16,2048]{1,0:T(8,128)(2,1)S(1)}, u32[]{:S(2)}, u32[]{:S(2)}) collective-permute-start(bf16[16,2048]{1,0:T(8,128)(2,1)S(1)} %get-tuple-element.58), channel_id=1, source_target_pairs={{0,3},{1,0},{2,1},{3,2},{4,7},{5,4},{6,5},{7,6},{8,11},{9,8},{10,9... | collective-permute-start | bytes 196616 | tf_op jit(solution)/shard_map/ppermute | solution.py:456
  20.6 7.2 %collective-permute-start.6 = (bf16[16,1536]{1,0:T(8,128)(2,1)S(1)}, bf16[16,1536]{1,0:T(8,128)(2,1)S(1)}, u32[]{:S(2)}, u32[]{:S(2)}) collective-permute-start(bf16[16,1536]{1,0:T(8,128)(2,1)S(1)} %get-tuple-element.55), channel_id=1, source_target_pairs={{0,2},{1,3},{2,0},{3,1},{4,6},{5,7},{6,4},{7,5},{8,10},{9,11},{10,... | collective-permute-start | bytes 147464 | tf_op jit(solution)/shard_map/ppermute | solution.py:456
  21.5 6.2 %collective-permute-start.7 = (bf16[16,512]{1,0:T(8,128)(2,1)S(1)}, bf16[16,512]{1,0:T(8,128)(2,1)S(1)}, u32[]{:S(2)}, u32[]{:S(2)}) collective-permute-start(bf16[16,512]{1,0:T(8,128)(2,1)S(1)} %get-tuple-element.56), channel_id=1, source_target_pairs={{0,2},{1,3},{2,0},{3,1},{4,6},{5,7},{6,4},{7,5},{8,10},{9,11},{10,... | collective-permute-start | bytes 49160 | tf_op jit(solution)/shard_map/ppermute | solution.py:456

commit v7 on v6

--- a/solution.py
+++ b/solution.py
@@ -16,7 +16,7 @@
 REACH = 2 * HI + 32
 F32 = jnp.float32
 BF16 = jnp.bfloat16
-NEAR = 4
+NEAR = 5
 VMEM = pltpu.VMEM
 ANY = pl.BlockSpec(memory_space=pl.ANY)
 IN_VMEM = pl.BlockSpec(memory_space=pltpu.VMEM)
@@ -259,35 +259,12 @@
 
 
 def edge_late_kernel(
-    nbr_ref, got_near, got_far, tiles_ref, wide_in, smooth_in, wide_ref, smooth_ref, edge_ref
+    nbr_ref, got_far, tiles_ref, wide_in, smooth_in, wide_ref, smooth_ref, edge_ref
 ):
-    near = got_near.shape[0]
-    half = near + got_far.shape[0]
-    reach = half - 1
+    far = got_far.shape[0]
     blocks = tiles_ref.shape[0]
-    top = blocks + reach
     flip = is_flipped()
-    present = is_present()
-
-    def there(value):
-        return jnp.where(present, value, jnp.zeros_like(value))
-
-    @pl.when(jnp.logical_not(flip))
-    def _():
-        wide_ref[0 : half - near] = there(got_far[...])
-        wide_ref[half - near : reach - 1] = there(got_near[0 : near - 2])
-        both = wide_ref[reach - 1 : reach + 1].astype(F32) + there(got_near[near - 2 :].astype(F32))
-        wide_ref[reach - 1] = there(both[0]).astype(BF16)
-        wide_ref[reach] = both[1].astype(BF16)
-
-    @pl.when(flip)
-    def _():
-        both = wide_ref[top - 1 : top + 1].astype(F32) + there(got_near[0:2].astype(F32))
-        wide_ref[top - 1] = both[0].astype(BF16)
-        wide_ref[top] = there(both[1]).astype(BF16)
-        wide_ref[top + 1 : top - 1 + near] = there(got_near[2:near])
-        wide_ref[top - 1 + near : top + reach] = there(got_far[...])
-
+    wide_ref[pl.ds(jnp.where(flip, wide_ref.shape[0] - far, 0), far)] = there(got_far[...])
     b = jnp.where(flip, blocks - 1, 0)
     edge = convolve(wide_ref, tiles_ref, nbr_ref, b)
     smooth_ref[b + 1] = edge
@@ -308,16 +285,52 @@
     out_ref[place, :, pl.ds(lane, CHUNK)] = value.astype(BF16)
 
 
+def there(value):
+    return jnp.where(is_present(), value, jnp.zeros_like(value))
+
+
 def early_kernel(
-    steps, nbr_ref, wide_ref, tiles_ref, table_ref, anom_ref, smooth_in, smooth_ref, out_ref
+    steps,
+    nbr_ref,
+    got_near,
+    wide_in,
+    tiles_ref,
+    table_ref,
+    anom_ref,
+    smooth_in,
+    wide_ref,
+    smooth_ref,
+    out_ref,
 ):
     blocks = tiles_ref.shape[0]
+    near = got_near.shape[0]
+    half = blocks - steps - 1
+    reach = half - 1
+    top = blocks + reach
     flip = is_flipped()
     start = jnp.where(flip, 1, blocks - 1 - steps)
     for i in range(steps):
         smooth_ref[start + i + 1] = convolve(wide_ref, tiles_ref, nbr_ref, start + i)
-    start = jnp.where(flip, 1, blocks - steps)
-    for i in range(steps - 1):
+
+    @pl.when(jnp.logical_not(flip))
+    def _():
+        wide_ref[half - near : reach - 1] = there(got_near[0 : near - 2])
+        both = wide_ref[reach - 1 : reach + 1].astype(F32) + there(got_near[near - 2 :].astype(F32))
+        wide_ref[reach - 1] = there(both[0]).astype(BF16)
+        wide_ref[reach] = both[1].astype(BF16)
+
+    @pl.when(flip)
+    def _():
+        both = wide_ref[top - 1 : top + 1].astype(F32) + there(got_near[0:2].astype(F32))
+        wide_ref[top - 1] = both[0].astype(BF16)
+        wide_ref[top] = there(both[1]).astype(BF16)
+        wide_ref[top + 1 : top - 1 + near] = there(got_near[2:near])
+
+    start = jnp.where(flip, blocks - half, half - near)
+    for i in range(near):
+        smooth_ref[start + i + 1] = convolve(wide_ref, tiles_ref, nbr_ref, start + i)
+    start = jnp.where(flip, 1, half - near + 1)
+    for i in range(steps - 1 + near):
         back_chunk(smooth_ref, table_ref, anom_ref, out_ref, start + i)
 
 
@@ -340,9 +353,9 @@
     start = jnp.where(flip, blocks - 1 - steps, 1)
     for i in range(steps):
         smooth_ref[start + i + 1] = convolve(wide_ref, tiles_ref, nbr_ref, start + i)
+    start = jnp.where(flip, blocks - 2 - steps, 1)
     smooth_ref[jnp.where(flip, 0, blocks + 1)] = halo_ref[...]
     back_chunk(smooth_ref, table_ref, anom_ref, out_ref, jnp.where(flip, 0, blocks - 1))
-    start = jnp.where(flip, blocks - 2 - steps, 1)
     for i in range(steps + 1):
         back_chunk(smooth_ref, table_ref, anom_ref, out_ref, start + i)
     width = main_ref.shape[1]
@@ -379,11 +392,11 @@
     )(neighbours, own_a, own_near, own_far, got_a, tiles)
 
 
-def edge_late_call(neighbours, got_near, got_far, tiles, wide, smooth):
-    _, rows, _ = got_near.shape
+def edge_late_call(neighbours, got_far, tiles, wide, smooth):
+    _, rows, _ = got_far.shape
     return call(
         edge_late_kernel,
-        [IN_SMEM] + [IN_VMEM] * 5,
+        [IN_SMEM] + [IN_VMEM] * 4,
         [IN_VMEM] * 3,
         [
             VMEM(wide.shape, BF16),
@@ -391,20 +404,24 @@
             jax.ShapeDtypeStruct((rows, BLOCK), BF16),
         ],
         [],
-        {4: 0, 5: 1},
-    )(neighbours, got_near, got_far, tiles, wide, smooth)
-
-
-def early_call(steps, shares, neighbours, wide, tiles, table, anom, smooth):
+        {3: 0, 4: 1},
+    )(neighbours, got_far, tiles, wide, smooth)
+
+
+def early_call(steps, shares, neighbours, got_near, wide, tiles, table, anom, smooth):
     _, fields, columns = anom.shape
     return call(
         functools.partial(early_kernel, steps),
-        [IN_SMEM] + [IN_VMEM] * 5,
-        [IN_VMEM] * 2,
-        [VMEM(smooth.shape, BF16), VMEM((shares, fields, columns // shares), BF16)],
+        [IN_SMEM] + [IN_VMEM] * 6,
+        [IN_VMEM] * 3,
+        [
+            VMEM(wide.shape, BF16),
+            VMEM(smooth.shape, BF16),
+            VMEM((shares, fields, columns // shares), BF16),
+        ],
         [],
-        {5: 0},
-    )(neighbours, wide, tiles, table, anom, smooth)
+        {2: 0, 6: 1},
+    )(neighbours, got_near, wide, tiles, table, anom, smooth)
 
 
 def late_call(steps, neighbours, halo, wide, tiles, table, anom, smooth, out):
@@ -478,11 +495,13 @@
         neighbours, own_a, own_near, own_far, got_a, tiles
     )
     halo_a = swap(edge_a, inner)
-    smooth, out = early_call(early, shares, neighbours, wide, tiles, table, anom, smooth)
-    wide, smooth, edge_b = edge_late_call(neighbours, got_near, got_far, tiles, wide, smooth)
+    wide, smooth, out = early_call(
+        early, shares, neighbours, got_near, wide, tiles, table, anom, smooth
+    )
+    wide, smooth, edge_b = edge_late_call(neighbours, got_far, tiles, wide, smooth)
     halo_b = swap(edge_b, outer)
     smooth, out, main = late_call(
-        head - 1, neighbours, halo_a, wide, tiles, table, anom, smooth, out
+        head - 1 - NEAR, neighbours, halo_a, wide, tiles, table, anom, smooth, out
     )
     half = shares // 2
     main = pass_on(main, half, shares)

time: 29 us -> 29.1 us (level); the launches traced: 28.5 us -> 28.9 us
  starting transfers between devices: 12 us -> 12.5 us
  waiting for transfers between devices: 8.3 us -> 7.95 us
    pallas_call x2, Pallas kernels: 1.28 us -> 2.19 us  [the longest x1 1.93 us: early_call(): call(functools.partial(early_kernel, steps), [IN_SMEM] + [IN_VMEM] * 6, [...]
    pallas_call x1, Pallas kernels: 1.6 us -> 0.87 us  [late_call(): call(functools.partial(late_kernel, steps), [IN_SMEM] + [IN_VMEM] * 7, [I...]
  transfers between devices with their start and end apart: 9 -> 9, of which waited for: 3 -> 3; matrix products, arithmetic and copies ran while one was open for 0% -> 0% of each run, Pallas kernels for 11% -> 12%
where the time goes in v7:
time: 29.1 us; the launch traced here: 28.9 us
  starting transfers between devices  12.5 us (43%)
  waiting for transfers between devices  7.95 us (27%)
  Pallas kernels  7.61 us (26%)
  other arithmetic  0.7 us (2%)
    ppermute x4, starting transfers between devices, pass_on(): lax.ppermute(value, 'mem', [(i, (i + shift) % shares) for i in range(shar...  7.1 us
    ppermute x5, starting transfers between devices, swap(): return lax.ppermute(value, ('space', 'mem'), pairs)  5.45 us
    ppermute x4, waiting for transfers between devices, pass_on(): lax.ppermute(value, 'mem', [(i, (i + shift) % shares) for i in range(shar...  4.13 us
    ppermute x5, waiting for transfers between devices, swap(): return lax.ppermute(value, ('space', 'mem'), pairs)  3.82 us
    pallas_call x1, Pallas kernels, spread_first_call(): call(functools.partial(spread_kernel, steps, 0, chunks), [ANY] * 5, [IN_V...  2.21 us
    pallas_call x1, Pallas kernels, early_call(): call(functools.partial(early_kernel, steps), [IN_SMEM] + [IN_VMEM] * 6, [...  1.93 us
    pallas_call x2, Pallas kernels, spread_more_call(): call(functools.partial(spread_kernel, steps, done, chunks), [IN_VMEM] * 6...  1.81 us
    pallas_call x1, Pallas kernels, late_call(): call(functools.partial(late_kernel, steps), [IN_SMEM] + [IN_VMEM] * 7, [I...  0.87 us
  transfers between devices with their start and end apart: 9, of which 3 were waited for; matrix products, arithmetic and copies ran while one was open for 0% of the time, Pallas kernels for 12%

profile of v7, /device:TPU:0, one launch (start us, length us, event | category | flops | bytes accessed | tf_op | source)
XLA Modules:
  0.0 28.9 jit_solution(14742104390974868445)
XLA Ops:
  0.0 2.2 %shard_map.64 = (bf16[16,384,512]{2,1,0:T(8,128)(2,1)S(1)}, bf16[5,128,128]{2,1,0:T(8,128)(2,1)S(1)}, f32[2,128,128]{2,1,0:T(8,128)S(1)}, bf16[8,16,8192]{2,1,0:...) custom-call(bf16[8,16,8192]{2,1,0:T(8,128)(2,1)} %refs_0_.1, ...), custom_call_target="tpu_custom_call" | custom-call | tf_op jit(solution)/shard_map/pallas_call | solution.py:176
  2.2 0.7 %shard_map.65 = (bf16[16,384,512]{2,1,0:T(8,128)(2,1)S(1)}, bf16[4,128,128]{2,1,0:T(8,128)(2,1)S(1)}, f32[2,128,128]{2,1,0:T(8,128)S(1)}) custom-call(bf16[8,16,8192]{2,1,0:T(8,128)(2,1)S(1)} %get-tuple-element.33.refs_0_.anom_ref, f32[16,8192]{1,0:T(8,128)S(1)} %get-tuple-element.34.refs_1_, ...), custom_call_target="tpu_custom_call", output_to_operand_aliasing={{0}: (5, {})} | custom-call | tf_op jit(solution)/shard_map/pallas_call | solution.py:208
  2.9 0.0 slice-start
  3.0 0.0 slice-start.1
  3.0 1.1 %shard_map.66 = (bf16[16,384,512]{2,1,0:T(8,128)(2,1)S(1)}, bf16[9,128,128]{2,1,0:T(8,128)(2,1)S(1)}) custom-call(bf16[8,16,8192]{2,1,0:T(8,128)(2,1)S(1)} %get-tuple-element.33.refs_0_.anom_ref, f32[16,8192]{1,0:T(8,128)S(1)} %get-tuple-element.34.refs_1_, s32[3,8192]{1,0:T(4,128)S(1)} %get-tuple-element.35.refs_2_, ...), custom_call_target="tpu_custom_call", output_to_operand_aliasing={{0}: (5, {})} | custom-call | tf_op jit(solution)/shard_map/pallas_call | solution.py:208
  4.1 0.6 %collective-permute-start.2 = (bf16[9,128,128]{2,1,0:T(8,128)(2,1)S(1)}, bf16[9,128,128]{2,1,0:T(8,128)(2,1)S(1)}, u32[]{:S(2)}, u32[]{:S(2)}) collective-permute-start(bf16[9,128,128]{2,1,0:T(8,128)(2,1)S(1)} %get-tuple-element.43.own_a), channel_id=1, source_target_pairs={{0,4},{1,5},{2,6},{3,7},{4,0},{5,1},{6,2},{7,3},{8,12},{9,13},{10,... | collective-permute-start | bytes 884744 | tf_op jit(solution)/shard_map/ppermute | solution.py:469
  4.6 2.6 %collective-permute-start.1 = (bf16[5,128,128]{2,1,0:T(8,128)(2,1)S(1)}, bf16[5,128,128]{2,1,0:T(8,128)(2,1)S(1)}, u32[]{:S(2)}, u32[]{:S(2)}) collective-permute-start(bf16[5,128,128]{2,1,0:T(8,128)(2,1)S(1)} %get-tuple-element.40.own_near), channel_id=1, source_target_pairs={{0,1},{1,0},{2,3},{3,2},{4,8},{5,9},{6,10},{7,11},{8,4},{9,5},{10,... | collective-permute-start | bytes 491528 | tf_op jit(solution)/shard_map/ppermute | solution.py:469
  7.2 0.1 collective-permute-start
  7.3 0.0 collective-permute-done.2.got_a
  7.3 0.0 slice-done
  7.3 0.0 slice-done.1
  7.3 0.3 %shard_map.67 = (bf16[32,128,128]{2,1,0:T(8,128)(2,1)S(1)}, bf16[18,128,128]{2,1,0:T(8,128)(2,1)S(1)}, bf16[128,128]{1,0:T(8,128)(2,1)S(1)}) custom-call(s32[9,16]{1,0:T(8,128)S(4)} %get-tuple-element.32.nbr_ref, bf16[9,128,128]{2,1,0:T(8,128)(2,1)S(1)} %get-tuple-element.43.own_a, bf16[5,128,128]{2,1,0:T(8,128)(2,1)S(1)} %get-tuple-element.40.own_near, ...), custom_call_target="tpu_custom_call" | custom-call | tf_op jit(solution)/shard_map/pallas_call | solution.py:382
  7.7 0.1 collective-permute-start.4
  7.7 2.8 %collective-permute-done.1.got_near = bf16[5,128,128]{2,1,0:T(8,128)(2,1)S(1)} collective-permute-done((bf16[5,128,128]{2,1,0:T(8,128)(2,1)S(1)}, bf16[5,128,128]{2,1,0:T(8,128)(2,1)S(1)}, u32[]{:S(2)}, u32[]{:S(2)}) %collective-permute-start.1) | collective-permute-done | bytes 163872 | tf_op jit(solution)/shard_map/ppermute | solution.py:469
  10.5 1.9 %shard_map.68 = (bf16[32,128,128]{2,1,0:T(8,128)(2,1)S(1)}, bf16[18,128,128]{2,1,0:T(8,128)(2,1)S(1)}, bf16[4,16,2048]{2,1,0:T(8,128)(2,1)S(1)}) custom-call(s32[9,16]{1,0:T(8,128)S(4)} %get-tuple-element.32.nbr_ref, bf16[5,128,128]{2,1,0:T(8,128)(2,1)S(1)} %collective-permute-done.1.got_near, ...), custom_call_target="tpu_custom_call", output_to_operand_aliasing={{0}: (2, {}), {1}: (6, {})} | custom-call | tf_op jit(solution)/shard_map/pallas_call | solution.py:413
  12.5 0.0 collective-permute-done.got_far
  12.5 0.3 shard_map.69
  12.8 2.1 %collective-permute-start.3 = (bf16[128,128]{1,0:T(8,128)(2,1)S(1)}, bf16[128,128]{1,0:T(8,128)(2,1)S(1)}, u32[]{:S(2)}, u32[]{:S(2)}) collective-permute-start(bf16[128,128]{1,0:T(8,128)(2,1)S(1)} %get-tuple-element.49), channel_id=1, source_target_pairs={{0,1},{1,0},{2,3},{3,2},{4,8},{5,9},{6,10},{7,11},{8,4},{9,5},{10,... | collective-permute-start | bytes 98312 | tf_op jit(solution)/shard_map/ppermute | solution.py:469
  14.8 0.0 collective-permute-done.4.halo_ref
  14.8 0.9 %shard_map.70 = (bf16[18,128,128]{2,1,0:T(8,128)(2,1)S(1)}, bf16[4,16,2048]{2,1,0:T(8,128)(2,1)S(1)}, bf16[16,1536]{1,0:T(8,128)(2,1)S(1)}) custom-call(s32[9,16]{1,0:T(8,128)S(4)} %get-tuple-element.32.nbr_ref, bf16[128,128]{1,0:T(8,128)(2,1)S(1)} %collective-permute-done.4.halo_ref, ...), custom_call_target="tpu_custom_call", output_to_operand_aliasing={{0}: (6, {}), {1}: (7, {})} | custom-call | tf_op jit(solution)/shard_map/pallas_call | solution.py:428
  15.7 1.0 %collective-permute-done.3.halo_ref = bf16[128,128]{1,0:T(8,128)(2,1)S(1)} collective-permute-done((bf16[128,128]{1,0:T(8,128)(2,1)S(1)}, bf16[128,128]{1,0:T(8,128)(2,1)S(1)}, u32[]{:S(2)}, u32[]{:S(2)}) %collective-permute-start.3) | collective-permute-done | bytes 32800 | tf_op jit(solution)/shard_map/ppermute | solution.py:469
  16.7 0.2 shard_map.71
  17.0 2.1 %collective-permute-start.5 = (bf16[16,2048]{1,0:T(8,128)(2,1)S(1)}, bf16[16,2048]{1,0:T(8,128)(2,1)S(1)}, u32[]{:S(2)}, u32[]{:S(2)}) collective-permute-start(bf16[16,2048]{1,0:T(8,128)(2,1)S(1)} %get-tuple-element.59), channel_id=1, source_target_pairs={{0,1},{1,2},{2,3},{3,0},{4,5},{5,6},{6,7},{7,4},{8,9},{9,10},{10,1... | collective-permute-start | bytes 196616 | tf_op jit(solution)/shard_map/ppermute | solution.py:473
  19.1 2.1 %collective-permute-start.8 = (bf16[16,2048]{1,0:T(8,128)(2,1)S(1)}, bf16[16,2048]{1,0:T(8,128)(2,1)S(1)}, u32[]{:S(2)}, u32[]{:S(2)}) collective-permute-start(bf16[16,2048]{1,0:T(8,128)(2,1)S(1)} %get-tuple-element.60), channel_id=1, source_target_pairs={{0,3},{1,0},{2,1},{3,2},{4,7},{5,4},{6,5},{7,6},{8,11},{9,8},{10,9... | collective-permute-start | bytes 196616 | tf_op jit(solution)/shard_map/ppermute | solution.py:473
  21.2 0.9 %collective-permute-start.6 = (bf16[16,1536]{1,0:T(8,128)(2,1)S(1)}, bf16[16,1536]{1,0:T(8,128)(2,1)S(1)}, u32[]{:S(2)}, u32[]{:S(2)}) collective-permute-start(bf16[16,1536]{1,0:T(8,128)(2,1)S(1)} %get-tuple-element.57), channel_id=1, source_target_pairs={{0,2},{1,3},{2,0},{3,1},{4,6},{5,7},{6,4},{7,5},{8,10},{9,11},{10,... | collective-permute-start | bytes 147464 | tf_op jit(solution)/shard_map/ppermute | solution.py:473
  22.1 2.0 %collective-permute-start.7 = (bf16[16,512]{1,0:T(8,128)(2,1)S(1)}, bf16[16,512]{1,0:T(8,128)(2,1)S(1)}, u32[]{:S(2)}, u32[]{:S(2)}) collective-permute-start(bf16[16,512]{1,0:T(8,128)(2,1)S(1)} %get-tuple-element.58), channel_id=1, source_target_pairs={{0,2},{1,3},{2,0},{3,1},{4,6},{5,7},{6,4},{7,5},{8,10},{9,11},{10,... | collective-permute-start | bytes 49160 | tf_op jit(solution)/shard_map/ppermute | solution.py:473
  24.1 4.1 %collective-permute-done.7 = bf16[16,512]{1,0:T(8,128)(2,1)S(1)} collective-permute-done((bf16[16,512]{1,0:T(8,128)(2,1)S(1)}, bf16[16,512]{1,0:T(8,128)(2,1)S(1)}, u32[]{:S(2)}, u32[]{:S(2)}) %collective-permute-start.7) | collective-permute-done | bytes 16416 | tf_op jit(solution)/shard_map/ppermute | solution.py:473
  28.2 0.0 collective-permute-done.6
  28.2 0.0 collective-permute-done.5
  28.2 0.0 collective-permute-done.8
  28.2 0.7 %fusion.2 = f32[16,2048]{1,0:T(8,128)} fusion(bf16[16,2048]{1,0:T(8,128)(2,1)S(1)} %collective-permute-done.8, bf16[16,2048]{1,0:T(8,128)(2,1)S(1)} %collective-permute-done.5, bf16[16,512]{1,0:T(8,128)(2,1)S(1)} %collective-permute-done.7, bf16[16,1536]{1,0:T(8,128)(2,1)S(1)} %collective-permute-done.6, bf16[4,16,2048]{2,1,0:T(8,128)(2,1)S(1)} %get-tuple-element.56, ...), kind=kLoop, calls=%fused_computation.3 | loop fusion | flops 557056 | bytes 393217 | tf_op jit(solution)/shard_map/div | solution.py:521
  (2 shorter events, 0.0 us)
Async XLA Ops:
  2.9 4.4 %slice-start = ((s8[4718592]{0:T(1024)(128)(4,1)}), s8[4194304]{0:T(1024)(128)(4,1)S(1)}, s32[]{:S(2)}) async-start(s8[4718592]{0:T(1024)(128)(4,1)} %bitcast.7), calls=%async_computation | async-start | bytes 8388608
  3.0 4.4 %slice-start.1 = ((s8[4718592]{0:T(1024)(128)(4,1)}), s8[524288]{0:T(1024)(128)(4,1)S(1)}, s32[]{:S(2)}) async-start(s8[4718592]{0:T(1024)(128)(4,1)} %bitcast.7), calls=%async_computation.1 | async-start | bytes 1048576
  4.1 3.3 %collective-permute-start.2 = (bf16[9,128,128]{2,1,0:T(8,128)(2,1)S(1)}, bf16[9,128,128]{2,1,0:T(8,128)(2,1)S(1)}, u32[]{:S(2)}, u32[]{:S(2)}) collective-permute-start(bf16[9,128,128]{2,1,0:T(8,128)(2,1)S(1)} %get-tuple-element.43.own_a), channel_id=1, source_target_pairs={{0,4},{1,5},{2,6},{3,7},{4,0},{5,1},{6,2},{7,3},{8,12},{9,13},{10,... | collective-permute-start | bytes 884744 | tf_op jit(solution)/shard_map/ppermute | solution.py:469
  4.6 5.9 %collective-permute-start.1 = (bf16[5,128,128]{2,1,0:T(8,128)(2,1)S(1)}, bf16[5,128,128]{2,1,0:T(8,128)(2,1)S(1)}, u32[]{:S(2)}, u32[]{:S(2)}) collective-permute-start(bf16[5,128,128]{2,1,0:T(8,128)(2,1)S(1)} %get-tuple-element.40.own_near), channel_id=1, source_target_pairs={{0,1},{1,0},{2,3},{3,2},{4,8},{5,9},{6,10},{7,11},{8,4},{9,5},{10,... | collective-permute-start | bytes 491528 | tf_op jit(solution)/shard_map/ppermute | solution.py:469
  7.2 5.2 %collective-permute-start = (bf16[4,128,128]{2,1,0:T(8,128)(2,1)S(1)}, bf16[4,128,128]{2,1,0:T(8,128)(2,1)S(1)}, u32[]{:S(2)}, u32[]{:S(2)}) collective-permute-start(bf16[4,128,128]{2,1,0:T(8,128)(2,1)S(1)} %get-tuple-element.39.own_far), channel_id=1, source_target_pairs={{0,1},{1,0},{2,3},{3,2},{4,8},{5,9},{6,10},{7,11},{8,4},{9,5},{10,... | collective-permute-start | bytes 393224 | tf_op jit(solution)/shard_map/ppermute | solution.py:469
  7.7 7.2 %collective-permute-start.4 = (bf16[128,128]{1,0:T(8,128)(2,1)S(1)}, bf16[128,128]{1,0:T(8,128)(2,1)S(1)}, u32[]{:S(2)}, u32[]{:S(2)}) collective-permute-start(bf16[128,128]{1,0:T(8,128)(2,1)S(1)} %get-tuple-element.50), channel_id=1, source_target_pairs={{0,4},{1,5},{2,6},{3,7},{4,0},{5,1},{6,2},{7,3},{8,12},{9,13},{10,... | collective-permute-start | bytes 98312 | tf_op jit(solution)/shard_map/ppermute | solution.py:469
  12.8 4.0 %collective-permute-start.3 = (bf16[128,128]{1,0:T(8,128)(2,1)S(1)}, bf16[128,128]{1,0:T(8,128)(2,1)S(1)}, u32[]{:S(2)}, u32[]{:S(2)}) collective-permute-start(bf16[128,128]{1,0:T(8,128)(2,1)S(1)} %get-tuple-element.49), channel_id=1, source_target_pairs={{0,1},{1,0},{2,3},{3,2},{4,8},{5,9},{6,10},{7,11},{8,4},{9,5},{10,... | collective-permute-start | bytes 98312 | tf_op jit(solution)/shard_map/ppermute | solution.py:469
  17.0 11.2 %collective-permute-start.5 = (bf16[16,2048]{1,0:T(8,128)(2,1)S(1)}, bf16[16,2048]{1,0:T(8,128)(2,1)S(1)}, u32[]{:S(2)}, u32[]{:S(2)}) collective-permute-start(bf16[16,2048]{1,0:T(8,128)(2,1)S(1)} %get-tuple-element.59), channel_id=1, source_target_pairs={{0,1},{1,2},{2,3},{3,0},{4,5},{5,6},{6,7},{7,4},{8,9},{9,10},{10,1... | collective-permute-start | bytes 196616 | tf_op jit(solution)/shard_map/ppermute | solution.py:473
  19.1 9.1 %collective-permute-start.8 = (bf16[16,2048]{1,0:T(8,128)(2,1)S(1)}, bf16[16,2048]{1,0:T(8,128)(2,1)S(1)}, u32[]{:S(2)}, u32[]{:S(2)}) collective-permute-start(bf16[16,2048]{1,0:T(8,128)(2,1)S(1)} %get-tuple-element.60), channel_id=1, source_target_pairs={{0,3},{1,0},{2,1},{3,2},{4,7},{5,4},{6,5},{7,6},{8,11},{9,8},{10,9... | collective-permute-start | bytes 196616 | tf_op jit(solution)/shard_map/ppermute | solution.py:473
  21.2 7.0 %collective-permute-start.6 = (bf16[16,1536]{1,0:T(8,128)(2,1)S(1)}, bf16[16,1536]{1,0:T(8,128)(2,1)S(1)}, u32[]{:S(2)}, u32[]{:S(2)}) collective-permute-start(bf16[16,1536]{1,0:T(8,128)(2,1)S(1)} %get-tuple-element.57), channel_id=1, source_target_pairs={{0,2},{1,3},{2,0},{3,1},{4,6},{5,7},{6,4},{7,5},{8,10},{9,11},{10,... | collective-permute-start | bytes 147464 | tf_op jit(solution)/shard_map/ppermute | solution.py:473
  22.1 6.1 %collective-permute-start.7 = (bf16[16,512]{1,0:T(8,128)(2,1)S(1)}, bf16[16,512]{1,0:T(8,128)(2,1)S(1)}, u32[]{:S(2)}, u32[]{:S(2)}) collective-permute-start(bf16[16,512]{1,0:T(8,128)(2,1)S(1)} %get-tuple-element.58), channel_id=1, source_target_pairs={{0,2},{1,3},{2,0},{3,1},{4,6},{5,7},{6,4},{7,5},{8,10},{9,11},{10,... | collective-permute-start | bytes 49160 | tf_op jit(solution)/shard_map/ppermute | solution.py:473

commit v8 on v7

--- a/solution.py
+++ b/solution.py
@@ -16,7 +16,7 @@
 REACH = 2 * HI + 32
 F32 = jnp.float32
 BF16 = jnp.bfloat16
-NEAR = 5
+NEAR = 4
 VMEM = pltpu.VMEM
 ANY = pl.BlockSpec(memory_space=pl.ANY)
 IN_VMEM = pl.BlockSpec(memory_space=pltpu.VMEM)
@@ -360,7 +360,7 @@
         back_chunk(smooth_ref, table_ref, anom_ref, out_ref, start + i)
     width = main_ref.shape[1]
     here = pl.ds(pl.multiple_of(jnp.where(flip, 0, CHUNK), CHUNK), width)
-    main_ref[...] = out_ref[out_ref.shape[0] // 2, :, here]
+    main_ref[...] = out_ref[1, :, here]
 
 
 def last_kernel(
@@ -371,9 +371,9 @@
     halo = halo_ref[...]
     smooth_ref[jnp.where(flip, blocks + 1, 0)] = jnp.where(is_present(), halo, jnp.zeros_like(halo))
     back_chunk(smooth_ref, table_ref, anom_ref, out_ref, jnp.where(flip, blocks - 1, 0))
-    shares, _, columns = out_ref.shape
+    _, _, columns = out_ref.shape
     here = pl.ds(pl.multiple_of(jnp.where(flip, columns - CHUNK, 0), CHUNK), CHUNK)
-    edge_ref[...] = out_ref[shares // 2, :, here]
+    edge_ref[...] = out_ref[1, :, here]
 
 
 def edge_early_call(neighbours, own_a, own_near, own_far, got_a, tiles):
@@ -503,7 +503,7 @@
     smooth, out, main = late_call(
         head - 1 - NEAR, neighbours, halo_a, wide, tiles, table, anom, smooth, out
     )
-    half = shares // 2
+    half = 1
     main = pass_on(main, half, shares)
     _, pieces, edge = last_call(halo_b, table, anom, smooth, out)
     total = pieces[0].astype(F32)

time: 29.1 us -> 31.6 us (1.086)
  the two profiles are of different devices: /device:TPU:0 before, /device:TPU:4 now
where the time goes in v8:
time: 31.6 us; the launch traced here: 31.5 us
  starting transfers between devices  11.6 us (37%)
  waiting for transfers between devices  11.6 us (37%)
  Pallas kernels  7.49 us (24%)
  other arithmetic  0.7 us (2%)
    ppermute x5, waiting for transfers between devices, swap(): return lax.ppermute(value, ('space', 'mem'), pairs)  7.64 us
    ppermute x4, starting transfers between devices, pass_on(): lax.ppermute(value, 'mem', [(i, (i + shift) % shares) for i in range(shar...  6.83 us
    ppermute x5, starting transfers between devices, swap(): return lax.ppermute(value, ('space', 'mem'), pairs)  4.73 us
    ppermute x4, waiting for transfers between devices, pass_on(): lax.ppermute(value, 'mem', [(i, (i + shift) % shares) for i in range(shar...  3.96 us
    pallas_call x1, Pallas kernels, spread_first_call(): call(functools.partial(spread_kernel, steps, 0, chunks), [ANY] * 5, [IN_V...  2.03 us
    pallas_call x2, Pallas kernels, spread_more_call(): call(functools.partial(spread_kernel, steps, done, chunks), [IN_VMEM] * 6...  1.89 us
    pallas_call x1, Pallas kernels, early_call(): call(functools.partial(early_kernel, steps), [IN_SMEM] + [IN_VMEM] * 6, [...  1.75 us
    pallas_call x1, Pallas kernels, late_call(): call(functools.partial(late_kernel, steps), [IN_SMEM] + [IN_VMEM] * 7, [I...  1.01 us
  transfers between devices with their start and end apart: 9, of which 3 were waited for; matrix products, arithmetic and copies ran while one was open for 0% of the time, Pallas kernels for 11%

profile of v8, /device:TPU:4, one launch (start us, length us, event | category | flops | bytes accessed | tf_op | source)
XLA Modules:
  0.0 31.5 jit_solution(15454477190058606276)
XLA Ops:
  0.0 2.0 %shard_map.64 = (bf16[16,384,512]{2,1,0:T(8,128)(2,1)S(1)}, bf16[4,128,128]{2,1,0:T(8,128)(2,1)S(1)}, f32[2,128,128]{2,1,0:T(8,128)S(1)}, bf16[8,16,8192]{2,1,0:...) custom-call(bf16[8,16,8192]{2,1,0:T(8,128)(2,1)} %refs_0_.1, ...), custom_call_target="tpu_custom_call" | custom-call | tf_op jit(solution)/shard_map/pallas_call | solution.py:176
  2.0 0.8 %shard_map.65 = (bf16[16,384,512]{2,1,0:T(8,128)(2,1)S(1)}, bf16[5,128,128]{2,1,0:T(8,128)(2,1)S(1)}, f32[2,128,128]{2,1,0:T(8,128)S(1)}) custom-call(bf16[8,16,8192]{2,1,0:T(8,128)(2,1)S(1)} %get-tuple-element.33.refs_0_.anom_ref, f32[16,8192]{1,0:T(8,128)S(1)} %get-tuple-element.34.refs_1_, ...), custom_call_target="tpu_custom_call", output_to_operand_aliasing={{0}: (5, {})} | custom-call | tf_op jit(solution)/shard_map/pallas_call | solution.py:208
  2.8 0.0 slice-start
  2.9 0.0 slice-start.1
  2.9 1.1 %shard_map.66 = (bf16[16,384,512]{2,1,0:T(8,128)(2,1)S(1)}, bf16[9,128,128]{2,1,0:T(8,128)(2,1)S(1)}) custom-call(bf16[8,16,8192]{2,1,0:T(8,128)(2,1)S(1)} %get-tuple-element.33.refs_0_.anom_ref, f32[16,8192]{1,0:T(8,128)S(1)} %get-tuple-element.34.refs_1_, s32[3,8192]{1,0:T(4,128)S(1)} %get-tuple-element.35.refs_2_, ...), custom_call_target="tpu_custom_call", output_to_operand_aliasing={{0}: (5, {})} | custom-call | tf_op jit(solution)/shard_map/pallas_call | solution.py:208
  4.0 0.1 collective-permute-start.2
  4.0 1.5 %collective-permute-start = (bf16[5,128,128]{2,1,0:T(8,128)(2,1)S(1)}, bf16[5,128,128]{2,1,0:T(8,128)(2,1)S(1)}, u32[]{:S(2)}, u32[]{:S(2)}) collective-permute-start(bf16[5,128,128]{2,1,0:T(8,128)(2,1)S(1)} %get-tuple-element.39.own_far), channel_id=1, source_target_pairs={{0,1},{1,0},{2,3},{3,2},{4,8},{5,9},{6,10},{7,11},{8,4},{9,5},{10,... | collective-permute-start | bytes 491528 | tf_op jit(solution)/shard_map/ppermute | solution.py:469
  5.6 1.2 %collective-permute-start.1 = (bf16[4,128,128]{2,1,0:T(8,128)(2,1)S(1)}, bf16[4,128,128]{2,1,0:T(8,128)(2,1)S(1)}, u32[]{:S(2)}, u32[]{:S(2)}) collective-permute-start(bf16[4,128,128]{2,1,0:T(8,128)(2,1)S(1)} %get-tuple-element.40.own_near), channel_id=1, source_target_pairs={{0,1},{1,0},{2,3},{3,2},{4,8},{5,9},{6,10},{7,11},{8,4},{9,5},{10,... | collective-permute-start | bytes 393224 | tf_op jit(solution)/shard_map/ppermute | solution.py:469
  6.7 0.0 collective-permute-done.2.got_a
  6.8 0.0 slice-done
  6.8 0.0 slice-done.1
  6.8 0.3 shard_map.67
  7.1 0.1 collective-permute-start.4
  7.2 6.2 %collective-permute-done.1.got_near = bf16[4,128,128]{2,1,0:T(8,128)(2,1)S(1)} collective-permute-done((bf16[4,128,128]{2,1,0:T(8,128)(2,1)S(1)}, bf16[4,128,128]{2,1,0:T(8,128)(2,1)S(1)}, u32[]{:S(2)}, u32[]{:S(2)}) %collective-permute-start.1) | collective-permute-done | bytes 131104 | tf_op jit(solution)/shard_map/ppermute | solution.py:469
  13.4 1.8 %shard_map.68 = (bf16[32,128,128]{2,1,0:T(8,128)(2,1)S(1)}, bf16[18,128,128]{2,1,0:T(8,128)(2,1)S(1)}, bf16[4,16,2048]{2,1,0:T(8,128)(2,1)S(1)}) custom-call(s32[9,16]{1,0:T(8,128)S(4)} %get-tuple-element.32.nbr_ref, bf16[4,128,128]{2,1,0:T(8,128)(2,1)S(1)} %collective-permute-done.1.got_near, ...), custom_call_target="tpu_custom_call", output_to_operand_aliasing={{0}: (2, {}), {1}: (6, {})} | custom-call | tf_op jit(solution)/shard_map/pallas_call | solution.py:413
  15.2 0.0 collective-permute-done.got_far
  15.2 0.3 shard_map.69
  15.4 1.9 %collective-permute-start.3 = (bf16[128,128]{1,0:T(8,128)(2,1)S(1)}, bf16[128,128]{1,0:T(8,128)(2,1)S(1)}, u32[]{:S(2)}, u32[]{:S(2)}) collective-permute-start(bf16[128,128]{1,0:T(8,128)(2,1)S(1)} %get-tuple-element.49), channel_id=1, source_target_pairs={{0,1},{1,0},{2,3},{3,2},{4,8},{5,9},{6,10},{7,11},{8,4},{9,5},{10,... | collective-permute-start | bytes 98312 | tf_op jit(solution)/shard_map/ppermute | solution.py:469
  17.3 0.0 collective-permute-done.4.halo_ref
  17.3 1.0 %shard_map.70 = (bf16[18,128,128]{2,1,0:T(8,128)(2,1)S(1)}, bf16[4,16,2048]{2,1,0:T(8,128)(2,1)S(1)}, bf16[16,1536]{1,0:T(8,128)(2,1)S(1)}) custom-call(s32[9,16]{1,0:T(8,128)S(4)} %get-tuple-element.32.nbr_ref, bf16[128,128]{1,0:T(8,128)(2,1)S(1)} %collective-permute-done.4.halo_ref, ...), custom_call_target="tpu_custom_call", output_to_operand_aliasing={{0}: (6, {}), {1}: (7, {})} | custom-call | tf_op jit(solution)/shard_map/pallas_call | solution.py:428
  18.3 1.4 %collective-permute-done.3.halo_ref = bf16[128,128]{1,0:T(8,128)(2,1)S(1)} collective-permute-done((bf16[128,128]{1,0:T(8,128)(2,1)S(1)}, bf16[128,128]{1,0:T(8,128)(2,1)S(1)}, u32[]{:S(2)}, u32[]{:S(2)}) %collective-permute-start.3) | collective-permute-done | bytes 32800 | tf_op jit(solution)/shard_map/ppermute | solution.py:469
  19.7 0.2 shard_map.71
  20.0 3.2 %collective-permute-start.7 = (bf16[16,2048]{1,0:T(8,128)(2,1)S(1)}, bf16[16,2048]{1,0:T(8,128)(2,1)S(1)}, u32[]{:S(2)}, u32[]{:S(2)}) collective-permute-start(bf16[16,2048]{1,0:T(8,128)(2,1)S(1)} %get-tuple-element.59), channel_id=1, source_target_pairs={{0,2},{1,3},{2,0},{3,1},{4,6},{5,7},{6,4},{7,5},{8,10},{9,11},{10,... | collective-permute-start | bytes 196616 | tf_op jit(solution)/shard_map/ppermute | solution.py:473
  23.2 1.3 %collective-permute-start.8 = (bf16[16,2048]{1,0:T(8,128)(2,1)S(1)}, bf16[16,2048]{1,0:T(8,128)(2,1)S(1)}, u32[]{:S(2)}, u32[]{:S(2)}) collective-permute-start(bf16[16,2048]{1,0:T(8,128)(2,1)S(1)} %get-tuple-element.60), channel_id=1, source_target_pairs={{0,3},{1,0},{2,1},{3,2},{4,7},{5,4},{6,5},{7,6},{8,11},{9,8},{10,9... | collective-permute-start | bytes 196616 | tf_op jit(solution)/shard_map/ppermute | solution.py:473
  24.6 0.7 %collective-permute-start.5 = (bf16[16,1536]{1,0:T(8,128)(2,1)S(1)}, bf16[16,1536]{1,0:T(8,128)(2,1)S(1)}, u32[]{:S(2)}, u32[]{:S(2)}) collective-permute-start(bf16[16,1536]{1,0:T(8,128)(2,1)S(1)} %get-tuple-element.57), channel_id=1, source_target_pairs={{0,1},{1,2},{2,3},{3,0},{4,5},{5,6},{6,7},{7,4},{8,9},{9,10},{10,1... | collective-permute-start | bytes 147464 | tf_op jit(solution)/shard_map/ppermute | solution.py:473
  25.2 1.6 %collective-permute-start.6 = (bf16[16,512]{1,0:T(8,128)(2,1)S(1)}, bf16[16,512]{1,0:T(8,128)(2,1)S(1)}, u32[]{:S(2)}, u32[]{:S(2)}) collective-permute-start(bf16[16,512]{1,0:T(8,128)(2,1)S(1)} %get-tuple-element.58), channel_id=1, source_target_pairs={{0,1},{1,2},{2,3},{3,0},{4,5},{5,6},{6,7},{7,4},{8,9},{9,10},{10,1... | collective-permute-start | bytes 49160 | tf_op jit(solution)/shard_map/ppermute | solution.py:473
  26.8 4.0 %collective-permute-done.6 = bf16[16,512]{1,0:T(8,128)(2,1)S(1)} collective-permute-done((bf16[16,512]{1,0:T(8,128)(2,1)S(1)}, bf16[16,512]{1,0:T(8,128)(2,1)S(1)}, u32[]{:S(2)}, u32[]{:S(2)}) %collective-permute-start.6) | collective-permute-done | bytes 16416 | tf_op jit(solution)/shard_map/ppermute | solution.py:473
  30.8 0.0 collective-permute-done.5
  30.8 0.0 collective-permute-done.7
  30.8 0.0 collective-permute-done.8
  30.8 0.7 %fusion.2 = f32[16,2048]{1,0:T(8,128)} fusion(bf16[16,2048]{1,0:T(8,128)(2,1)S(1)} %collective-permute-done.8, bf16[16,2048]{1,0:T(8,128)(2,1)S(1)} %collective-permute-done.7, bf16[16,512]{1,0:T(8,128)(2,1)S(1)} %collective-permute-done.6, bf16[16,1536]{1,0:T(8,128)(2,1)S(1)} %collective-permute-done.5, bf16[4,16,2048]{2,1,0:T(8,128)(2,1)S(1)} %get-tuple-element.56, ...), kind=kLoop, calls=%fused_computation.3 | loop fusion | flops 557056 | bytes 393217 | tf_op jit(solution)/shard_map/div | solution.py:521
  (2 shorter events, 0.0 us)
Async XLA Ops:
  2.8 3.9 %slice-start = ((s8[4718592]{0:T(1024)(128)(4,1)}), s8[4194304]{0:T(1024)(128)(4,1)S(1)}, s32[]{:S(2)}) async-start(s8[4718592]{0:T(1024)(128)(4,1)} %bitcast.7), calls=%async_computation | async-start | bytes 8388608
  2.9 3.9 %slice-start.1 = ((s8[4718592]{0:T(1024)(128)(4,1)}), s8[524288]{0:T(1024)(128)(4,1)S(1)}, s32[]{:S(2)}) async-start(s8[4718592]{0:T(1024)(128)(4,1)} %bitcast.7), calls=%async_computation.1 | async-start | bytes 1048576
  4.0 2.8 %collective-permute-start.2 = (bf16[9,128,128]{2,1,0:T(8,128)(2,1)S(1)}, bf16[9,128,128]{2,1,0:T(8,128)(2,1)S(1)}, u32[]{:S(2)}, u32[]{:S(2)}) collective-permute-start(bf16[9,128,128]{2,1,0:T(8,128)(2,1)S(1)} %get-tuple-element.43.own_a), channel_id=1, source_target_pairs={{0,4},{1,5},{2,6},{3,7},{4,0},{5,1},{6,2},{7,3},{8,12},{9,13},{10,... | collective-permute-start | bytes 884744 | tf_op jit(solution)/shard_map/ppermute | solution.py:469
  4.0 11.1 %collective-permute-start = (bf16[5,128,128]{2,1,0:T(8,128)(2,1)S(1)}, bf16[5,128,128]{2,1,0:T(8,128)(2,1)S(1)}, u32[]{:S(2)}, u32[]{:S(2)}) collective-permute-start(bf16[5,128,128]{2,1,0:T(8,128)(2,1)S(1)} %get-tuple-element.39.own_far), channel_id=1, source_target_pairs={{0,1},{1,0},{2,3},{3,2},{4,8},{5,9},{6,10},{7,11},{8,4},{9,5},{10,... | collective-permute-start | bytes 491528 | tf_op jit(solution)/shard_map/ppermute | solution.py:469
  5.6 7.8 %collective-permute-start.1 = (bf16[4,128,128]{2,1,0:T(8,128)(2,1)S(1)}, bf16[4,128,128]{2,1,0:T(8,128)(2,1)S(1)}, u32[]{:S(2)}, u32[]{:S(2)}) collective-permute-start(bf16[4,128,128]{2,1,0:T(8,128)(2,1)S(1)} %get-tuple-element.40.own_near), channel_id=1, source_target_pairs={{0,1},{1,0},{2,3},{3,2},{4,8},{5,9},{6,10},{7,11},{8,4},{9,5},{10,... | collective-permute-start | bytes 393224 | tf_op jit(solution)/shard_map/ppermute | solution.py:469
  7.1 10.2 %collective-permute-start.4 = (bf16[128,128]{1,0:T(8,128)(2,1)S(1)}, bf16[128,128]{1,0:T(8,128)(2,1)S(1)}, u32[]{:S(2)}, u32[]{:S(2)}) collective-permute-start(bf16[128,128]{1,0:T(8,128)(2,1)S(1)} %get-tuple-element.50), channel_id=1, source_target_pairs={{0,4},{1,5},{2,6},{3,7},{4,0},{5,1},{6,2},{7,3},{8,12},{9,13},{10,... | collective-permute-start | bytes 98312 | tf_op jit(solution)/shard_map/ppermute | solution.py:469
  15.4 4.3 %collective-permute-start.3 = (bf16[128,128]{1,0:T(8,128)(2,1)S(1)}, bf16[128,128]{1,0:T(8,128)(2,1)S(1)}, u32[]{:S(2)}, u32[]{:S(2)}) collective-permute-start(bf16[128,128]{1,0:T(8,128)(2,1)S(1)} %get-tuple-element.49), channel_id=1, source_target_pairs={{0,1},{1,0},{2,3},{3,2},{4,8},{5,9},{6,10},{7,11},{8,4},{9,5},{10,... | collective-permute-start | bytes 98312 | tf_op jit(solution)/shard_map/ppermute | solution.py:469
  20.0 10.8 %collective-permute-start.7 = (bf16[16,2048]{1,0:T(8,128)(2,1)S(1)}, bf16[16,2048]{1,0:T(8,128)(2,1)S(1)}, u32[]{:S(2)}, u32[]{:S(2)}) collective-permute-start(bf16[16,2048]{1,0:T(8,128)(2,1)S(1)} %get-tuple-element.59), channel_id=1, source_target_pairs={{0,2},{1,3},{2,0},{3,1},{4,6},{5,7},{6,4},{7,5},{8,10},{9,11},{10,... | collective-permute-start | bytes 196616 | tf_op jit(solution)/shard_map/ppermute | solution.py:473
  23.2 7.6 %collective-permute-start.8 = (bf16[16,2048]{1,0:T(8,128)(2,1)S(1)}, bf16[16,2048]{1,0:T(8,128)(2,1)S(1)}, u32[]{:S(2)}, u32[]{:S(2)}) collective-permute-start(bf16[16,2048]{1,0:T(8,128)(2,1)S(1)} %get-tuple-element.60), channel_id=1, source_target_pairs={{0,3},{1,0},{2,1},{3,2},{4,7},{5,4},{6,5},{7,6},{8,11},{9,8},{10,9... | collective-permute-start | bytes 196616 | tf_op jit(solution)/shard_map/ppermute | solution.py:473
  24.6 6.2 %collective-permute-start.5 = (bf16[16,1536]{1,0:T(8,128)(2,1)S(1)}, bf16[16,1536]{1,0:T(8,128)(2,1)S(1)}, u32[]{:S(2)}, u32[]{:S(2)}) collective-permute-start(bf16[16,1536]{1,0:T(8,128)(2,1)S(1)} %get-tuple-element.57), channel_id=1, source_target_pairs={{0,1},{1,2},{2,3},{3,0},{4,5},{5,6},{6,7},{7,4},{8,9},{9,10},{10,1... | collective-permute-start | bytes 147464 | tf_op jit(solution)/shard_map/ppermute | solution.py:473
  25.2 5.5 %collective-permute-start.6 = (bf16[16,512]{1,0:T(8,128)(2,1)S(1)}, bf16[16,512]{1,0:T(8,128)(2,1)S(1)}, u32[]{:S(2)}, u32[]{:S(2)}) collective-permute-start(bf16[16,512]{1,0:T(8,128)(2,1)S(1)} %get-tuple-element.58), channel_id=1, source_target_pairs={{0,1},{1,2},{2,3},{3,0},{4,5},{5,6},{6,7},{7,4},{8,9},{9,10},{10,1... | collective-permute-start | bytes 49160 | tf_op jit(solution)/shard_map/ppermute | solution.py:473
